TPU v7x, 256 devices: a whole 4x4x8 slice. The times are simulated.
256 devices in a mesh: obs: 4 (over y), par: 64 (over x, z, core).
Axes of the slice: x: 4, y: 4, z: 8, core: 2. Of those that a mesh axis runs over, the one named last changes fastest.
Arguments:
- jacobian: bfloat16 [2048, 262144], P('obs', 'par'), may hold values from -0.01171875 to 0.01171875
- probes: bfloat16 [262144, 256], P('par'), may hold values from -6 to 6
- coeffs: bfloat16 [2048, 3, 128, 128], P('par'), may hold values from -0.3125 to 0.3125
- offsets: int32 [2048, 2], P('par'), may hold values from -4 to 4
Outputs:
- ritz_basis: bfloat16 [262144, 256], P('par')
- basis_image: bfloat16 [262144, 256], P('par')
- ritz_matrix: float32 [256, 256], replicated
All inputs are finite; a program needn't handle non-finite values.
Results may differ from a plain program's by a relative error of at most 0.015.
Values may be sent and summed in bfloat16 or wider, within the bound.
No kernel may reach another device: no remote copies, remote signals or barrier semaphores. Data moves between devices by JAX's collectives and lax.ppermute only.
A program may use at most 128 MiB of HBM per device.

v0:
```python
import functools

import jax
import jax.numpy as jnp
from jax import lax
from jax.experimental import pallas as pl
from jax.experimental.pallas import tpu as pltpu
from jax.sharding import PartitionSpec as P

BLK = 128
REACH = 4
EDGE = REACH * BLK
NB = 64
F32 = jnp.float32
BF16 = jnp.bfloat16
HI = lax.Precision.HIGHEST
VMEM = pl.BlockSpec(memory_space=pltpu.VMEM)
SMEM = pl.BlockSpec(memory_space=pltpu.SMEM)


def call(kernel, name, outs, specs, args, scratch=(), mib=24, flops=0):
    return pl.pallas_call(
        kernel,
        name=name,
        out_shape=outs,
        in_specs=specs,
        out_specs=jax.tree.map(lambda _: VMEM, outs),
        scratch_shapes=scratch,
        compiler_params=pltpu.CompilerParams(vmem_limit_bytes=mib * 2**20),
        cost_estimate=pl.CostEstimate(flops=flops, bytes_accessed=0, transcendentals=0),
    )(*args)


def dot(a, b):
    return jnp.dot(a, b, preferred_element_type=F32)


def dot_tn(a, b, precision=None):
    return lax.dot_general(a, b, (((0,), (0,)), ((), ())), precision=precision, preferred_element_type=F32)


def dot_nt(a, b, precision=None):
    return lax.dot_general(a, b, (((1,), (1,)), ((), ())), precision=precision, preferred_element_type=F32)


def shape(*dims, dtype=BF16):
    return jax.ShapeDtypeStruct(dims, dtype)


def edges_kernel(off_ref, jac_ref, coef_ref, low_ref, high_ref, acc):
    count = coef_ref.shape[0]
    acc[...] = jnp.zeros_like(acc)
    for side, first in ((0, 0), (1, count - REACH)):
        for i in range(REACH):
            block = first + i
            columns = jac_ref[:, block * BLK : (block + 1) * BLK]
            for j in range(2):
                target = block + off_ref[block, j]
                place = target + REACH if side == 0 else target - count + REACH
                outside = target < 0 if side == 0 else target >= count

                @pl.when(outside)
                def _():
                    acc[place] += dot(columns, coef_ref[block, j + 1])

    for i in range(REACH):
        low_ref[:, i * BLK : (i + 1) * BLK] = acc[i].astype(BF16)
        high_ref[:, i * BLK : (i + 1) * BLK] = acc[i + REACH].astype(BF16)


def own_kernel(off_ref, jac_ref, coef_ref, out_ref, acc):
    count = coef_ref.shape[0]

    def diagonal(block, carry):
        columns = jac_ref[:, pl.ds(pl.multiple_of(block * BLK, BLK), BLK)]
        acc[block] = dot(columns, coef_ref[block, 0])
        return carry

    lax.fori_loop(0, count, diagonal, 0, unroll=2)

    def band(block, carry):
        columns = jac_ref[:, pl.ds(pl.multiple_of(block * BLK, BLK), BLK)]
        both = jnp.concatenate([coef_ref[block, 1], coef_ref[block, 2]], axis=1)
        terms = dot(columns, both)
        for j in range(2):
            target = block + off_ref[block, j]

            @pl.when((target >= 0) & (target < count))
            def _():
                acc[target] += terms[:, j * BLK : (j + 1) * BLK]

        return carry

    lax.fori_loop(0, count, band, 0)
    for block in range(count):
        out_ref[:, block * BLK : (block + 1) * BLK] = acc[block].astype(BF16)


def forward_kernel(own_ref, left_ref, right_ref, probe_ref, full_ref, part_ref):
    width = own_ref.shape[1]
    first = (own_ref[:, :EDGE].astype(F32) + left_ref[...].astype(F32)).astype(BF16)
    last = (own_ref[:, width - EDGE :].astype(F32) + right_ref[...].astype(F32)).astype(BF16)
    full_ref[:, :EDGE] = first
    full_ref[:, EDGE : width - EDGE] = own_ref[:, EDGE : width - EDGE]
    full_ref[:, width - EDGE :] = last
    part_ref[...] = dot(full_ref[...], probe_ref[...]).astype(BF16)


def total_kernel(parts_ref, out_ref):
    total = parts_ref[0].astype(F32)
    for i in range(1, parts_ref.shape[0]):
        total += parts_ref[i].astype(F32)
    total = total.astype(BF16)
    for i in range(out_ref.shape[0]):
        out_ref[i] = total


def sample_kernel(ranks, me_ref, full_ref, fwd_ref, *outs):
    rows = full_ref.shape[1] // ranks // 2
    fwd = fwd_ref[...]
    for rel in range(ranks):
        owner = lax.rem(me_ref[0] + rel, ranks)
        for half in range(2):
            start = pl.multiple_of(owner * (2 * rows) + half * rows, rows)
            outs[2 * rel + half][...] = dot_tn(full_ref[:, pl.ds(start, rows)], fwd).astype(BF16)


def project_kernel(ranks, me_ref, full_ref, *refs):
    pieces, (sample_ref, part_ref, low_ref, high_ref) = refs[: 2 * ranks], refs[2 * ranks :]
    rows = pieces[0].shape[0]
    total = jnp.zeros(part_ref.shape, F32)
    for rel in range(ranks):
        owner = lax.rem(me_ref[0] + rel, ranks)
        for half in range(2):
            piece = pieces[2 * rel + half][...]
            start = pl.multiple_of(owner * (2 * rows) + half * rows, rows)
            sample_ref[pl.ds(start, rows), :] = piece
            total += dot(full_ref[:, pl.ds(start, rows)], piece)
    part_ref[...] = total.astype(BF16)
    low_ref[...] = sample_ref[:EDGE, :]
    high_ref[...] = sample_ref[sample_ref.shape[0] - EDGE :, :]


def prior_kernel(off_ref, coef_ref, sample_ref, below_ref, above_ref, out_ref, ext):
    count, rows = coef_ref.shape[0], sample_ref.shape[0]
    ext[:EDGE] = below_ref[...]
    ext[EDGE : EDGE + rows] = sample_ref[...]
    ext[EDGE + rows :] = above_ref[...]

    def apply(block, carry):
        picked = [ext[pl.ds(pl.multiple_of((block + REACH) * BLK, BLK), BLK), :]]
        for j in range(2):
            start = (block + REACH + off_ref[block, j]) * BLK
            picked.append(ext[pl.ds(pl.multiple_of(start, BLK), BLK), :])
        wide = jnp.concatenate([coef_ref[block, j] for j in range(3)], axis=1)
        result = dot(wide, jnp.concatenate(picked, axis=0))
        out_ref[pl.ds(pl.multiple_of(block * BLK, BLK), BLK), :] = result.astype(BF16)
        return carry

    lax.fori_loop(0, count, apply, 0, unroll=2)


def packed(full):
    half = full.shape[0] // 2
    return jnp.concatenate([full[:half, :half], full[:half, half:], full[half:, half:]], axis=0)


def moments_kernel(fwd_ref, proj_ref, gram_ref, second_ref):
    proj = proj_ref[...]
    gram = dot_tn(fwd_ref[...], proj)
    gram_ref[...] = packed(0.5 * (gram + gram.T))
    second_ref[...] = packed(dot_tn(proj, proj)).astype(BF16)


def row_of(tile, k):
    return jnp.broadcast_to(tile[k : k + 1, :], tile.shape)


def lane_of(tile, k):
    return jnp.broadcast_to(tile[:, k : k + 1], (8, 2 * NB))


def factor_inverse(block):
    index = [lax.broadcasted_iota(jnp.int32, (NB, NB), d) for d in (0, 1)]
    wide = jnp.concatenate([block, (index[0] == index[1]).astype(F32)], axis=1)
    groups = NB // 8
    tiles = [wide[8 * t : 8 * t + 8] for t in range(groups)]
    row = lax.broadcasted_iota(jnp.int32, (8, 2 * NB), 0)
    out = []
    for g in range(groups):
        cols = {t: [lane_of(tiles[t], 8 * g + k) for k in range(8)] for t in range(g, groups)}
        scale = jnp.ones((8, 2 * NB), F32)
        for k in range(8):
            pivot = row_of(cols[g][k], k)
            inverse = 1.0 / pivot
            scale = jnp.where(row == k, lax.rsqrt(pivot), scale)
            pivot_row = row_of(tiles[g], k)
            heads = [row_of(cols[g][j], k) for j in range(k + 1, 8)]
            for t in range(g, groups):
                ratio = cols[t][k] * inverse
                if t == g:
                    ratio = jnp.where(row > k, ratio, 0.0)
                tiles[t] = tiles[t] - ratio * pivot_row
                for j in range(k + 1, 8):
                    cols[t][j] = cols[t][j] - ratio * heads[j - k - 1]
        out.append(tiles[g] * scale)
    return jnp.concatenate(out, axis=0)[:, NB:]


def factor_kernel(scale, *refs):
    parts, (out_ref, a_ref, m_ref) = refs[:-3], refs[-3:]
    n = out_ref.shape[0]
    half = n // 2
    total = parts[0][...]
    for part in parts[1:]:
        total += part[...]
    total *= scale
    a_ref[...] = jnp.zeros((n, n), F32)
    a_ref[:half, :half] = total[:half]
    a_ref[:half, half:] = total[half:n]
    a_ref[half:, half:] = total[n:]
    m_ref[...] = jnp.zeros((n, n), F32)
    out_ref[...] = jnp.zeros((n, n), F32)
    for lo in range(0, n, NB):
        hi = lo + NB
        inverse = factor_inverse(a_ref[lo:hi, lo:hi])
        out_ref[lo:hi, lo:hi] = inverse
        if lo:
            out_ref[lo:hi, :lo] = jnp.dot(inverse, m_ref[lo:hi, :lo], precision=HI, preferred_element_type=F32)
        if hi < n:
            upper = jnp.dot(inverse, a_ref[lo:hi, hi:], precision=HI, preferred_element_type=F32)
            a_ref[hi:, hi:] -= dot_tn(upper, upper, HI)
            m_ref[hi:, :hi] -= dot_tn(upper, out_ref[lo:hi, :hi], HI)


def final_kernel(scale, inv_ref, sample_ref, image_ref, *refs):
    seconds, (basis_ref, mapped_ref, ritz_ref) = refs[:-3], refs[-3:]
    inverse = inv_ref[...]
    low = inverse.astype(BF16)
    basis_ref[...] = dot_nt(sample_ref[...], low).astype(BF16)
    mapped_ref[...] = dot_nt(image_ref[...], low).astype(BF16)

    @pl.when(pl.program_id(0) == 0)
    def _():
        n = inverse.shape[0]
        half = n // 2
        total = seconds[0][...].astype(F32)
        for part in seconds[1:]:
            total += part[...].astype(F32)
        upper = total[half:n]
        full = jnp.concatenate(
            [
                jnp.concatenate([total[:half], upper], axis=1),
                jnp.concatenate([upper.T, total[n:]], axis=1),
            ],
            axis=0,
        )
        left = jnp.dot(inverse, full, precision=HI, preferred_element_type=F32)
        ritz_ref[...] = dot_nt(left, inverse, HI) * scale


def shifted(value, axis, by, wrap=True):
    count = lax.axis_size(axis)
    pairs = [(i, (i + by) % count) for i in range(count) if wrap or 0 <= i + by < count]
    return lax.ppermute(value, axis, pairs)


def added(*values):
    return sum(v.astype(F32) for v in values).astype(BF16)


def summed_over_par(part):
    rows, width = part.shape
    count = lax.axis_size("par")
    parts = lax.all_to_all(part.reshape(count, rows // count, width), "par", 0, 0, tiled=True)
    own = call(total_kernel, "total", shape(*parts.shape), [VMEM], [parts], mib=4)
    return lax.all_to_all(own, "par", 0, 0, tiled=True).reshape(rows, width)


def body(jacobian, probes, coeffs, offsets):
    ranks = lax.axis_size("obs")
    nobs, npar = jacobian.shape[0], jacobian.shape[1]
    width = probes.shape[1]
    count = coeffs.shape[0]
    me = lax.axis_index("obs").reshape(1)
    flops = 2 * nobs * npar * width

    low, high = call(
        edges_kernel,
        "edges",
        [shape(nobs, EDGE)] * 2,
        [SMEM, VMEM, VMEM],
        [offsets, jacobian, coeffs],
        [pltpu.VMEM((2 * REACH, nobs, BLK), F32)],
        flops=flops // 4,
    )
    from_left = shifted(high, "par", 1, False)
    from_right = shifted(low, "par", -1, False)
    own = call(
        own_kernel,
        "own",
        shape(nobs, npar),
        [SMEM, VMEM, VMEM],
        [offsets, jacobian, coeffs],
        [pltpu.VMEM((count, nobs, BLK), F32)],
        flops=4 * flops,
    )
    full, part = call(
        forward_kernel,
        "forward",
        [shape(nobs, npar), shape(nobs, width)],
        [VMEM] * 4,
        [own, from_left, from_right, probes],
        flops=flops,
    )
    forward = summed_over_par(part)

    pieces = call(
        functools.partial(sample_kernel, ranks),
        "sample",
        [shape(npar // ranks // 2, width)] * (2 * ranks),
        [SMEM, VMEM, VMEM],
        [me, full, forward],
        flops=flops,
    )
    here0, here1, right0, right1, far0, far1, left0, left1 = pieces
    via_left = shifted(far0, "obs", 1)
    via_right = shifted(far1, "obs", -1)
    a1 = shifted(right1, "obs", 1)
    b0 = shifted(left0, "obs", -1)
    a0 = shifted(added(right0, via_left), "obs", 1)
    b1 = shifted(added(left1, via_right), "obs", -1)
    sum0 = added(here0, a0, b0)
    sum1 = added(here1, a1, b1)

    l0 = shifted(sum0, "obs", 1)
    r1 = shifted(sum1, "obs", -1)
    l1 = shifted(sum1, "obs", 1)
    r0 = shifted(sum0, "obs", -1)
    f0 = shifted(l0, "obs", 1)
    f1 = shifted(r1, "obs", -1)

    sample, part2, tail_low, tail_high = call(
        functools.partial(project_kernel, ranks),
        "project",
        [shape(npar, width), shape(nobs, width), shape(EDGE, width), shape(EDGE, width)],
        [SMEM] + [VMEM] * (1 + 2 * ranks),
        [me, full, sum0, sum1, r0, r1, f0, f1, l0, l1],
        flops=flops,
    )
    below = shifted(tail_high, "par", 1, False)
    above = shifted(tail_low, "par", -1, False)
    projected = summed_over_par(part2)
    image = call(
        prior_kernel,
        "prior",
        shape(npar, width),
        [SMEM] + [VMEM] * 4,
        [offsets, coeffs, sample, below, above],
        [pltpu.VMEM((npar + 2 * EDGE, width), BF16)],
        flops=flops,
    )

    gram, second = call(
        moments_kernel,
        "moments",
        [shape(3 * width // 2, width // 2, dtype=F32), shape(3 * width // 2, width // 2)],
        [VMEM] * 2,
        [forward, projected],
        mib=8,
        flops=flops // 8,
    )
    grams = [gram] + [shifted(gram, "obs", by) for by in (1, -1, 2)]
    seconds = [second] + [shifted(second, "obs", by) for by in (1, -1, 2)]
    total_par = npar * lax.axis_size("par")
    total_obs = nobs * ranks
    inverse = call(
        functools.partial(factor_kernel, 1.0 / total_par),
        "factor",
        shape(width, width, dtype=F32),
        [VMEM] * len(grams),
        grams,
        [pltpu.VMEM((width, width), F32)] * 2,
        mib=8,
        flops=16 * flops,
    )
    steps = 4
    rows = npar // steps
    whole = lambda *dims: pl.BlockSpec(dims, lambda i: (0,) * len(dims))
    by_rows = pl.BlockSpec((rows, width), lambda i: (i, 0))
    return pl.pallas_call(
        functools.partial(final_kernel, 1.0 / total_obs),
        name="final",
        grid=(steps,),
        out_shape=[shape(npar, width), shape(npar, width), shape(width, width, dtype=F32)],
        in_specs=[whole(width, width), by_rows, by_rows] + [whole(*second.shape)] * len(seconds),
        out_specs=[by_rows, by_rows, whole(width, width)],
        compiler_params=pltpu.CompilerParams(vmem_limit_bytes=16 * 2**20),
    )(inverse, sample, image, *seconds)


def solution(mesh):
    return jax.shard_map(
        body,
        mesh=mesh,
        in_specs=(P("obs", "par"), P("par", None), P("par", None, None, None), P("par", None)),
        out_specs=(P("par", None), P("par", None), P()),
        check_vma=False,
    )
```

profile of v0, /device:TPU:6, one launch (start us, length us, event | category | flops | bytes accessed | tf_op | source)
XLA Modules:
  0.0 192.2 jit_solution(10557974670567384042)
XLA Ops:
  0.6 0.8 copy.7.off_ref
  1.4 1.9 copy-done.2
  3.3 2.2 %copy-done.6 = bf16[512,4096]{1,0:T(8,128)(2,1)S(1)} copy-done((bf16[512,4096]{1,0:T(8,128)(2,1)S(1)}, bf16[512,4096]{1,0:T(8,128)(2,1)}, u32[]{:S(2)}) %copy-start.6) | copy-done | bytes 4194328
  5.5 1.8 edges.1
  7.2 1.9 collective-permute-start
  9.2 7.8 %collective-permute-start.1 = (bf16[512,512]{1,0:T(8,128)(2,1)S(1)}, bf16[512,512]{1,0:T(8,128)(2,1)S(1)}, u32[]{:S(2)}, u32[]{:S(2)}) collective-permute-start(bf16[512,512]{1,0:T(8,128)(2,1)S(1)} %get-tuple-element.22), channel_id=1, source_target_pairs={{1,0},{2,1},{3,2},{4,3},{5,4},{6,5},{7,6},{8,7},{9,8},{10,9},{11,1... | collective-permute-start | bytes 1572872 | tf_op jit(solution)/shard_map/ppermute | solution.py:265
  16.9 14.0 %own.1.own_ref = bf16[512,4096]{1,0:T(8,128)(2,1)S(1)} custom-call(s32[32,2]{1,0:T(8,128)S(1)} %copy.7.off_ref, bf16[512,4096]{1,0:T(8,128)(2,1)S(1)} %copy-done.6, bf16[32,3,128,128]{3,2,1,0:T(8,128)(2,1)S(1)} %copy-done.2), custom_call_target="tpu_custom_call" | custom-call | flops 4294967296 | tf_op jit(solution)/shard_map/own/pallas_call | solution.py:22
  31.0 1.4 forward.1
  32.4 2.0 %copy-done = bf16[512,4096]{1,0:T(8,128)(2,1)} copy-done((bf16[512,4096]{1,0:T(8,128)(2,1)}, bf16[512,4096]{1,0:T(8,128)(2,1)S(1)}, u32[]{:S(2)}) %copy-start) | copy-done | bytes 4194328
  34.3 21.1 %all_to_all.20.parts_ref = bf16[64,8,256]{2,1,0:T(8,128)(2,1)S(1)} all-to-all(bf16[64,8,256]{2,1,0:T(8,128)(2,1)S(1)} %bitcast.8), channel_id=1, replica_groups=mesh['obs'=4,'par'=64] {'par'}, dimensions={0} | all-to-all | bytes 524288 | tf_op jit(solution)/shard_map/all_to_all | solution.py:275
  55.5 0.8 total.2
  56.3 6.5 %all-to-all-start.1 = ((bf16[64,8,256]{2,1,0:T(8,128)(2,1)}), bf16[64,8,256]{2,1,0:T(8,128)(2,1)S(1)}, u32[]{:S(2)}, u32[]{:S(2)}) async-start(bf16[64,8,256]{2,1,0:T(8,128)(2,1)} %total.2), calls=%async_computation.1 | async-start | bytes 524288 | tf_op jit(solution)/shard_map/all_to_all | solution.py:277
  62.7 11.5 %all-to-all-done.1 = bf16[64,8,256]{2,1,0:T(8,128)(2,1)S(1)} async-done(((bf16[64,8,256]{2,1,0:T(8,128)(2,1)}), bf16[64,8,256]{2,1,0:T(8,128)(2,1)S(1)}, u32[]{:S(2)}, u32[]{:S(2)}) %all-to-all-start.1) | async-done | bytes 262176 | tf_op jit(solution)/shard_map/all_to_all | solution.py:277
  74.3 2.2 %copy-done.1 = bf16[512,4096]{1,0:T(8,128)(2,1)S(1)} copy-done((bf16[512,4096]{1,0:T(8,128)(2,1)S(1)}, bf16[512,4096]{1,0:T(8,128)(2,1)}, u32[]{:S(2)}) %copy-start.1) | copy-done | bytes 4194328
  76.5 1.4 sample.1
  77.8 3.1 %collective-permute-start.6 = (bf16[512,256]{1,0:T(8,128)(2,1)S(1)}, bf16[512,256]{1,0:T(8,128)(2,1)S(1)}, u32[]{:S(2)}, u32[]{:S(2)}) collective-permute-start(bf16[512,256]{1,0:T(8,128)(2,1)S(1)} %get-tuple-element.32), channel_id=1, source_target_pairs={{0,192},{64,0},{128,64},{192,128},{1,193},{65,1},{129,65},{193,129... | collective-permute-start | bytes 786440 | tf_op jit(solution)/shard_map/ppermute | solution.py:265
  80.9 0.6 collective-permute-start.5
  81.5 5.3 %collective-permute-done.6 = bf16[512,256]{1,0:T(8,128)(2,1)S(1)} collective-permute-done((bf16[512,256]{1,0:T(8,128)(2,1)S(1)}, bf16[512,256]{1,0:T(8,128)(2,1)S(1)}, u32[]{:S(2)}, u32[]{:S(2)}) %collective-permute-start.6) | collective-permute-done | bytes 262176 | tf_op jit(solution)/shard_map/ppermute | solution.py:265
  86.9 3.8 %collective-permute-start.7 = (bf16[512,256]{1,0:T(8,128)(2,1)S(1)}, bf16[512,256]{1,0:T(8,128)(2,1)S(1)}, u32[]{:S(2)}, u32[]{:S(2)}) collective-permute-start(bf16[512,256]{1,0:T(8,128)(2,1)S(1)} %add_convert_fusion.1), channel_id=1, source_target_pairs={{0,192},{64,0},{128,64},{192,128},{1,193},{65,1},{129,65},{193,129... | collective-permute-start | bytes 786440 | tf_op jit(solution)/shard_map/ppermute | solution.py:265
  90.7 0.6 collective-permute-done.2
  91.4 1.6 collective-permute-start.3
  93.0 3.9 %collective-permute-done.5 = bf16[512,256]{1,0:T(8,128)(2,1)S(1)} collective-permute-done((bf16[512,256]{1,0:T(8,128)(2,1)S(1)}, bf16[512,256]{1,0:T(8,128)(2,1)S(1)}, u32[]{:S(2)}, u32[]{:S(2)}) %collective-permute-start.5) | collective-permute-done | bytes 262176 | tf_op jit(solution)/shard_map/ppermute | solution.py:265
  97.4 3.8 %collective-permute-start.9 = (bf16[512,256]{1,0:T(8,128)(2,1)S(1)}, bf16[512,256]{1,0:T(8,128)(2,1)S(1)}, u32[]{:S(2)}, u32[]{:S(2)}) collective-permute-start(bf16[512,256]{1,0:T(8,128)(2,1)S(1)} %add_convert_fusion.refs_1_), channel_id=1, source_target_pairs={{0,192},{64,0},{128,64},{192,128},{1,193},{65,1},{129,65},{193,129... | collective-permute-start | bytes 786440 | tf_op jit(solution)/shard_map/ppermute | solution.py:265
  101.2 1.7 collective-permute-done.4
  103.2 1.9 collective-permute-start.13
  105.0 2.0 %collective-permute-start.8 = (bf16[512,256]{1,0:T(8,128)(2,1)S(1)}, bf16[512,256]{1,0:T(8,128)(2,1)S(1)}, u32[]{:S(2)}, u32[]{:S(2)}) collective-permute-start(bf16[512,256]{1,0:T(8,128)(2,1)S(1)} %add_convert_fusion.2.refs_0_), channel_id=1, source_target_pairs={{0,192},{64,0},{128,64},{192,128},{1,193},{65,1},{129,65},{193,129... | collective-permute-start | bytes 786440 | tf_op jit(solution)/shard_map/ppermute | solution.py:265
  107.0 1.5 collective-permute-done.9.refs_3_
  108.6 3.7 %collective-permute-start.12 = (bf16[512,256]{1,0:T(8,128)(2,1)S(1)}, bf16[512,256]{1,0:T(8,128)(2,1)S(1)}, u32[]{:S(2)}, u32[]{:S(2)}) collective-permute-start(bf16[512,256]{1,0:T(8,128)(2,1)S(1)} %collective-permute-done.9.refs_3_), channel_id=1, source_target_pairs={{0,192},{64,0},{128,64},{192,128},{1,193},{65,1},{129,65},{193,129... | collective-permute-start | bytes 786440 | tf_op jit(solution)/shard_map/ppermute | solution.py:265
  112.3 0.9 collective-permute-done.10.refs_6_
  113.2 5.3 %collective-permute-done.13.refs_7_ = bf16[512,256]{1,0:T(8,128)(2,1)S(1)} collective-permute-done((bf16[512,256]{1,0:T(8,128)(2,1)S(1)}, bf16[512,256]{1,0:T(8,128)(2,1)S(1)}, u32[]{:S(2)}, u32[]{:S(2)}) %collective-permute-start.13) | collective-permute-done | bytes 262176 | tf_op jit(solution)/shard_map/ppermute | solution.py:265
  118.5 2.8 %collective-permute-done.11.refs_4_ = bf16[512,256]{1,0:T(8,128)(2,1)S(1)} collective-permute-done((bf16[512,256]{1,0:T(8,128)(2,1)S(1)}, bf16[512,256]{1,0:T(8,128)(2,1)S(1)}, u32[]{:S(2)}, u32[]{:S(2)}) %collective-permute-start.11) | collective-permute-done | bytes 262176 | tf_op jit(solution)/shard_map/ppermute | solution.py:265
  121.3 1.3 project.1
  122.6 1.3 copy-done.4
  123.9 17.6 %all_to_all.21.parts_ref = bf16[64,8,256]{2,1,0:T(8,128)(2,1)S(1)} all-to-all(bf16[64,8,256]{2,1,0:T(8,128)(2,1)S(1)} %bitcast.7), channel_id=1, replica_groups=mesh['obs'=4,'par'=64] {'par'}, dimensions={0} | all-to-all | bytes 524288 | tf_op jit(solution)/shard_map/all_to_all | solution.py:275
  141.6 0.7 copy-done.8
  142.3 6.7 %all-to-all-start.3 = ((bf16[64,8,256]{2,1,0:T(8,128)(2,1)}), bf16[64,8,256]{2,1,0:T(8,128)(2,1)}, u32[]{:S(2)}, u32[]{:S(2)}) async-start(bf16[64,8,256]{2,1,0:T(8,128)(2,1)} %copy-done.8), calls=%async_computation.3 | async-start | bytes 524288 | tf_op jit(solution)/shard_map/all_to_all | solution.py:277
  149.0 2.0 %collective-permute-start.17 = (bf16[512,256]{1,0:T(8,128)(2,1)}, bf16[512,256]{1,0:T(8,128)(2,1)}, u32[]{:S(2)}, u32[]{:S(2)}) collective-permute-start(bf16[512,256]{1,0:T(8,128)(2,1)} %copy-done.10), channel_id=1, source_target_pairs={{0,1},{1,2},{2,3},{3,4},{4,5},{5,6},{6,7},{7,8},{8,9},{9,10},{10,1... | collective-permute-start | bytes 786440 | tf_op jit(solution)/shard_map/ppermute | solution.py:265
  151.0 5.6 %collective-permute-start.18 = (bf16[512,256]{1,0:T(8,128)(2,1)}, bf16[512,256]{1,0:T(8,128)(2,1)}, u32[]{:S(2)}, u32[]{:S(2)}) collective-permute-start(bf16[512,256]{1,0:T(8,128)(2,1)} %copy-done.9), channel_id=1, source_target_pairs={{1,0},{2,1},{3,2},{4,3},{5,4},{6,5},{7,6},{8,7},{9,8},{10,9},{11,1... | collective-permute-start | bytes 786440 | tf_op jit(solution)/shard_map/ppermute | solution.py:265
  156.7 4.1 %all-to-all-done.3 = bf16[64,8,256]{2,1,0:T(8,128)(2,1)} async-done(((bf16[64,8,256]{2,1,0:T(8,128)(2,1)}), bf16[64,8,256]{2,1,0:T(8,128)(2,1)}, u32[]{:S(2)}, u32[]{:S(2)}) %all-to-all-start.3) | async-done | bytes 262176 | tf_op jit(solution)/shard_map/all_to_all | solution.py:277
  160.8 1.3 moments.1
  162.2 3.2 %collective-permute-start.15 = (f32[384,128]{1,0:T(8,128)S(1)}, f32[384,128]{1,0:T(8,128)S(1)}, u32[]{:S(2)}, u32[]{:S(2)}) collective-permute-start(f32[384,128]{1,0:T(8,128)S(1)} %get-tuple-element.34.refs_0_), channel_id=1, source_target_pairs={{0,192},{64,0},{128,64},{192,128},{1,193},{65,1},{129,65},{193,129... | collective-permute-start | bytes 589832 | tf_op jit(solution)/shard_map/ppermute | solution.py:265
  165.5 1.6 copy-done.5
  167.0 5.0 %prior.1.image_ref = bf16[4096,256]{1,0:T(8,128)(2,1)S(1)} custom-call(s32[32,2]{1,0:T(8,128)S(1)} %copy.7.off_ref, bf16[32,3,128,128]{3,2,1,0:T(8,128)(2,1)S(1)} %copy-done.3, bf16[4096,256]{1,0:T(8,128)(2,1)S(1)} %copy-done.5, bf16[512,256]{1,0:T(8,128)(2,1)} %collective-permute-done.17.below_ref, bf16[512,256]{1,0:T(8,128)(2,1)} %collective-permute-done.18.above_ref), custom_call_target="tpu_custom_call" | custom-call | flops 1073741824 | tf_op jit(solution)/shard_map/prior/pallas_call | solution.py:22
  172.1 1.4 collective-permute-start.19
  173.5 1.9 %collective-permute-start.20 = (bf16[384,128]{1,0:T(8,128)(2,1)S(1)}, bf16[384,128]{1,0:T(8,128)(2,1)S(1)}, u32[]{:S(2)}, u32[]{:S(2)}) collective-permute-start(bf16[384,128]{1,0:T(8,128)(2,1)S(1)} %get-tuple-element.38.refs_0_), channel_id=1, source_target_pairs={{0,192},{64,0},{128,64},{192,128},{1,193},{65,1},{129,65},{193,129... | collective-permute-start | bytes 294920 | tf_op jit(solution)/shard_map/ppermute | solution.py:265
  175.4 2.3 %collective-permute-start.21 = (bf16[384,128]{1,0:T(8,128)(2,1)S(1)}, bf16[384,128]{1,0:T(8,128)(2,1)S(1)}, u32[]{:S(2)}, u32[]{:S(2)}) collective-permute-start(bf16[384,128]{1,0:T(8,128)(2,1)S(1)} %get-tuple-element.38.refs_0_), channel_id=1, source_target_pairs={{0,128},{64,192},{128,0},{192,64},{1,129},{65,193},{129,1},{193,65... | collective-permute-start | bytes 294920 | tf_op jit(solution)/shard_map/ppermute | solution.py:265
  177.7 9.9 %factor.1.inv_ref = f32[256,256]{1,0:T(8,128)S(1)} custom-call(f32[384,128]{1,0:T(8,128)S(1)} %get-tuple-element.34.refs_0_, f32[384,128]{1,0:T(8,128)S(1)} %collective-permute-done.14.refs_1_, f32[384,128]{1,0:T(8,128)S(1)} %collective-permute-done.15.refs_2_, f32[384,128]{1,0:T(8,128)S(1)} %collective-permute-done.16.refs_3_), custom_call_target="tpu_custom_call" | custom-call | flops 17179869184 | tf_op jit(solution)/shard_map/factor/pallas_call | solution.py:22
  187.6 4.6 %final.1 = (bf16[4096,256]{1,0:T(8,128)(2,1)}, bf16[4096,256]{1,0:T(8,128)(2,1)}, f32[256,256]{1,0:T(8,128)}) custom-call(f32[256,256]{1,0:T(8,128)S(1)} %factor.1.inv_ref, bf16[4096,256]{1,0:T(8,128)(2,1)S(1)} %copy-done.5, bf16[4096,256]{1,0:T(8,128)(2,1)S(1)} %prior.1.image_ref, bf16[384,128]{1,0:T(8,128)(2,1)S(1)} %get-tuple-element.38.refs_0_, ...), custom_call_target="tpu_custom_call" | custom-call | tf_op jit(solution)/shard_map/final/pallas_call | solution.py:391
  (40 shorter events, 1.2 us)
Async XLA Ops:
  1.4 1.9 copy-start.2
  3.3 2.2 %copy-start.6 = (bf16[512,4096]{1,0:T(8,128)(2,1)S(1)}, bf16[512,4096]{1,0:T(8,128)(2,1)}, u32[]{:S(2)}) copy-start(bf16[512,4096]{1,0:T(8,128)(2,1)} %jac_ref.3) | copy-start | bytes 12582916
  7.2 23.7 %collective-permute-start = (bf16[512,512]{1,0:T(8,128)(2,1)S(1)}, bf16[512,512]{1,0:T(8,128)(2,1)S(1)}, u32[]{:S(2)}, u32[]{:S(2)}) collective-permute-start(bf16[512,512]{1,0:T(8,128)(2,1)S(1)} %get-tuple-element.21), channel_id=1, source_target_pairs={{0,1},{1,2},{2,3},{3,4},{4,5},{5,6},{6,7},{7,8},{8,9},{9,10},{10,1... | collective-permute-start | bytes 1572872 | tf_op jit(solution)/shard_map/ppermute | solution.py:265
  9.2 21.8 %copy-start.7 = (bf16[4096,256]{1,0:T(8,128)(2,1)S(1)}, bf16[4096,256]{1,0:T(8,128)(2,1)}, u32[]{:S(2)}) copy-start(bf16[4096,256]{1,0:T(8,128)(2,1)} %probe_ref.1) | copy-start | bytes 6291460
  9.2 21.8 %collective-permute-start.1 = (bf16[512,512]{1,0:T(8,128)(2,1)S(1)}, bf16[512,512]{1,0:T(8,128)(2,1)S(1)}, u32[]{:S(2)}, u32[]{:S(2)}) collective-permute-start(bf16[512,512]{1,0:T(8,128)(2,1)S(1)} %get-tuple-element.22), channel_id=1, source_target_pairs={{1,0},{2,1},{3,2},{4,3},{5,4},{6,5},{7,6},{8,7},{9,8},{10,9},{11,1... | collective-permute-start | bytes 1572872 | tf_op jit(solution)/shard_map/ppermute | solution.py:265
  32.4 2.0 %copy-start = (bf16[512,4096]{1,0:T(8,128)(2,1)}, bf16[512,4096]{1,0:T(8,128)(2,1)S(1)}, u32[]{:S(2)}) copy-start(bf16[512,4096]{1,0:T(8,128)(2,1)S(1)} %get-tuple-element.24.full_ref) | copy-start | bytes 12582916
  56.3 18.0 %all-to-all-start.1 = ((bf16[64,8,256]{2,1,0:T(8,128)(2,1)}), bf16[64,8,256]{2,1,0:T(8,128)(2,1)S(1)}, u32[]{:S(2)}, u32[]{:S(2)}) async-start(bf16[64,8,256]{2,1,0:T(8,128)(2,1)} %total.2), calls=%async_computation.1 | async-start | bytes 524288 | tf_op jit(solution)/shard_map/all_to_all | solution.py:277
  74.3 2.2 %copy-start.1 = (bf16[512,4096]{1,0:T(8,128)(2,1)S(1)}, bf16[512,4096]{1,0:T(8,128)(2,1)}, u32[]{:S(2)}) copy-start(bf16[512,4096]{1,0:T(8,128)(2,1)} %copy-done) | copy-start | bytes 12582916
  77.8 9.0 %collective-permute-start.6 = (bf16[512,256]{1,0:T(8,128)(2,1)S(1)}, bf16[512,256]{1,0:T(8,128)(2,1)S(1)}, u32[]{:S(2)}, u32[]{:S(2)}) collective-permute-start(bf16[512,256]{1,0:T(8,128)(2,1)S(1)} %get-tuple-element.32), channel_id=1, source_target_pairs={{0,192},{64,0},{128,64},{192,128},{1,193},{65,1},{129,65},{193,129... | collective-permute-start | bytes 786440 | tf_op jit(solution)/shard_map/ppermute | solution.py:265
  80.9 10.4 %collective-permute-start.2 = (bf16[512,256]{1,0:T(8,128)(2,1)S(1)}, bf16[512,256]{1,0:T(8,128)(2,1)S(1)}, u32[]{:S(2)}, u32[]{:S(2)}) collective-permute-start(bf16[512,256]{1,0:T(8,128)(2,1)S(1)} %get-tuple-element.27), channel_id=1, source_target_pairs={{0,64},{64,128},{128,192},{192,0},{1,65},{65,129},{129,193},{193,1... | collective-permute-start | bytes 786440 | tf_op jit(solution)/shard_map/ppermute | solution.py:265
  80.9 16.0 %collective-permute-start.5 = (bf16[512,256]{1,0:T(8,128)(2,1)S(1)}, bf16[512,256]{1,0:T(8,128)(2,1)S(1)}, u32[]{:S(2)}, u32[]{:S(2)}) collective-permute-start(bf16[512,256]{1,0:T(8,128)(2,1)S(1)} %get-tuple-element.30), channel_id=1, source_target_pairs={{0,64},{64,128},{128,192},{192,0},{1,65},{65,129},{129,193},{193,1... | collective-permute-start | bytes 786440 | tf_op jit(solution)/shard_map/ppermute | solution.py:265
  86.9 10.5 %collective-permute-start.7 = (bf16[512,256]{1,0:T(8,128)(2,1)S(1)}, bf16[512,256]{1,0:T(8,128)(2,1)S(1)}, u32[]{:S(2)}, u32[]{:S(2)}) collective-permute-start(bf16[512,256]{1,0:T(8,128)(2,1)S(1)} %add_convert_fusion.1), channel_id=1, source_target_pairs={{0,192},{64,0},{128,64},{192,128},{1,193},{65,1},{129,65},{193,129... | collective-permute-start | bytes 786440 | tf_op jit(solution)/shard_map/ppermute | solution.py:265
  90.6 12.3 %collective-permute-start.4 = (bf16[512,256]{1,0:T(8,128)(2,1)S(1)}, bf16[512,256]{1,0:T(8,128)(2,1)S(1)}, u32[]{:S(2)}, u32[]{:S(2)}) collective-permute-start(bf16[512,256]{1,0:T(8,128)(2,1)S(1)} %get-tuple-element.28), channel_id=1, source_target_pairs={{0,192},{64,0},{128,64},{192,128},{1,193},{65,1},{129,65},{193,129... | collective-permute-start | bytes 786440 | tf_op jit(solution)/shard_map/ppermute | solution.py:265
  91.4 11.6 %collective-permute-start.3 = (bf16[512,256]{1,0:T(8,128)(2,1)S(1)}, bf16[512,256]{1,0:T(8,128)(2,1)S(1)}, u32[]{:S(2)}, u32[]{:S(2)}) collective-permute-start(bf16[512,256]{1,0:T(8,128)(2,1)S(1)} %add_convert_fusion.3), channel_id=1, source_target_pairs={{0,64},{64,128},{128,192},{192,0},{1,65},{65,129},{129,193},{193,1... | collective-permute-start | bytes 786440 | tf_op jit(solution)/shard_map/ppermute | solution.py:265
  97.4 11.1 %collective-permute-start.9 = (bf16[512,256]{1,0:T(8,128)(2,1)S(1)}, bf16[512,256]{1,0:T(8,128)(2,1)S(1)}, u32[]{:S(2)}, u32[]{:S(2)}) collective-permute-start(bf16[512,256]{1,0:T(8,128)(2,1)S(1)} %add_convert_fusion.refs_1_), channel_id=1, source_target_pairs={{0,192},{64,0},{128,64},{192,128},{1,193},{65,1},{129,65},{193,129... | collective-permute-start | bytes 786440 | tf_op jit(solution)/shard_map/ppermute | solution.py:265
  103.1 10.1 %collective-permute-start.10 = (bf16[512,256]{1,0:T(8,128)(2,1)S(1)}, bf16[512,256]{1,0:T(8,128)(2,1)S(1)}, u32[]{:S(2)}, u32[]{:S(2)}) collective-permute-start(bf16[512,256]{1,0:T(8,128)(2,1)S(1)} %add_convert_fusion.2.refs_0_), channel_id=1, source_target_pairs={{0,64},{64,128},{128,192},{192,0},{1,65},{65,129},{129,193},{193,1... | collective-permute-start | bytes 786440 | tf_op jit(solution)/shard_map/ppermute | solution.py:265
  103.2 15.3 %collective-permute-start.13 = (bf16[512,256]{1,0:T(8,128)(2,1)S(1)}, bf16[512,256]{1,0:T(8,128)(2,1)S(1)}, u32[]{:S(2)}, u32[]{:S(2)}) collective-permute-start(bf16[512,256]{1,0:T(8,128)(2,1)S(1)} %add_convert_fusion.refs_1_), channel_id=1, source_target_pairs={{0,64},{64,128},{128,192},{192,0},{1,65},{65,129},{129,193},{193,1... | collective-permute-start | bytes 786440 | tf_op jit(solution)/shard_map/ppermute | solution.py:265
  105.0 13.4 %collective-permute-start.8 = (bf16[512,256]{1,0:T(8,128)(2,1)S(1)}, bf16[512,256]{1,0:T(8,128)(2,1)S(1)}, u32[]{:S(2)}, u32[]{:S(2)}) collective-permute-start(bf16[512,256]{1,0:T(8,128)(2,1)S(1)} %add_convert_fusion.2.refs_0_), channel_id=1, source_target_pairs={{0,192},{64,0},{128,64},{192,128},{1,193},{65,1},{129,65},{193,129... | collective-permute-start | bytes 786440 | tf_op jit(solution)/shard_map/ppermute | solution.py:265
  108.6 9.9 %collective-permute-start.12 = (bf16[512,256]{1,0:T(8,128)(2,1)S(1)}, bf16[512,256]{1,0:T(8,128)(2,1)S(1)}, u32[]{:S(2)}, u32[]{:S(2)}) collective-permute-start(bf16[512,256]{1,0:T(8,128)(2,1)S(1)} %collective-permute-done.9.refs_3_), channel_id=1, source_target_pairs={{0,192},{64,0},{128,64},{192,128},{1,193},{65,1},{129,65},{193,129... | collective-permute-start | bytes 786440 | tf_op jit(solution)/shard_map/ppermute | solution.py:265
  113.2 8.1 %collective-permute-start.11 = (bf16[512,256]{1,0:T(8,128)(2,1)S(1)}, bf16[512,256]{1,0:T(8,128)(2,1)S(1)}, u32[]{:S(2)}, u32[]{:S(2)}) collective-permute-start(bf16[512,256]{1,0:T(8,128)(2,1)S(1)} %collective-permute-done.10.refs_6_), channel_id=1, source_target_pairs={{0,64},{64,128},{128,192},{192,0},{1,65},{65,129},{129,193},{193,1... | collective-permute-start | bytes 786440 | tf_op jit(solution)/shard_map/ppermute | solution.py:265
  121.3 44.2 %copy-start.3 = (bf16[32,3,128,128]{3,2,1,0:T(8,128)(2,1)S(1)}, bf16[32,3,128,128]{3,2,1,0:T(8,128)(2,1)}, u32[]{:S(2)}) copy-start(bf16[32,3,128,128]{3,2,1,0:T(8,128)(2,1)} %coef_ref.5) | copy-start | bytes 9437188
  122.6 1.3 copy-start.4
  123.9 17.6 %copy-start.9 = (bf16[512,256]{1,0:T(8,128)(2,1)}, bf16[512,256]{1,0:T(8,128)(2,1)S(1)}, u32[]{:S(2)}) copy-start(bf16[512,256]{1,0:T(8,128)(2,1)S(1)} %get-tuple-element.37) | copy-start | bytes 786436
  123.9 17.6 %copy-start.10 = (bf16[512,256]{1,0:T(8,128)(2,1)}, bf16[512,256]{1,0:T(8,128)(2,1)S(1)}, u32[]{:S(2)}) copy-start(bf16[512,256]{1,0:T(8,128)(2,1)S(1)} %get-tuple-element.36) | copy-start | bytes 786436
  141.6 0.7 copy-start.8
  142.3 18.4 %all-to-all-start.3 = ((bf16[64,8,256]{2,1,0:T(8,128)(2,1)}), bf16[64,8,256]{2,1,0:T(8,128)(2,1)}, u32[]{:S(2)}, u32[]{:S(2)}) async-start(bf16[64,8,256]{2,1,0:T(8,128)(2,1)} %copy-done.8), calls=%async_computation.3 | async-start | bytes 524288 | tf_op jit(solution)/shard_map/all_to_all | solution.py:277
  149.0 16.4 %collective-permute-start.17 = (bf16[512,256]{1,0:T(8,128)(2,1)}, bf16[512,256]{1,0:T(8,128)(2,1)}, u32[]{:S(2)}, u32[]{:S(2)}) collective-permute-start(bf16[512,256]{1,0:T(8,128)(2,1)} %copy-done.10), channel_id=1, source_target_pairs={{0,1},{1,2},{2,3},{3,4},{4,5},{5,6},{6,7},{7,8},{8,9},{9,10},{10,1... | collective-permute-start | bytes 786440 | tf_op jit(solution)/shard_map/ppermute | solution.py:265
  151.0 14.4 %collective-permute-start.18 = (bf16[512,256]{1,0:T(8,128)(2,1)}, bf16[512,256]{1,0:T(8,128)(2,1)}, u32[]{:S(2)}, u32[]{:S(2)}) collective-permute-start(bf16[512,256]{1,0:T(8,128)(2,1)} %copy-done.9), channel_id=1, source_target_pairs={{1,0},{2,1},{3,2},{4,3},{5,4},{6,5},{7,6},{8,7},{9,8},{10,9},{11,1... | collective-permute-start | bytes 786440 | tf_op jit(solution)/shard_map/ppermute | solution.py:265
  162.1 13.3 %collective-permute-start.14 = (f32[384,128]{1,0:T(8,128)S(1)}, f32[384,128]{1,0:T(8,128)S(1)}, u32[]{:S(2)}, u32[]{:S(2)}) collective-permute-start(f32[384,128]{1,0:T(8,128)S(1)} %get-tuple-element.34.refs_0_), channel_id=1, source_target_pairs={{0,64},{64,128},{128,192},{192,0},{1,65},{65,129},{129,193},{193,1... | collective-permute-start | bytes 589832 | tf_op jit(solution)/shard_map/ppermute | solution.py:265
  162.2 15.5 %collective-permute-start.15 = (f32[384,128]{1,0:T(8,128)S(1)}, f32[384,128]{1,0:T(8,128)S(1)}, u32[]{:S(2)}, u32[]{:S(2)}) collective-permute-start(f32[384,128]{1,0:T(8,128)S(1)} %get-tuple-element.34.refs_0_), channel_id=1, source_target_pairs={{0,192},{64,0},{128,64},{192,128},{1,193},{65,1},{129,65},{193,129... | collective-permute-start | bytes 589832 | tf_op jit(solution)/shard_map/ppermute | solution.py:265
  165.4 12.3 %collective-permute-start.16 = (f32[384,128]{1,0:T(8,128)S(1)}, f32[384,128]{1,0:T(8,128)S(1)}, u32[]{:S(2)}, u32[]{:S(2)}) collective-permute-start(f32[384,128]{1,0:T(8,128)S(1)} %get-tuple-element.34.refs_0_), channel_id=1, source_target_pairs={{0,128},{64,192},{128,0},{192,64},{1,129},{65,193},{129,1},{193,65... | collective-permute-start | bytes 589832 | tf_op jit(solution)/shard_map/ppermute | solution.py:265
  165.4 1.6 copy-start.5
  172.1 15.5 %collective-permute-start.19 = (bf16[384,128]{1,0:T(8,128)(2,1)S(1)}, bf16[384,128]{1,0:T(8,128)(2,1)S(1)}, u32[]{:S(2)}, u32[]{:S(2)}) collective-permute-start(bf16[384,128]{1,0:T(8,128)(2,1)S(1)} %get-tuple-element.38.refs_0_), channel_id=1, source_target_pairs={{0,64},{64,128},{128,192},{192,0},{1,65},{65,129},{129,193},{193,1... | collective-permute-start | bytes 294920 | tf_op jit(solution)/shard_map/ppermute | solution.py:265
  173.5 14.2 %collective-permute-start.20 = (bf16[384,128]{1,0:T(8,128)(2,1)S(1)}, bf16[384,128]{1,0:T(8,128)(2,1)S(1)}, u32[]{:S(2)}, u32[]{:S(2)}) collective-permute-start(bf16[384,128]{1,0:T(8,128)(2,1)S(1)} %get-tuple-element.38.refs_0_), channel_id=1, source_target_pairs={{0,192},{64,0},{128,64},{192,128},{1,193},{65,1},{129,65},{193,129... | collective-permute-start | bytes 294920 | tf_op jit(solution)/shard_map/ppermute | solution.py:265
  175.4 12.2 %collective-permute-start.21 = (bf16[384,128]{1,0:T(8,128)(2,1)S(1)}, bf16[384,128]{1,0:T(8,128)(2,1)S(1)}, u32[]{:S(2)}, u32[]{:S(2)}) collective-permute-start(bf16[384,128]{1,0:T(8,128)(2,1)S(1)} %get-tuple-element.38.refs_0_), channel_id=1, source_target_pairs={{0,128},{64,192},{128,0},{192,64},{1,129},{65,193},{129,1},{193,65... | collective-permute-start | bytes 294920 | tf_op jit(solution)/shard_map/ppermute | solution.py:265
where the time goes:
time: 193 us; the launch traced here: 192 us
  starting transfers between devices  59.9 us (31%)
  Pallas kernels  41.5 us (22%)
  blocking collectives  38.8 us (20%)
  waiting for transfers between devices  38.1 us (20%)
  local copies, waits for them, and re-layouts  12.6 us (7%)
    ppermute x22, starting transfers between devices, shifted(): return lax.ppermute(value, axis, pairs)  46.8 us
    all_to_all x2, blocking collectives, summed_over_par(): lax.all_to_all(part.reshape(count, rows // count, width), 'par', 0, 0, ti...  38.8 us
    pallas_call x10, Pallas kernels, call(): pl.pallas_call(kernel, name=name, out_shape=outs, in_specs=specs, out_spe...  36.9 us
    ppermute x22, waiting for transfers between devices, shifted(): return lax.ppermute(value, axis, pairs)  22.5 us
    all_to_all x2, waiting for transfers between devices, summed_over_par(): return lax.all_to_all(own, 'par', 0, 0, tiled=True).reshape(rows, width)  15.6 us
    all_to_all x2, starting transfers between devices, summed_over_par(): return lax.all_to_all(own, 'par', 0, 0, tiled=True).reshape(rows, width)  13.1 us
    unnamed x23, local copies, waits for them, and re-layouts  12.6 us
    pallas_call x1, Pallas kernels, body(): pl.pallas_call(functools.partial(final_kernel, 1.0 / total_obs), name='fi...  4.56 us
  transfers between devices with their start and end apart: 24, of which 11 were waited for; matrix products, arithmetic and copies ran while one was open for 0% of the time, Pallas kernels for 16%

commit v1 on v0

v1 whole, which is shorter than its diff:
```python
import functools

import jax
import jax.numpy as jnp
from jax import lax
from jax.experimental import pallas as pl
from jax.experimental.pallas import tpu as pltpu
from jax.sharding import PartitionSpec as P

BLK = 128
REACH = 4
EDGE = REACH * BLK
NB = 64
F32 = jnp.float32
BF16 = jnp.bfloat16
HI = lax.Precision.HIGHEST
VMEM = pl.BlockSpec(memory_space=pltpu.VMEM)
SMEM = pl.BlockSpec(memory_space=pltpu.SMEM)


def call(kernel, name, outs, specs, args, scratch=(), mib=24, flops=0):
    return pl.pallas_call(
        kernel,
        name=name,
        out_shape=outs,
        in_specs=specs,
        out_specs=jax.tree.map(lambda _: VMEM, outs),
        scratch_shapes=scratch,
        compiler_params=pltpu.CompilerParams(vmem_limit_bytes=mib * 2**20),
        cost_estimate=pl.CostEstimate(flops=flops, bytes_accessed=0, transcendentals=0),
    )(*args)


def dot(a, b):
    return jnp.dot(a, b, preferred_element_type=F32)


def dot_tn(a, b, precision=None):
    return lax.dot_general(a, b, (((0,), (0,)), ((), ())), precision=precision, preferred_element_type=F32)


def dot_nt(a, b, precision=None):
    return lax.dot_general(a, b, (((1,), (1,)), ((), ())), precision=precision, preferred_element_type=F32)


def shape(*dims, dtype=BF16):
    return jax.ShapeDtypeStruct(dims, dtype)


def edges_kernel(count, off_ref, jac_low, jac_high, coef_low, coef_high, low_ref, high_ref, acc):
    acc[...] = jnp.zeros_like(acc)
    for side, (jac, coef) in enumerate(((jac_low, coef_low), (jac_high, coef_high))):
        for i in range(REACH):
            block = i + side * (count - REACH)
            columns = jac[:, i * BLK : (i + 1) * BLK]
            for j in range(2):
                target = block + off_ref[j, block]
                place = target + REACH if side == 0 else target - count + REACH
                outside = target < 0 if side == 0 else target >= count

                @pl.when(outside)
                def _():
                    acc[place] += dot(columns, coef[i, j + 1])

    for i in range(REACH):
        low_ref[:, i * BLK : (i + 1) * BLK] = acc[i].astype(BF16)
        high_ref[:, i * BLK : (i + 1) * BLK] = acc[i + REACH].astype(BF16)


def own_kernel(off_ref, jac_ref, coef_ref, out_ref, acc):
    count = coef_ref.shape[0]
    for i in range(REACH):
        acc[i] = jnp.zeros_like(acc[i])
        acc[count + REACH + i] = jnp.zeros_like(acc[i])

    def diagonal(block, carry):
        columns = jac_ref[:, pl.ds(pl.multiple_of(block * BLK, BLK), BLK)]
        acc[block + REACH] = dot(columns, coef_ref[block, 0])
        return carry

    lax.fori_loop(0, count, diagonal, 0, unroll=4)

    def band(block, carry):
        columns = jac_ref[:, pl.ds(pl.multiple_of(block * BLK, BLK), BLK)]
        for j in range(2):
            acc[block + REACH + off_ref[j, block]] += dot(columns, coef_ref[block, j + 1])
        return carry

    lax.fori_loop(0, count, band, 0, unroll=4)
    for block in range(count):
        out_ref[:, block * BLK : (block + 1) * BLK] = acc[block + REACH].astype(BF16)


def forward_kernel(me_ref, own_ref, left_ref, right_ref, probe_ref, full_ref, keep_ref, give_ref):
    width = own_ref.shape[1]
    first = (own_ref[:, :EDGE].astype(F32) + left_ref[...].astype(F32)).astype(BF16)
    last = (own_ref[:, width - EDGE :].astype(F32) + right_ref[...].astype(F32)).astype(BF16)
    full_ref[:, :EDGE] = first
    full_ref[:, EDGE : width - EDGE] = own_ref[:, EDGE : width - EDGE]
    full_ref[:, width - EDGE :] = last
    rows = keep_ref.shape[0]
    core = me_ref[1]
    keep_ref[...] = dot(full_ref[pl.ds(pl.multiple_of(core * rows, rows), rows), :], probe_ref[...]).astype(BF16)
    give_ref[...] = dot(full_ref[pl.ds(pl.multiple_of((1 - core) * rows, rows), rows), :], probe_ref[...]).astype(BF16)


def pair_kernel(keep_ref, come_ref, out_ref):
    out_ref[...] = (keep_ref[...].astype(F32) + come_ref[...].astype(F32)).astype(BF16)


def total_kernel(parts_ref, out_ref):
    total = parts_ref[0].astype(F32)
    for i in range(1, parts_ref.shape[0]):
        total += parts_ref[i].astype(F32)
    total = total.astype(BF16)
    for i in range(out_ref.shape[0]):
        out_ref[i] = total


def in_order(me_ref, mine_ref, other_ref, out):
    rows = mine_ref.shape[0]
    out[pl.ds(pl.multiple_of(me_ref[1] * rows, rows), rows), :] = mine_ref[...]
    out[pl.ds(pl.multiple_of((1 - me_ref[1]) * rows, rows), rows), :] = other_ref[...]


def sample_kernel(ranks, me_ref, full_ref, mine_ref, other_ref, *refs):
    outs, fwd = refs[:-1], refs[-1]
    rows = full_ref.shape[1] // ranks // 2
    in_order(me_ref, mine_ref, other_ref, fwd)
    for rel in range(ranks):
        owner = lax.rem(me_ref[0] + rel, ranks)
        for half in range(2):
            start = pl.multiple_of(owner * (2 * rows) + half * rows, rows)
            outs[2 * rel + half][...] = dot_tn(full_ref[:, pl.ds(start, rows)], fwd[...]).astype(BF16)


def project_kernel(ranks, me_ref, full_ref, *refs):
    pieces = refs[: 2 * ranks]
    sample_ref, low_ref, high_ref, keep_ref, give_ref, acc = refs[2 * ranks :]
    rows = pieces[0].shape[0]
    total = jnp.zeros(acc.shape, F32)
    for rel in range(ranks):
        owner = lax.rem(me_ref[0] + rel, ranks)
        for half in range(2):
            piece = pieces[2 * rel + half][...]
            start = pl.multiple_of(owner * (2 * rows) + half * rows, rows)
            sample_ref[pl.ds(start, rows), :] = piece
            total += dot(full_ref[:, pl.ds(start, rows)], piece)
    acc[...] = total
    rows = keep_ref.shape[0]
    core = me_ref[1]
    keep_ref[...] = acc[pl.ds(pl.multiple_of(core * rows, rows), rows), :].astype(BF16)
    give_ref[...] = acc[pl.ds(pl.multiple_of((1 - core) * rows, rows), rows), :].astype(BF16)
    low_ref[...] = sample_ref[:EDGE, :]
    high_ref[...] = sample_ref[sample_ref.shape[0] - EDGE :, :]


def prior_kernel(off_ref, coef_ref, sample_ref, below_ref, above_ref, out_ref, ext):
    count, rows = coef_ref.shape[0], sample_ref.shape[0]
    ext[:EDGE] = below_ref[...]
    ext[EDGE : EDGE + rows] = sample_ref[...]
    ext[EDGE + rows :] = above_ref[...]

    def apply(block, carry):
        starts = [(block + REACH) * BLK] + [(block + REACH + off_ref[j, block]) * BLK for j in range(2)]
        result = sum(dot(coef_ref[block, j], ext[pl.ds(pl.multiple_of(starts[j], BLK), BLK), :]) for j in range(3))
        out_ref[pl.ds(pl.multiple_of(block * BLK, BLK), BLK), :] = result.astype(BF16)
        return carry

    lax.fori_loop(0, count, apply, 0, unroll=4)


def packed(full):
    return jnp.concatenate(
        [
            full[:NB, : 2 * NB],
            full[:NB, 2 * NB :],
            full[NB : 2 * NB, NB : 3 * NB],
            full[2 * NB : 3 * NB, 2 * NB :],
            jnp.concatenate([full[NB : 2 * NB, 3 * NB :], full[3 * NB :, 3 * NB :]], axis=1),
        ],
        axis=0,
    )


def unpacked(pack):
    r = [pack[i * NB : (i + 1) * NB] for i in range(5)]
    zero = jnp.zeros((NB, NB), F32)
    join = lambda *p: jnp.concatenate(p, axis=1)
    return jnp.concatenate(
        [join(r[0], r[1]), join(zero, r[2], r[4][:, :NB]), join(zero, zero, r[3]), join(zero, zero, zero, r[4][:, NB:])],
        axis=0,
    )


def moments_kernel(me_ref, fwd_mine, fwd_other, proj_mine, proj_other, out_ref, fwd, proj):
    in_order(me_ref, fwd_mine, fwd_other, fwd)
    in_order(me_ref, proj_mine, proj_other, proj)
    gram = dot_tn(fwd[...], proj[...])
    gram = packed(0.5 * (gram + gram.T))
    rows = gram.shape[0]
    high = gram.astype(BF16)
    out_ref[:rows] = high
    out_ref[rows : 2 * rows] = (gram - high.astype(F32)).astype(BF16)
    out_ref[2 * rows :] = packed(dot_tn(proj[...], proj[...])).astype(BF16)


def row_of(tile, k):
    return jnp.broadcast_to(tile[k : k + 1, :], tile.shape)


def lane_of(tile, k):
    return jnp.broadcast_to(tile[:, k : k + 1], (8, 2 * NB))


def factor_inverse(block):
    index = [lax.broadcasted_iota(jnp.int32, (NB, NB), d) for d in (0, 1)]
    wide = jnp.concatenate([block, (index[0] == index[1]).astype(F32)], axis=1)
    groups = NB // 8
    tiles = [wide[8 * t : 8 * t + 8] for t in range(groups)]
    row = lax.broadcasted_iota(jnp.int32, (8, 2 * NB), 0)
    out = []
    for g in range(groups):
        cols = {t: [lane_of(tiles[t], 8 * g + k) for k in range(8)] for t in range(g, groups)}
        scale = jnp.ones((8, 2 * NB), F32)
        for k in range(8):
            root = lax.rsqrt(row_of(cols[g][k], k))
            inverse = root * root
            scale = jnp.where(row == k, root, scale)
            pivot_row = row_of(tiles[g], k)
            heads = [row_of(cols[g][j], k) for j in range(k + 1, 8)]
            for t in range(g, groups):
                ratio = cols[t][k] * inverse
                if t == g:
                    ratio = jnp.where(row > k, ratio, 0.0)
                tiles[t] = tiles[t] - ratio * pivot_row
                for j in range(k + 1, 8):
                    cols[t][j] = cols[t][j] - ratio * heads[j - k - 1]
        out.append(tiles[g] * scale)
    return jnp.concatenate(out, axis=0)[:, NB:]


def factor_kernel(scale, *refs):
    parts, (out_ref, second_ref, a_ref, m_ref) = refs[:-4], refs[-4:]
    n = out_ref.shape[0]
    total = parts[0][...].astype(F32)
    for part in parts[1:]:
        total += part[...].astype(F32)
    rows = total.shape[0] // 3
    a_ref[...] = unpacked((total[:rows] + total[rows : 2 * rows]) * scale)
    upper = unpacked(total[2 * rows :])
    index = [lax.broadcasted_iota(jnp.int32, (n, n), d) for d in (0, 1)]
    second_ref[...] = jnp.where(index[0] <= index[1], upper, upper.T)
    m_ref[...] = jnp.zeros((n, n), F32)
    out_ref[...] = jnp.zeros((n, n), F32)
    for lo in range(0, n, NB):
        hi = lo + NB
        inverse = factor_inverse(a_ref[lo:hi, lo:hi])
        out_ref[lo:hi, lo:hi] = inverse
        if lo:
            out_ref[lo:hi, :lo] = jnp.dot(inverse, m_ref[lo:hi, :lo], precision=HI, preferred_element_type=F32)
        if hi < n:
            upper = jnp.dot(inverse, a_ref[lo:hi, hi:], precision=HI, preferred_element_type=F32)
            a_ref[hi:, hi:] -= dot_tn(upper, upper, HI)
            m_ref[hi:, :hi] -= dot_tn(upper, out_ref[lo:hi, :hi], HI)


def final_kernel(scale, inv_ref, rows_ref, second_ref, sample_ref, image_ref, basis_ref, mapped_ref, ritz_ref):
    low = inv_ref[...].astype(BF16)
    basis_ref[...] = dot_nt(sample_ref[...], low).astype(BF16)
    mapped_ref[...] = dot_nt(image_ref[...], low).astype(BF16)
    left = jnp.dot(rows_ref[...], second_ref[...], precision=HI, preferred_element_type=F32)
    ritz_ref[...] = dot_nt(left, inv_ref[...], HI) * scale


def shifted(value, axis, by, wrap=True):
    count = lax.axis_size(axis)
    pairs = [(i, (i + by) % count) for i in range(count) if wrap or 0 <= i + by < count]
    return lax.ppermute(value, axis, pairs)


def added(*values):
    return sum(v.astype(F32) for v in values).astype(BF16)


def swapped(value):
    return lax.ppermute(value, "par", [(i, i ^ 1) for i in range(lax.axis_size("par"))])


def summed_over_par(keep, give):
    rows, width = keep.shape
    chips = lax.axis_size("par") // 2
    groups = [[2 * i + core for i in range(chips)] for core in range(2)]
    part = call(pair_kernel, "pair", shape(rows, width), [VMEM] * 2, [keep, swapped(give)], mib=4)
    exchange = lambda x: lax.all_to_all(x, "par", 0, 0, axis_index_groups=groups, tiled=True)
    parts = exchange(part.reshape(chips, rows // chips, width))
    own = call(total_kernel, "total", shape(*parts.shape), [VMEM], [parts], mib=4)
    mine = exchange(own).reshape(rows, width)
    return mine, swapped(mine)


def body(jacobian, probes, coeffs, offsets):
    ranks = lax.axis_size("obs")
    nobs, npar = jacobian.shape[0], jacobian.shape[1]
    width = probes.shape[1]
    count = coeffs.shape[0]
    me = jnp.stack([lax.axis_index("obs"), lax.axis_index("par") % 2])
    offsets = offsets.T
    flops = 2 * nobs * npar * width

    low, high = call(
        functools.partial(edges_kernel, count),
        "edges",
        [shape(nobs, EDGE)] * 2,
        [SMEM] + [VMEM] * 4,
        [offsets, jacobian[:, :EDGE], jacobian[:, npar - EDGE :], coeffs[:REACH], coeffs[count - REACH :]],
        [pltpu.VMEM((2 * REACH, nobs, BLK), F32)],
        mib=8,
        flops=flops // 4,
    )
    from_left = shifted(high, "par", 1, False)
    from_right = shifted(low, "par", -1, False)
    own = call(
        own_kernel,
        "own",
        shape(nobs, npar),
        [SMEM, VMEM, VMEM],
        [offsets, jacobian, coeffs],
        [pltpu.VMEM((count + 2 * REACH, nobs, BLK), F32)],
        flops=4 * flops,
    )
    half = shape(nobs // 2, width)
    full, keep, give = call(
        forward_kernel,
        "forward",
        [shape(nobs, npar), half, half],
        [SMEM] + [VMEM] * 4,
        [me, own, from_left, from_right, probes],
        flops=flops,
    )
    forward = summed_over_par(keep, give)

    pieces = call(
        functools.partial(sample_kernel, ranks),
        "sample",
        [shape(npar // ranks // 2, width)] * (2 * ranks),
        [SMEM] + [VMEM] * 3,
        [me, full, *forward],
        [pltpu.VMEM((nobs, width), BF16)],
        flops=flops,
    )
    here0, here1, right0, right1, far0, far1, left0, left1 = pieces
    via_left = shifted(far0, "obs", 1)
    via_right = shifted(far1, "obs", -1)
    a1 = shifted(right1, "obs", 1)
    b0 = shifted(left0, "obs", -1)
    a0 = shifted(added(right0, via_left), "obs", 1)
    b1 = shifted(added(left1, via_right), "obs", -1)
    sum0 = added(here0, a0, b0)
    sum1 = added(here1, a1, b1)

    l0 = shifted(sum0, "obs", 1)
    r1 = shifted(sum1, "obs", -1)
    l1 = shifted(sum1, "obs", 1)
    r0 = shifted(sum0, "obs", -1)
    f0 = shifted(l0, "obs", 1)
    f1 = shifted(r1, "obs", -1)

    edge = shape(EDGE, width)
    sample, tail_low, tail_high, keep, give = call(
        functools.partial(project_kernel, ranks),
        "project",
        [shape(npar, width), edge, edge, half, half],
        [SMEM] + [VMEM] * (1 + 2 * ranks),
        [me, full, sum0, sum1, r0, r1, f0, f1, l0, l1],
        [pltpu.VMEM((nobs, width), F32)],
        flops=flops,
    )
    below = shifted(tail_high, "par", 1, False)
    above = shifted(tail_low, "par", -1, False)
    projected = summed_over_par(keep, give)
    moments = call(
        moments_kernel,
        "moments",
        shape(15 * NB, 2 * NB),
        [SMEM] + [VMEM] * 4,
        [me, *forward, *projected],
        [pltpu.VMEM((nobs, width), BF16)] * 2,
        mib=8,
        flops=flops // 8,
    )
    parts = [moments] + [shifted(moments, "obs", by) for by in (1, -1, 2)]
    image = call(
        prior_kernel,
        "prior",
        shape(npar, width),
        [SMEM] + [VMEM] * 4,
        [offsets, coeffs, sample, below, above],
        [pltpu.VMEM((npar + 2 * EDGE, width), BF16)],
        mib=8,
        flops=flops,
    )
    total_par = npar * lax.axis_size("par")
    square = shape(width, width, dtype=F32)
    inverse, second = call(
        functools.partial(factor_kernel, 1.0 / total_par),
        "factor",
        [square, square],
        [VMEM] * len(parts),
        parts,
        [pltpu.VMEM((width, width), F32)] * 2,
        mib=8,
        flops=16 * flops,
    )
    steps = 4
    whole = pl.BlockSpec((width, width), lambda i: (0, 0))
    by_rows = pl.BlockSpec((npar // steps, width), lambda i: (i, 0))
    few = pl.BlockSpec((width // steps, width), lambda i: (i, 0))
    return pl.pallas_call(
        functools.partial(final_kernel, 1.0 / (nobs * ranks)),
        name="final",
        grid=(steps,),
        out_shape=[shape(npar, width), shape(npar, width), square],
        in_specs=[whole, few, whole, by_rows, by_rows],
        out_specs=[by_rows, by_rows, few],
        compiler_params=pltpu.CompilerParams(vmem_limit_bytes=12 * 2**20),
    )(inverse, inverse, second, sample, image)


def solution(mesh):
    return jax.shard_map(
        body,
        mesh=mesh,
        in_specs=(P("obs", "par"), P("par", None), P("par", None, None, None), P("par", None)),
        out_specs=(P("par", None), P("par", None), P()),
        check_vma=False,
    )
```

time: 193 us -> 178 us (0.922); the launches traced: 192 us -> 175 us
  starting transfers between devices: 59.9 us -> 32.1 us
  blocking collectives: 38.8 us -> 59.4 us
  local copies, waits for them, and re-layouts: 12.6 us -> 4.8 us
  Pallas kernels: 41.5 us -> 38.3 us
    all_to_all x2 -> x4, blocking collectives: 38.8 us -> 59.4 us  [summed_over_par(): lax.all_to_all(x, 'par', 0, 0, axis_index_groups=groups, tiled=True)]
    all_to_all x2 -> x0, waiting for transfers between devices: 15.6 us -> none  [summed_over_par(): return lax.all_to_all(own, 'par', 0, 0, tiled=True).reshape(rows, width)]
    ppermute x22 -> x19, starting transfers between devices: 46.8 us -> 31.9 us  [shifted(): return lax.ppermute(value, axis, pairs)]
    all_to_all x2 -> x0, starting transfers between devices: 13.1 us -> none  [summed_over_par(): return lax.all_to_all(own, 'par', 0, 0, tiled=True).reshape(rows, width)]
    ppermute x22 -> x19, waiting for transfers between devices: 22.5 us -> 35.1 us  [shifted(): return lax.ppermute(value, axis, pairs)]
    unnamed x23 -> x8, local copies, waits for them, and re-layouts: 12.6 us -> 2.2 us
    pallas_call x10 -> x12, Pallas kernels: 36.9 us -> 32.7 us  [call(): pl.pallas_call(kernel, name=name, out_shape=outs, in_specs=specs, out_spe...]
    ppermute x0 -> x4, waiting for transfers between devices: none -> 4.02 us  [swapped(): lax.ppermute(value, 'par', [(i, i ^ 1) for i in range(lax.axis_size('par'...]
  transfers between devices with their start and end apart: 24 -> 23, of which waited for: 11 -> 16; matrix products, arithmetic and copies ran while one was open for 0% -> 0% of each run, Pallas kernels for 16% -> 7%
where the time goes in v1:
time: 178 us; the launch traced here: 175 us
  blocking collectives  59.4 us (33%)
  waiting for transfers between devices  39.1 us (22%)
  Pallas kernels  38.3 us (22%)
  starting transfers between devices  32.1 us (18%)
  local copies, waits for them, and re-layouts  4.8 us (3%)
    all_to_all x4, blocking collectives, summed_over_par(): lax.all_to_all(x, 'par', 0, 0, axis_index_groups=groups, tiled=True)  59.4 us
    ppermute x19, waiting for transfers between devices, shifted(): return lax.ppermute(value, axis, pairs)  35.1 us
    pallas_call x12, Pallas kernels, call(): pl.pallas_call(kernel, name=name, out_shape=outs, in_specs=specs, out_spe...  32.7 us
    ppermute x19, starting transfers between devices, shifted(): return lax.ppermute(value, axis, pairs)  31.9 us
    pallas_call x1, Pallas kernels, body(): pl.pallas_call(functools.partial(final_kernel, 1.0 / (nobs * ranks)), nam...  5.56 us
    ppermute x4, waiting for transfers between devices, swapped(): lax.ppermute(value, 'par', [(i, i ^ 1) for i in range(lax.axis_size('par'...  4.02 us
  transfers between devices with their start and end apart: 23, of which 16 were waited for; matrix products, arithmetic and copies ran while one was open for 0% of the time, Pallas kernels for 7%

profile of v1, /device:TPU:6, one launch (start us, length us, event | category | flops | bytes accessed | tf_op | source)
XLA Modules:
  0.0 174.9 jit_solution(4119587127535546650)
XLA Ops:
  0.7 1.3 fusion.1
  2.0 1.3 fusion
  3.3 2.8 %edges.1 = (bf16[512,512]{1,0:T(8,128)(2,1)}, bf16[512,512]{1,0:T(8,128)(2,1)}) custom-call(s32[2,32]{1,0:T(2,128)S(1)} %bitcast.14, bf16[512,512]{1,0:T(8,128)(2,1)S(1)} %get-tuple-element.44.jac_low, bf16[512,512]{1,0:T(8,128)(2,1)S(1)} %get-tuple-element.43.jac_high, bf16[4,3,128,128]{3,2,1,0:T(8,128)(2,1)S(1)} %get-tuple-element.46.coef_low, ...), custom_call_target="tpu_custom_call" | custom-call | flops 268435456 | tf_op jit(solution)/shard_map/edges/pallas_call | solution.py:22
  6.1 2.1 %collective-permute-start = (bf16[512,512]{1,0:T(8,128)(2,1)}, bf16[512,512]{1,0:T(8,128)(2,1)}, u32[]{:S(2)}, u32[]{:S(2)}) collective-permute-start(bf16[512,512]{1,0:T(8,128)(2,1)} %get-tuple-element.23), channel_id=1, source_target_pairs={{0,1},{1,2},{2,3},{3,4},{4,5},{5,6},{6,7},{7,8},{8,9},{9,10},{10,1... | collective-permute-start | bytes 1572872 | tf_op jit(solution)/shard_map/ppermute | solution.py:279
  8.2 6.8 %collective-permute-start.1 = (bf16[512,512]{1,0:T(8,128)(2,1)}, bf16[512,512]{1,0:T(8,128)(2,1)}, u32[]{:S(2)}, u32[]{:S(2)}) collective-permute-start(bf16[512,512]{1,0:T(8,128)(2,1)} %get-tuple-element.24), channel_id=1, source_target_pairs={{1,0},{2,1},{3,2},{4,3},{5,4},{6,5},{7,6},{8,7},{9,8},{10,9},{11,1... | collective-permute-start | bytes 1572872 | tf_op jit(solution)/shard_map/ppermute | solution.py:279
  15.1 2.2 %copy-done.2 = bf16[512,4096]{1,0:T(8,128)(2,1)S(1)} copy-done((bf16[512,4096]{1,0:T(8,128)(2,1)S(1)}, bf16[512,4096]{1,0:T(8,128)(2,1)}, u32[]{:S(2)}) %copy-start.2) | copy-done | bytes 4194328
  17.3 7.9 %own.1.own_ref = bf16[512,4096]{1,0:T(8,128)(2,1)S(1)} custom-call(s32[2,32]{1,0:T(2,128)S(1)} %bitcast.15, bf16[512,4096]{1,0:T(8,128)(2,1)S(1)} %copy-done.2, bf16[32,3,128,128]{3,2,1,0:T(8,128)(2,1)S(1)} %copy-done), custom_call_target="tpu_custom_call" | custom-call | flops 4294967296 | tf_op jit(solution)/shard_map/own/pallas_call | solution.py:22
  25.2 3.1 %forward.1 = (bf16[512,4096]{1,0:T(8,128)(2,1)S(1)}, bf16[256,256]{1,0:T(8,128)(2,1)S(1)}, bf16[256,256]{1,0:T(8,128)(2,1)S(1)}) custom-call(s32[2]{0:T(128)S(1)} %pad_add_fusion.me_ref, bf16[512,4096]{1,0:T(8,128)(2,1)S(1)} %own.1.own_ref, bf16[512,512]{1,0:T(8,128)(2,1)} %collective-permute-done.left_ref, ...), custom_call_target="tpu_custom_call" | custom-call | flops 1073741824 | tf_op jit(solution)/shard_map/forward/pallas_call | solution.py:22
  28.4 1.3 collective-permute-done.2.come_ref
  29.8 17.4 %all_to_all.20.parts_ref = bf16[32,8,256]{2,1,0:T(8,128)(2,1)S(1)} all-to-all(bf16[32,8,256]{2,1,0:T(8,128)(2,1)S(1)} %bitcast.10), channel_id=1, replica_groups={{0,2,4,6,8,10,12,14,16,18,20,22,24,26,28,30,32,34,36,38,40,42,44,46,48,..., dimensions={0} | all-to-all | bytes 262144 | tf_op jit(solution)/shard_map/all_to_all | solution.py:295
  47.2 13.9 %all_to_all.21 = bf16[32,8,256]{2,1,0:T(8,128)(2,1)S(1)} all-to-all(bf16[32,8,256]{2,1,0:T(8,128)(2,1)S(1)} %total.2), channel_id=1, replica_groups={{0,2,4,6,8,10,12,14,16,18,20,22,24,26,28,30,32,34,36,38,40,42,44,46,48,..., dimensions={0} | all-to-all | bytes 262144 | tf_op jit(solution)/shard_map/all_to_all | solution.py:295
  61.2 1.3 collective-permute-done.3.other_ref.fwd_other
  62.5 2.0 %sample.1 = (bf16[512,256]{1,0:T(8,128)(2,1)S(1)}, bf16[512,256]{1,0:T(8,128)(2,1)S(1)}, bf16[512,256]{1,0:T(8,128)(2,1)S(1)}, bf16[512,256]{1,0:T(8,128)(2,1)S(...) custom-call(s32[2]{0:T(128)S(1)} %pad_add_fusion.me_ref, ...), custom_call_target="tpu_custom_call" | custom-call | flops 1073741824 | tf_op jit(solution)/shard_map/sample/pallas_call | solution.py:22
  64.5 1.7 collective-permute-start.4
  66.1 1.7 collective-permute-start.8
  67.8 1.8 %collective-permute-start.6 = (bf16[512,256]{1,0:T(8,128)(2,1)S(1)}, bf16[512,256]{1,0:T(8,128)(2,1)S(1)}, u32[]{:S(2)}, u32[]{:S(2)}) collective-permute-start(bf16[512,256]{1,0:T(8,128)(2,1)S(1)} %get-tuple-element.31), channel_id=1, source_target_pairs={{0,192},{64,0},{128,64},{192,128},{1,193},{65,1},{129,65},{193,129... | collective-permute-start | bytes 786440 | tf_op jit(solution)/shard_map/ppermute | solution.py:279
  69.6 4.6 %collective-permute-done.4 = bf16[512,256]{1,0:T(8,128)(2,1)S(1)} collective-permute-done((bf16[512,256]{1,0:T(8,128)(2,1)S(1)}, bf16[512,256]{1,0:T(8,128)(2,1)S(1)}, u32[]{:S(2)}, u32[]{:S(2)}) %collective-permute-start.4) | collective-permute-done | bytes 262176 | tf_op jit(solution)/shard_map/ppermute | solution.py:279
  74.3 0.4 collective-permute-start.5
  74.7 1.6 collective-permute-start.7
  76.3 2.0 %collective-permute-start.9 = (bf16[512,256]{1,0:T(8,128)(2,1)S(1)}, bf16[512,256]{1,0:T(8,128)(2,1)S(1)}, u32[]{:S(2)}, u32[]{:S(2)}) collective-permute-start(bf16[512,256]{1,0:T(8,128)(2,1)S(1)} %add_convert_fusion.1), channel_id=1, source_target_pairs={{0,192},{64,0},{128,64},{192,128},{1,193},{65,1},{129,65},{193,129... | collective-permute-start | bytes 786440 | tf_op jit(solution)/shard_map/ppermute | solution.py:279
  78.3 2.6 %collective-permute-done.6 = bf16[512,256]{1,0:T(8,128)(2,1)S(1)} collective-permute-done((bf16[512,256]{1,0:T(8,128)(2,1)S(1)}, bf16[512,256]{1,0:T(8,128)(2,1)S(1)}, u32[]{:S(2)}, u32[]{:S(2)}) %collective-permute-start.6) | collective-permute-done | bytes 262176 | tf_op jit(solution)/shard_map/ppermute | solution.py:279
  80.9 3.8 %collective-permute-done.5 = bf16[512,256]{1,0:T(8,128)(2,1)S(1)} collective-permute-done((bf16[512,256]{1,0:T(8,128)(2,1)S(1)}, bf16[512,256]{1,0:T(8,128)(2,1)S(1)}, u32[]{:S(2)}, u32[]{:S(2)}) %collective-permute-start.5) | collective-permute-done | bytes 262176 | tf_op jit(solution)/shard_map/ppermute | solution.py:279
  84.9 5.4 %collective-permute-done.7 = bf16[512,256]{1,0:T(8,128)(2,1)S(1)} collective-permute-done((bf16[512,256]{1,0:T(8,128)(2,1)S(1)}, bf16[512,256]{1,0:T(8,128)(2,1)S(1)}, u32[]{:S(2)}, u32[]{:S(2)}) %collective-permute-start.7) | collective-permute-done | bytes 262176 | tf_op jit(solution)/shard_map/ppermute | solution.py:279
  90.5 0.6 collective-permute-start.11
  91.1 0.7 collective-permute-start.10
  91.8 1.3 collective-permute-start.15
  93.1 2.9 %collective-permute-done.12.refs_6_ = bf16[512,256]{1,0:T(8,128)(2,1)S(1)} collective-permute-done((bf16[512,256]{1,0:T(8,128)(2,1)S(1)}, bf16[512,256]{1,0:T(8,128)(2,1)S(1)}, u32[]{:S(2)}, u32[]{:S(2)}) %collective-permute-start.12) | collective-permute-done | bytes 262176 | tf_op jit(solution)/shard_map/ppermute | solution.py:279
  96.0 3.7 %collective-permute-done.11.refs_3_ = bf16[512,256]{1,0:T(8,128)(2,1)S(1)} collective-permute-done((bf16[512,256]{1,0:T(8,128)(2,1)S(1)}, bf16[512,256]{1,0:T(8,128)(2,1)S(1)}, u32[]{:S(2)}, u32[]{:S(2)}) %collective-permute-start.11) | collective-permute-done | bytes 262176 | tf_op jit(solution)/shard_map/ppermute | solution.py:279
  99.7 0.8 collective-permute-start.14
  100.5 3.5 %collective-permute-done.10.refs_2_ = bf16[512,256]{1,0:T(8,128)(2,1)S(1)} collective-permute-done((bf16[512,256]{1,0:T(8,128)(2,1)S(1)}, bf16[512,256]{1,0:T(8,128)(2,1)S(1)}, u32[]{:S(2)}, u32[]{:S(2)}) %collective-permute-start.10) | collective-permute-done | bytes 262176 | tf_op jit(solution)/shard_map/ppermute | solution.py:279
  104.0 1.5 collective-permute-done.13.refs_4_
  105.6 1.3 collective-permute-done.14.refs_5_
  106.9 1.9 %project.1 = (bf16[4096,256]{1,0:T(8,128)(2,1)S(1)}, bf16[512,256]{1,0:T(8,128)(2,1)S(1)}, bf16[512,256]{1,0:T(8,128)(2,1)S(1)}, bf16[256,256]{1,0:T(8,128)(2,1)S(1)}, bf16[256,256]{1,0:T(8,128)(2,1)S(1)}) custom-call(s32[2]{0:T(128)S(1)} %pad_add_fusion.me_ref, bf16[512,4096]{1,0:T(8,128)(2,1)S(1)} %get-tuple-element.27.full_ref, ...), custom_call_target="tpu_custom_call" | custom-call | flops 1073741824 | tf_op jit(solution)/shard_map/project/pallas_call | solution.py:22
  108.8 1.3 collective-permute-done.16.come_ref
  110.2 14.1 %all_to_all.22.parts_ref = bf16[32,8,256]{2,1,0:T(8,128)(2,1)S(1)} all-to-all(bf16[32,8,256]{2,1,0:T(8,128)(2,1)S(1)} %bitcast.11), channel_id=1, replica_groups={{0,2,4,6,8,10,12,14,16,18,20,22,24,26,28,30,32,34,36,38,40,42,44,46,48,..., dimensions={0} | all-to-all | bytes 262144 | tf_op jit(solution)/shard_map/all_to_all | solution.py:295
  124.3 13.9 %all_to_all.23 = bf16[32,8,256]{2,1,0:T(8,128)(2,1)S(1)} all-to-all(bf16[32,8,256]{2,1,0:T(8,128)(2,1)S(1)} %total.3), channel_id=1, replica_groups={{0,2,4,6,8,10,12,14,16,18,20,22,24,26,28,30,32,34,36,38,40,42,44,46,48,..., dimensions={0} | all-to-all | bytes 262144 | tf_op jit(solution)/shard_map/all_to_all | solution.py:295
  138.3 2.4 %collective-permute-start.21 = (bf16[512,256]{1,0:T(8,128)(2,1)S(1)}, bf16[512,256]{1,0:T(8,128)(2,1)S(1)}, u32[]{:S(2)}, u32[]{:S(2)}) collective-permute-start(bf16[512,256]{1,0:T(8,128)(2,1)S(1)} %get-tuple-element.41), channel_id=1, source_target_pairs={{0,1},{1,2},{2,3},{3,4},{4,5},{5,6},{6,7},{7,8},{8,9},{9,10},{10,1... | collective-permute-start | bytes 786440 | tf_op jit(solution)/shard_map/ppermute | solution.py:279
  140.7 5.3 %collective-permute-start.22 = (bf16[512,256]{1,0:T(8,128)(2,1)S(1)}, bf16[512,256]{1,0:T(8,128)(2,1)S(1)}, u32[]{:S(2)}, u32[]{:S(2)}) collective-permute-start(bf16[512,256]{1,0:T(8,128)(2,1)S(1)} %get-tuple-element.42), channel_id=1, source_target_pairs={{1,0},{2,1},{3,2},{4,3},{5,4},{6,5},{7,6},{8,7},{9,8},{10,9},{11,1... | collective-permute-start | bytes 786440 | tf_op jit(solution)/shard_map/ppermute | solution.py:279
  146.0 1.1 moments.1.refs_0_
  147.1 0.7 collective-permute-start.20
  147.7 1.7 collective-permute-start.19
  149.4 0.4 collective-permute-start.18
  149.8 3.6 %prior.1.image_ref = bf16[4096,256]{1,0:T(8,128)(2,1)S(1)} custom-call(s32[2,32]{1,0:T(2,128)S(1)} %bitcast.16, bf16[32,3,128,128]{3,2,1,0:T(8,128)(2,1)S(1)} %copy-done, bf16[4096,256]{1,0:T(8,128)(2,1)S(1)} %get-tuple-element.40.sample_ref, bf16[512,256]{1,0:T(8,128)(2,1)S(1)} %collective-permute-done.21.below_ref, ...), custom_call_target="tpu_custom_call" | custom-call | flops 1073741824 | tf_op jit(solution)/shard_map/prior/pallas_call | solution.py:22
  153.4 3.0 %collective-permute-done.20.refs_3_ = bf16[960,128]{1,0:T(8,128)(2,1)S(1)} collective-permute-done((bf16[960,128]{1,0:T(8,128)(2,1)S(1)}, bf16[960,128]{1,0:T(8,128)(2,1)S(1)}, u32[]{:S(2)}, u32[]{:S(2)}) %collective-permute-start.20) | collective-permute-done | bytes 245792 | tf_op jit(solution)/shard_map/ppermute | solution.py:279
  156.5 1.6 collective-permute-done.19.refs_2_
  158.0 1.0 collective-permute-done.18.refs_1_
  159.1 10.2 %factor.1 = (f32[256,256]{1,0:T(8,128)S(1)}, f32[256,256]{1,0:T(8,128)S(1)}) custom-call(bf16[960,128]{1,0:T(8,128)(2,1)S(1)} %moments.1.refs_0_, bf16[960,128]{1,0:T(8,128)(2,1)S(1)} %collective-permute-done.18.refs_1_, bf16[960,128]{1,0:T(8,128)(2,1)S(1)} %collective-permute-done.19.refs_2_, bf16[960,128]{1,0:T(8,128)(2,1)S(1)} %collective-permute-done.20.refs_3_), custom_call_target="tpu_custom_call" | custom-call | flops 17179869184 | tf_op jit(solution)/shard_map/factor/pallas_call | solution.py:22
  169.3 5.6 %final.1 = (bf16[4096,256]{1,0:T(8,128)(2,1)}, bf16[4096,256]{1,0:T(8,128)(2,1)}, f32[256,256]{1,0:T(8,128)}) custom-call(f32[256,256]{1,0:T(8,128)S(1)} %get-tuple-element.38.inv_ref.rows_ref, f32[256,256]{1,0:T(8,128)S(1)} %get-tuple-element.38.inv_ref.rows_ref, f32[256,256]{1,0:T(8,128)S(1)} %get-tuple-element.39.second_ref, ...), custom_call_target="tpu_custom_call" | custom-call | tf_op jit(solution)/shard_map/final/pallas_call | solution.py:419
  (30 shorter events, 0.9 us)
Async XLA Ops:
  0.6 14.5 %copy-start = (bf16[32,3,128,128]{3,2,1,0:T(8,128)(2,1)S(1)}, bf16[32,3,128,128]{3,2,1,0:T(8,128)(2,1)}, u32[]{:S(2)}) copy-start(bf16[32,3,128,128]{3,2,1,0:T(8,128)(2,1)} %coef_ref.3) | copy-start | bytes 9437188
  0.6 2.6 %copy-start.3 = (s32[32,2]{0,1:T(2,128)S(1)}, s32[32,2]{0,1:T(2,128)}, u32[]{:S(2)}) copy-start(s32[32,2]{0,1:T(2,128)} %param.7) | copy-start | bytes 772
  6.1 19.1 %collective-permute-start = (bf16[512,512]{1,0:T(8,128)(2,1)}, bf16[512,512]{1,0:T(8,128)(2,1)}, u32[]{:S(2)}, u32[]{:S(2)}) collective-permute-start(bf16[512,512]{1,0:T(8,128)(2,1)} %get-tuple-element.23), channel_id=1, source_target_pairs={{0,1},{1,2},{2,3},{3,4},{4,5},{5,6},{6,7},{7,8},{8,9},{9,10},{10,1... | collective-permute-start | bytes 1572872 | tf_op jit(solution)/shard_map/ppermute | solution.py:279
  8.2 17.0 %collective-permute-start.1 = (bf16[512,512]{1,0:T(8,128)(2,1)}, bf16[512,512]{1,0:T(8,128)(2,1)}, u32[]{:S(2)}, u32[]{:S(2)}) collective-permute-start(bf16[512,512]{1,0:T(8,128)(2,1)} %get-tuple-element.24), channel_id=1, source_target_pairs={{1,0},{2,1},{3,2},{4,3},{5,4},{6,5},{7,6},{8,7},{9,8},{10,9},{11,1... | collective-permute-start | bytes 1572872 | tf_op jit(solution)/shard_map/ppermute | solution.py:279
  15.1 2.2 %copy-start.2 = (bf16[512,4096]{1,0:T(8,128)(2,1)S(1)}, bf16[512,4096]{1,0:T(8,128)(2,1)}, u32[]{:S(2)}) copy-start(bf16[512,4096]{1,0:T(8,128)(2,1)} %jac_ref.1) | copy-start | bytes 12582916
  17.3 7.9 %copy-start.1 = (bf16[4096,256]{1,0:T(8,128)(2,1)S(1)}, bf16[4096,256]{1,0:T(8,128)(2,1)}, u32[]{:S(2)}) copy-start(bf16[4096,256]{1,0:T(8,128)(2,1)} %probe_ref.1) | copy-start | bytes 6291460
  28.3 1.4 collective-permute-start.2
  61.2 1.3 collective-permute-start.3
  64.5 9.7 %collective-permute-start.4 = (bf16[512,256]{1,0:T(8,128)(2,1)S(1)}, bf16[512,256]{1,0:T(8,128)(2,1)S(1)}, u32[]{:S(2)}, u32[]{:S(2)}) collective-permute-start(bf16[512,256]{1,0:T(8,128)(2,1)S(1)} %get-tuple-element.30), channel_id=1, source_target_pairs={{0,64},{64,128},{128,192},{192,0},{1,65},{65,129},{129,193},{193,1... | collective-permute-start | bytes 786440 | tf_op jit(solution)/shard_map/ppermute | solution.py:279
  66.1 10.1 %collective-permute-start.8 = (bf16[512,256]{1,0:T(8,128)(2,1)S(1)}, bf16[512,256]{1,0:T(8,128)(2,1)S(1)}, u32[]{:S(2)}, u32[]{:S(2)}) collective-permute-start(bf16[512,256]{1,0:T(8,128)(2,1)S(1)} %get-tuple-element.35), channel_id=1, source_target_pairs={{0,192},{64,0},{128,64},{192,128},{1,193},{65,1},{129,65},{193,129... | collective-permute-start | bytes 786440 | tf_op jit(solution)/shard_map/ppermute | solution.py:279
  67.8 13.1 %collective-permute-start.6 = (bf16[512,256]{1,0:T(8,128)(2,1)S(1)}, bf16[512,256]{1,0:T(8,128)(2,1)S(1)}, u32[]{:S(2)}, u32[]{:S(2)}) collective-permute-start(bf16[512,256]{1,0:T(8,128)(2,1)S(1)} %get-tuple-element.31), channel_id=1, source_target_pairs={{0,192},{64,0},{128,64},{192,128},{1,193},{65,1},{129,65},{193,129... | collective-permute-start | bytes 786440 | tf_op jit(solution)/shard_map/ppermute | solution.py:279
  74.3 10.5 %collective-permute-start.5 = (bf16[512,256]{1,0:T(8,128)(2,1)S(1)}, bf16[512,256]{1,0:T(8,128)(2,1)S(1)}, u32[]{:S(2)}, u32[]{:S(2)}) collective-permute-start(bf16[512,256]{1,0:T(8,128)(2,1)S(1)} %add_convert_fusion.3), channel_id=1, source_target_pairs={{0,64},{64,128},{128,192},{192,0},{1,65},{65,129},{129,193},{193,1... | collective-permute-start | bytes 786440 | tf_op jit(solution)/shard_map/ppermute | solution.py:279
  74.7 15.7 %collective-permute-start.7 = (bf16[512,256]{1,0:T(8,128)(2,1)S(1)}, bf16[512,256]{1,0:T(8,128)(2,1)S(1)}, u32[]{:S(2)}, u32[]{:S(2)}) collective-permute-start(bf16[512,256]{1,0:T(8,128)(2,1)S(1)} %get-tuple-element.33), channel_id=1, source_target_pairs={{0,64},{64,128},{128,192},{192,0},{1,65},{65,129},{129,193},{193,1... | collective-permute-start | bytes 786440 | tf_op jit(solution)/shard_map/ppermute | solution.py:279
  76.3 14.1 %collective-permute-start.9 = (bf16[512,256]{1,0:T(8,128)(2,1)S(1)}, bf16[512,256]{1,0:T(8,128)(2,1)S(1)}, u32[]{:S(2)}, u32[]{:S(2)}) collective-permute-start(bf16[512,256]{1,0:T(8,128)(2,1)S(1)} %add_convert_fusion.1), channel_id=1, source_target_pairs={{0,192},{64,0},{128,64},{192,128},{1,193},{65,1},{129,65},{193,129... | collective-permute-start | bytes 786440 | tf_op jit(solution)/shard_map/ppermute | solution.py:279
  84.8 11.1 %collective-permute-start.12 = (bf16[512,256]{1,0:T(8,128)(2,1)S(1)}, bf16[512,256]{1,0:T(8,128)(2,1)S(1)}, u32[]{:S(2)}, u32[]{:S(2)}) collective-permute-start(bf16[512,256]{1,0:T(8,128)(2,1)S(1)} %add_convert_fusion.2.refs_0_), channel_id=1, source_target_pairs={{0,64},{64,128},{128,192},{192,0},{1,65},{65,129},{129,193},{193,1... | collective-permute-start | bytes 786440 | tf_op jit(solution)/shard_map/ppermute | solution.py:279
  90.5 9.3 %collective-permute-start.11 = (bf16[512,256]{1,0:T(8,128)(2,1)S(1)}, bf16[512,256]{1,0:T(8,128)(2,1)S(1)}, u32[]{:S(2)}, u32[]{:S(2)}) collective-permute-start(bf16[512,256]{1,0:T(8,128)(2,1)S(1)} %add_convert_fusion.refs_1_), channel_id=1, source_target_pairs={{0,192},{64,0},{128,64},{192,128},{1,193},{65,1},{129,65},{193,129... | collective-permute-start | bytes 786440 | tf_op jit(solution)/shard_map/ppermute | solution.py:279
  91.1 13.0 %collective-permute-start.10 = (bf16[512,256]{1,0:T(8,128)(2,1)S(1)}, bf16[512,256]{1,0:T(8,128)(2,1)S(1)}, u32[]{:S(2)}, u32[]{:S(2)}) collective-permute-start(bf16[512,256]{1,0:T(8,128)(2,1)S(1)} %add_convert_fusion.2.refs_0_), channel_id=1, source_target_pairs={{0,192},{64,0},{128,64},{192,128},{1,193},{65,1},{129,65},{193,129... | collective-permute-start | bytes 786440 | tf_op jit(solution)/shard_map/ppermute | solution.py:279
  91.8 12.2 %collective-permute-start.15 = (bf16[512,256]{1,0:T(8,128)(2,1)S(1)}, bf16[512,256]{1,0:T(8,128)(2,1)S(1)}, u32[]{:S(2)}, u32[]{:S(2)}) collective-permute-start(bf16[512,256]{1,0:T(8,128)(2,1)S(1)} %add_convert_fusion.refs_1_), channel_id=1, source_target_pairs={{0,64},{64,128},{128,192},{192,0},{1,65},{65,129},{129,193},{193,1... | collective-permute-start | bytes 786440 | tf_op jit(solution)/shard_map/ppermute | solution.py:279
  96.0 9.6 %collective-permute-start.13 = (bf16[512,256]{1,0:T(8,128)(2,1)S(1)}, bf16[512,256]{1,0:T(8,128)(2,1)S(1)}, u32[]{:S(2)}, u32[]{:S(2)}) collective-permute-start(bf16[512,256]{1,0:T(8,128)(2,1)S(1)} %collective-permute-done.12.refs_6_), channel_id=1, source_target_pairs={{0,64},{64,128},{128,192},{192,0},{1,65},{65,129},{129,193},{193,1... | collective-permute-start | bytes 786440 | tf_op jit(solution)/shard_map/ppermute | solution.py:279
  99.7 7.1 %collective-permute-start.14 = (bf16[512,256]{1,0:T(8,128)(2,1)S(1)}, bf16[512,256]{1,0:T(8,128)(2,1)S(1)}, u32[]{:S(2)}, u32[]{:S(2)}) collective-permute-start(bf16[512,256]{1,0:T(8,128)(2,1)S(1)} %collective-permute-done.11.refs_3_), channel_id=1, source_target_pairs={{0,192},{64,0},{128,64},{192,128},{1,193},{65,1},{129,65},{193,129... | collective-permute-start | bytes 786440 | tf_op jit(solution)/shard_map/ppermute | solution.py:279
  108.7 1.4 collective-permute-start.16
  138.3 7.7 %collective-permute-start.17 = (bf16[256,256]{1,0:T(8,128)(2,1)S(1)}, bf16[256,256]{1,0:T(8,128)(2,1)S(1)}, u32[]{:S(2)}, u32[]{:S(2)}) collective-permute-start(bf16[256,256]{1,0:T(8,128)(2,1)S(1)} %bitcast.12), channel_id=1, source_target_pairs={{0,1},{1,0},{2,3},{3,2},{4,5},{5,4},{6,7},{7,6},{8,9},{9,8},{10,11... | collective-permute-start | bytes 393224 | tf_op jit(solution)/shard_map/ppermute | solution.py:287
  138.3 11.5 %collective-permute-start.21 = (bf16[512,256]{1,0:T(8,128)(2,1)S(1)}, bf16[512,256]{1,0:T(8,128)(2,1)S(1)}, u32[]{:S(2)}, u32[]{:S(2)}) collective-permute-start(bf16[512,256]{1,0:T(8,128)(2,1)S(1)} %get-tuple-element.41), channel_id=1, source_target_pairs={{0,1},{1,2},{2,3},{3,4},{4,5},{5,6},{6,7},{7,8},{8,9},{9,10},{10,1... | collective-permute-start | bytes 786440 | tf_op jit(solution)/shard_map/ppermute | solution.py:279
  140.7 9.1 %collective-permute-start.22 = (bf16[512,256]{1,0:T(8,128)(2,1)S(1)}, bf16[512,256]{1,0:T(8,128)(2,1)S(1)}, u32[]{:S(2)}, u32[]{:S(2)}) collective-permute-start(bf16[512,256]{1,0:T(8,128)(2,1)S(1)} %get-tuple-element.42), channel_id=1, source_target_pairs={{1,0},{2,1},{3,2},{4,3},{5,4},{6,5},{7,6},{8,7},{9,8},{10,9},{11,1... | collective-permute-start | bytes 786440 | tf_op jit(solution)/shard_map/ppermute | solution.py:279
  147.1 9.4 %collective-permute-start.20 = (bf16[960,128]{1,0:T(8,128)(2,1)S(1)}, bf16[960,128]{1,0:T(8,128)(2,1)S(1)}, u32[]{:S(2)}, u32[]{:S(2)}) collective-permute-start(bf16[960,128]{1,0:T(8,128)(2,1)S(1)} %moments.1.refs_0_), channel_id=1, source_target_pairs={{0,128},{64,192},{128,0},{192,64},{1,129},{65,193},{129,1},{193,65... | collective-permute-start | bytes 737288 | tf_op jit(solution)/shard_map/ppermute | solution.py:279
  147.7 10.3 %collective-permute-start.19 = (bf16[960,128]{1,0:T(8,128)(2,1)S(1)}, bf16[960,128]{1,0:T(8,128)(2,1)S(1)}, u32[]{:S(2)}, u32[]{:S(2)}) collective-permute-start(bf16[960,128]{1,0:T(8,128)(2,1)S(1)} %moments.1.refs_0_), channel_id=1, source_target_pairs={{0,192},{64,0},{128,64},{192,128},{1,193},{65,1},{129,65},{193,129... | collective-permute-start | bytes 737288 | tf_op jit(solution)/shard_map/ppermute | solution.py:279
  149.4 9.7 %collective-permute-start.18 = (bf16[960,128]{1,0:T(8,128)(2,1)S(1)}, bf16[960,128]{1,0:T(8,128)(2,1)S(1)}, u32[]{:S(2)}, u32[]{:S(2)}) collective-permute-start(bf16[960,128]{1,0:T(8,128)(2,1)S(1)} %moments.1.refs_0_), channel_id=1, source_target_pairs={{0,64},{64,128},{128,192},{192,0},{1,65},{65,129},{129,193},{193,1... | collective-permute-start | bytes 737288 | tf_op jit(solution)/shard_map/ppermute | solution.py:279

commit v2 on v1

v2 whole, which is shorter than its diff:
```python
import functools

import jax
import jax.numpy as jnp
from jax import lax
from jax.experimental import pallas as pl
from jax.experimental.pallas import tpu as pltpu
from jax.sharding import PartitionSpec as P


BLK = 128
REACH = 4
EDGE = REACH * BLK
NB = 64
F32 = jnp.float32
BF16 = jnp.bfloat16
HI = lax.Precision.HIGHEST
VMEM = pl.BlockSpec(memory_space=pltpu.VMEM)
SMEM = pl.BlockSpec(memory_space=pltpu.SMEM)


def core_index():
    return lax.rem(lax.axis_index("par"), 2)


def call(kernel, outs, specs, args, scratch=(), mib=24, flops=0):
    return pl.pallas_call(
        kernel,
        out_shape=outs,
        in_specs=specs,
        out_specs=jax.tree.map(lambda _: VMEM, outs),
        scratch_shapes=scratch,
        compiler_params=pltpu.CompilerParams(vmem_limit_bytes=mib * 2**20),
        cost_estimate=pl.CostEstimate(flops=flops, bytes_accessed=0, transcendentals=0),
    )(*args)


def dot(a, b):
    return jnp.dot(a, b, preferred_element_type=F32)


def dot_tn(a, b, precision=None):
    return lax.dot_general(a, b, (((0,), (0,)), ((), ())), precision=precision, preferred_element_type=F32)


def dot_nt(a, b, precision=None):
    return lax.dot_general(a, b, (((1,), (1,)), ((), ())), precision=precision, preferred_element_type=F32)


def shape(*dims, dtype=BF16):
    return jax.ShapeDtypeStruct(dims, dtype)


def edges_kernel(off_ref, jac_ref, coef_ref, partner_ref, neighbor_ref, acc):
    count = coef_ref.shape[0]
    acc[...] = jnp.zeros_like(acc)
    for side in range(2):
        for i in range(REACH):
            block = i + side * (count - REACH)
            columns = jac_ref[:, block * BLK : (block + 1) * BLK]
            for j in range(2):
                target = block + off_ref[j, block]
                place = target + REACH if side == 0 else target - count + REACH
                outside = target < 0 if side == 0 else target >= count

                @pl.when(outside)
                def _():
                    acc[place] += dot(columns, coef_ref[block, j + 1])

    core = core_index()
    for i in range(REACH):
        partner_ref[:, i * BLK : (i + 1) * BLK] = acc[(1 - core) * REACH + i].astype(BF16)
        neighbor_ref[:, i * BLK : (i + 1) * BLK] = acc[core * REACH + i].astype(BF16)


def own_kernel(off_ref, jac_ref, coef_ref, out_ref, acc):
    count = coef_ref.shape[0]
    for i in range(REACH):
        acc[i] = jnp.zeros_like(acc[i])
        acc[count + REACH + i] = jnp.zeros_like(acc[i])

    def diagonal(block, carry):
        columns = jac_ref[:, pl.ds(pl.multiple_of(block * BLK, BLK), BLK)]
        acc[block + REACH] = dot(columns, coef_ref[block, 0])
        return carry

    lax.fori_loop(0, count, diagonal, 0, unroll=4)

    def band(block, carry):
        columns = jac_ref[:, pl.ds(pl.multiple_of(block * BLK, BLK), BLK)]
        for j in range(2):
            acc[block + REACH + off_ref[j, block]] += dot(columns, coef_ref[block, j + 1])
        return carry

    lax.fori_loop(0, count, band, 0, unroll=4)
    for block in range(count):
        out_ref[:, block * BLK : (block + 1) * BLK] = acc[block + REACH].astype(BF16)


def halves(rows):
    core = core_index()
    return [pl.ds(pl.multiple_of(i * rows, rows), rows) for i in (core, 1 - core)]


def forward_kernel(own_ref, partner_ref, neighbor_ref, probe_ref, full_ref, keep_ref, give_ref, acc):
    width = own_ref.shape[1]
    core = core_index()
    full_ref[...] = own_ref[...]
    for come, side in ((partner_ref, 1 - core), (neighbor_ref, core)):
        here = pl.ds(pl.multiple_of(side * (width - EDGE), EDGE), EDGE)
        full_ref[:, here] = (own_ref[:, here].astype(F32) + come[...].astype(F32)).astype(BF16)
    acc[...] = dot(full_ref[...], probe_ref[...])
    mine, other = halves(keep_ref.shape[0])
    keep_ref[...] = acc[mine, :].astype(BF16)
    give_ref[...] = acc[other, :].astype(BF16)


def pair_kernel(keep_ref, come_ref, out_ref):
    out_ref[...] = (keep_ref[...].astype(F32) + come_ref[...].astype(F32)).astype(BF16)


def total_kernel(parts_ref, out_ref):
    total = parts_ref[0].astype(F32)
    for i in range(1, parts_ref.shape[0]):
        total += parts_ref[i].astype(F32)
    total = total.astype(BF16)
    for i in range(out_ref.shape[0]):
        out_ref[i] = total


def split(value):
    high = value.astype(BF16)
    return high, (value - high.astype(F32)).astype(BF16)


def joined(both):
    return both[:, :BLK].astype(F32) + both[:, BLK:].astype(F32)


def pair_gram_kernel(keep_ref, come_ref, out_ref):
    half = keep_ref.shape[0] // 2
    for i in range(out_ref.shape[0]):
        rows = slice(8 * i, 8 * i + 8)
        out_ref[i, :8] = (keep_ref[rows].astype(F32) + come_ref[rows].astype(F32)).astype(BF16)
        rows = slice(half + 8 * i, half + 8 * i + 8)
        out_ref[i, 8:, :BLK], out_ref[i, 8:, BLK:] = split(joined(keep_ref[rows]) + joined(come_ref[rows]))


def total_gram_kernel(parts_ref, out_ref):
    total = parts_ref[0].astype(F32)
    for i in range(1, parts_ref.shape[0]):
        total += parts_ref[i].astype(F32)
    rows = total[:8].astype(BF16)
    high, low = split(total[8:, :BLK] + total[8:, BLK:])
    for i in range(out_ref.shape[0]):
        out_ref[i, :8] = rows
        out_ref[i, 8:, :BLK] = high
        out_ref[i, 8:, BLK:] = low


def in_order(mine_ref, other_ref, out):
    for part, rows in zip((mine_ref, other_ref), halves(mine_ref.shape[0])):
        out[rows, :] = part[...]


def sample_kernel(ranks, full_ref, mine_ref, other_ref, *refs):
    outs, fwd = refs[:-1], refs[-1]
    rows = full_ref.shape[1] // ranks // 2
    in_order(mine_ref, other_ref, fwd)
    for rel in range(ranks):
        owner = lax.rem(lax.axis_index("obs") + rel, ranks)
        for half in range(2):
            start = pl.multiple_of(owner * (2 * rows) + half * rows, rows)
            outs[2 * rel + half][...] = dot_tn(full_ref[:, pl.ds(start, rows)], fwd[...]).astype(BF16)


def project_kernel(ranks, full_ref, *refs):
    pieces = refs[: 2 * ranks]
    sample_ref, neighbor_ref, keep_ref, give_ref, acc, gram = refs[2 * ranks :]
    rows = pieces[0].shape[0]
    total = jnp.zeros(acc.shape, F32)
    square = jnp.zeros(gram.shape, F32)
    for rel in range(ranks):
        owner = lax.rem(lax.axis_index("obs") + rel, ranks)
        for half in range(2):
            piece = pieces[2 * rel + half][...]
            start = pl.multiple_of(owner * (2 * rows) + half * rows, rows)
            sample_ref[pl.ds(start, rows), :] = piece
            total += dot(full_ref[:, pl.ds(start, rows)], piece)
            square += dot_tn(piece, piece)
    acc[...] = total
    gram[...] = square
    rows = acc.shape[0] // 2
    for out_ref, mine in zip((keep_ref, give_ref), halves(rows)):
        out_ref[:rows] = acc[mine, :].astype(BF16)
    for out_ref, mine in zip((keep_ref, give_ref), halves(BLK)):
        out_ref[rows : 2 * rows, :BLK], out_ref[rows : 2 * rows, BLK:] = split(gram[:, mine])
    core = core_index()
    last = sample_ref.shape[0] - EDGE
    neighbor_ref[...] = sample_ref[pl.ds(pl.multiple_of(core * last, EDGE), EDGE), :]
    give_ref[2 * rows :] = sample_ref[pl.ds(pl.multiple_of((1 - core) * last, EDGE), EDGE), :]


def prior_kernel(off_ref, coef_ref, sample_ref, come_ref, neighbor_ref, out_ref, ext):
    count, rows = coef_ref.shape[0], sample_ref.shape[0]
    core = core_index()
    far = EDGE + rows
    ext[EDGE : EDGE + rows] = sample_ref[...]
    ext[pl.ds(pl.multiple_of((1 - core) * far, EDGE), EDGE)] = come_ref[come_ref.shape[0] - EDGE :]
    ext[pl.ds(pl.multiple_of(core * far, EDGE), EDGE)] = neighbor_ref[...]

    def apply(block, carry):
        starts = [(block + REACH) * BLK] + [(block + REACH + off_ref[j, block]) * BLK for j in range(2)]
        result = sum(dot(coef_ref[block, j], ext[pl.ds(pl.multiple_of(starts[j], BLK), BLK), :]) for j in range(3))
        out_ref[pl.ds(pl.multiple_of(block * BLK, BLK), BLK), :] = result.astype(BF16)
        return carry

    lax.fori_loop(0, count, apply, 0, unroll=4)


def packed(full):
    return jnp.concatenate(
        [
            full[:NB, : 2 * NB],
            full[:NB, 2 * NB :],
            full[NB : 2 * NB, NB : 3 * NB],
            full[2 * NB : 3 * NB, 2 * NB :],
            jnp.concatenate([full[NB : 2 * NB, 3 * NB :], full[3 * NB :, 3 * NB :]], axis=1),
        ],
        axis=0,
    )


def unpacked(pack):
    r = [pack[i * NB : (i + 1) * NB] for i in range(5)]
    zero = jnp.zeros((NB, NB), F32)
    lane = lax.broadcasted_iota(jnp.int32, (NB, 2 * NB), 1)
    head = lambda block: jnp.where(lane < NB, 0.5, 1.0) * block
    join = lambda *p: jnp.concatenate(p, axis=1)
    return jnp.concatenate(
        [
            join(head(r[0]), r[1]),
            join(zero, head(r[2]), r[4][:, :NB]),
            join(zero, zero, head(r[3])),
            join(zero, zero, zero, 0.5 * r[4][:, NB:]),
        ],
        axis=0,
    )


def moments_kernel(mine_ref, other_ref, gram_ref, second_ref, proj):
    count = mine_ref.shape[0]
    for part, core in ((mine_ref, core_index()), (other_ref, 1 - core_index())):
        columns = pl.ds(pl.multiple_of(core * BLK, BLK), BLK)
        for i in range(count):
            proj[pl.ds(pl.multiple_of(core * (8 * count) + 8 * i, 8), 8), :] = part[i, :8].astype(F32)
            gram_ref[8 * i : 8 * i + 8, columns] = joined(part[i, 8:])
    rounded = proj[...].astype(BF16)
    second_ref[...] = packed(dot_tn(rounded, rounded)).astype(BF16)


def row_of(tile, k):
    return jnp.broadcast_to(tile[k : k + 1, :], tile.shape)


def lane_of(tile, k):
    return jnp.broadcast_to(tile[:, k : k + 1], (8, 2 * NB))


def factor_inverse(block):
    index = [lax.broadcasted_iota(jnp.int32, (NB, NB), d) for d in (0, 1)]
    wide = jnp.concatenate([block, (index[0] == index[1]).astype(F32)], axis=1)
    groups = NB // 8
    tiles = [wide[8 * t : 8 * t + 8] for t in range(groups)]
    row = lax.broadcasted_iota(jnp.int32, (8, 2 * NB), 0)
    out = []
    for g in range(groups):
        cols = {t: [lane_of(tiles[t], 8 * g + k) for k in range(8)] for t in range(g, groups)}
        done = tiles[g]
        for k in range(0, 8, 2):
            here = cols[g]
            p, q, r = row_of(here[k], k), row_of(here[k + 1], k), row_of(here[k + 1], k + 1)
            root = lax.rsqrt(p * r - q * q)
            inverse = root * root
            p_root = lax.rsqrt(p)
            row0, row1 = row_of(tiles[g], k), row_of(tiles[g], k + 1)
            second = (p * p_root * root) * (row1 - (q * p_root * p_root) * row0)
            done = jnp.where(row == k, p_root * row0, jnp.where(row == k + 1, second, done))
            head0 = [row_of(here[j], k) for j in range(k + 2, 8)]
            head1 = [row_of(here[j], k + 1) for j in range(k + 2, 8)]
            for t in range(g, groups):
                c0, c1 = cols[t][k], cols[t][k + 1]
                w0 = r * c0 - q * c1
                w1 = p * c1 - q * c0
                for j in range(k + 2, 8):
                    cols[t][j] = cols[t][j] - inverse * (w0 * head0[j - k - 2] + w1 * head1[j - k - 2])
                change = inverse * (w0 * row0 + w1 * row1)
                if t == g:
                    change = jnp.where(row > k + 1, change, 0.0)
                tiles[t] = tiles[t] - change
        out.append(done)
    return jnp.concatenate(out, axis=0)[:, NB:]


def exact(a, b, nt=False):
    return dot_nt(a, b, HI) if nt else jnp.dot(a, b, precision=HI, preferred_element_type=F32)


def factor_kernel(scale, gram_ref, out_ref, a_ref, m_ref, inv_ref):
    n = out_ref.shape[0]
    gram = gram_ref[...] * scale
    index = [lax.broadcasted_iota(jnp.int32, (n, n), d) for d in (0, 1)]
    diagonal = jnp.where(index[0] == index[1], gram, 0.0)
    across = lax.rsqrt(jnp.sum(diagonal, axis=0, keepdims=True))
    a_ref[...] = gram * across * lax.rsqrt(jnp.sum(diagonal, axis=1, keepdims=True))
    m_ref[...] = jnp.zeros((n, n), F32)
    inv_ref[...] = jnp.zeros((n, n), F32)
    for lo in range(0, n, NB):
        hi, nx = lo + NB, lo + 2 * NB
        inverse = factor_inverse(a_ref[lo:hi, lo:hi])
        inv_ref[lo:hi, lo:hi] = inverse
        if hi < n:
            upper = exact(inverse, a_ref[lo:hi, hi:])
            lower = exact(a_ref[hi:, lo:hi], inverse, nt=True)
            a_ref[hi:nx, hi:nx] -= exact(lower[:NB], upper[:, :NB])
            if nx < n:
                a_ref[hi:nx, nx:] -= exact(lower[:NB], upper[:, NB:])
                a_ref[nx:, hi:] -= exact(lower[NB:], upper)
        if lo:
            inv_ref[lo:hi, :lo] = exact(inverse, m_ref[lo:hi, :lo])
        if hi < n:
            m_ref[hi:, :hi] -= exact(lower, inv_ref[lo:hi, :hi])
    out_ref[...] = (inv_ref[...] * across).astype(BF16)


def final_kernel(scale, inv_ref, rows_ref, sample_ref, image_ref, *refs):
    seconds, (basis_ref, mapped_ref, ritz_ref) = refs[:-3], refs[-3:]
    inverse = inv_ref[...]
    basis_ref[...] = dot_nt(sample_ref[...], inverse).astype(BF16)
    mapped_ref[...] = dot_nt(image_ref[...], inverse).astype(BF16)
    total = seconds[0][...].astype(F32)
    for part in seconds[1:]:
        total += part[...].astype(F32)
    upper = unpacked(total).astype(BF16)
    left = dot(rows_ref[...], upper) + dot_nt(rows_ref[...], upper)
    ritz_ref[...] = dot_nt(left.astype(BF16), inverse) * scale


def shifted(value, axis, by):
    count = lax.axis_size(axis)
    return lax.ppermute(value, axis, [(i, (i + by) % count) for i in range(count)])


def to_neighbor(value):
    count = lax.axis_size("par")
    pairs = [pair for i in range(1, count - 1, 2) for pair in ((i, i + 1), (i + 1, i))]
    return lax.ppermute(value, "par", pairs)


def added(*values):
    return sum(v.astype(F32) for v in values).astype(BF16)


def swapped(value):
    return lax.ppermute(value, "par", [(i, i ^ 1) for i in range(lax.axis_size("par"))])


def exchanged(parts):
    groups = [[2 * i + core for i in range(parts.shape[0])] for core in range(2)]
    return lax.all_to_all(parts, "par", 0, 0, axis_index_groups=groups, tiled=True)


def body(jacobian, probes, coeffs, offsets):
    ranks = lax.axis_size("obs")
    chips = lax.axis_size("par") // 2
    nobs, npar = jacobian.shape[0], jacobian.shape[1]
    width = probes.shape[1]
    count = coeffs.shape[0]
    offsets = offsets.T
    flops = 2 * nobs * npar * width

    partner, neighbor = call(
        edges_kernel,
        [shape(nobs, EDGE)] * 2,
        [SMEM, VMEM, VMEM],
        [offsets, jacobian, coeffs],
        [pltpu.VMEM((2 * REACH, nobs, BLK), F32)],
        flops=flops // 4,
    )
    from_neighbor = to_neighbor(neighbor)
    from_partner = swapped(partner)
    own = call(
        own_kernel,
        shape(nobs, npar),
        [SMEM, VMEM, VMEM],
        [offsets, jacobian, coeffs],
        [pltpu.VMEM((count + 2 * REACH, nobs, BLK), F32)],
        flops=4 * flops,
    )
    half = shape(nobs // 2, width)
    full, keep, give = call(
        forward_kernel,
        [shape(nobs, npar), half, half],
        [VMEM] * 4,
        [own, from_partner, from_neighbor, probes],
        [pltpu.VMEM((nobs, width), F32)],
        mib=16,
        flops=flops,
    )
    part = call(pair_kernel, half, [VMEM] * 2, [keep, swapped(give)], mib=4)
    parts = exchanged(part.reshape(chips, nobs // 2 // chips, width))
    total = call(total_kernel, shape(*parts.shape), [VMEM], [parts], mib=4)
    mine = exchanged(total).reshape(half.shape)
    other = swapped(mine)

    pieces = call(
        functools.partial(sample_kernel, ranks),
        [shape(npar // ranks // 2, width)] * (2 * ranks),
        [VMEM] * 3,
        [full, mine, other],
        [pltpu.VMEM((nobs, width), BF16)],
        mib=16,
        flops=flops,
    )
    here0, here1, right0, right1, far0, far1, left0, left1 = pieces

    def ring(value, by):
        return shifted(value, "obs", by)

    via_left = ring(far0, 1)
    via_right = ring(far1, -1)
    a1 = ring(right1, 1)
    b0 = ring(left0, -1)
    a0 = ring(added(right0, via_left), 1)
    b1 = ring(added(left1, via_right), -1)
    sum0 = added(here0, a0, b0)
    sum1 = added(here1, a1, b1)

    l0 = ring(sum0, 1)
    r1 = ring(sum1, -1)
    l1 = ring(sum1, 1)
    r0 = ring(sum0, -1)
    f0 = ring(l0, 1)
    f1 = ring(r1, -1)

    sample, neighbor, keep, give = call(
        functools.partial(project_kernel, ranks),
        [shape(npar, width), shape(EDGE, width), shape(nobs, width), shape(nobs + EDGE, width)],
        [VMEM] * (1 + 2 * ranks),
        [full, sum0, sum1, r0, r1, f0, f1, l0, l1],
        [pltpu.VMEM((nobs, width), F32), pltpu.VMEM((width, width), F32)],
        mib=16,
        flops=flops,
    )
    come = swapped(give)
    from_neighbor = to_neighbor(neighbor)
    both = shape(chips, 16, width)
    part = call(pair_gram_kernel, both, [VMEM] * 2, [keep, come], mib=4)
    total = call(total_gram_kernel, both, [VMEM], [exchanged(part)], mib=4)
    mine = exchanged(total)
    other = swapped(mine)
    gram, second = call(
        moments_kernel,
        [shape(width, width, dtype=F32), shape(5 * NB, 2 * NB)],
        [VMEM] * 2,
        [mine, other],
        [pltpu.VMEM((nobs, width), F32)],
        mib=8,
        flops=flops // 8,
    )
    seconds = [second] + [shifted(second, "obs", by) for by in (1, -1, 2)]
    image = call(
        prior_kernel,
        shape(npar, width),
        [SMEM] + [VMEM] * 4,
        [offsets, coeffs, sample, come, from_neighbor],
        [pltpu.VMEM((npar + 2 * EDGE, width), BF16)],
        mib=8,
        flops=flops,
    )
    total_par = npar * lax.axis_size("par")
    inverse = call(
        functools.partial(factor_kernel, 1.0 / total_par),
        shape(width, width),
        [VMEM],
        [gram],
        [pltpu.VMEM((width, width), F32)] * 3,
        mib=8,
        flops=16 * flops,
    )
    steps = 4
    whole = lambda *dims: pl.BlockSpec(dims, lambda i: (0, 0))
    by_rows = pl.BlockSpec((npar // steps, width), lambda i: (i, 0))
    few = pl.BlockSpec((width // steps, width), lambda i: (i, 0))
    return pl.pallas_call(
        functools.partial(final_kernel, 1.0 / (nobs * ranks)),
        name="final",
        grid=(steps,),
        out_shape=[shape(npar, width), shape(npar, width), shape(width, width, dtype=F32)],
        in_specs=[whole(width, width), few, by_rows, by_rows] + [whole(*second.shape)] * len(seconds),
        out_specs=[by_rows, by_rows, few],
        compiler_params=pltpu.CompilerParams(vmem_limit_bytes=12 * 2**20),
    )(inverse, inverse, sample, image, *seconds)


def solution(mesh):
    return jax.shard_map(
        body,
        mesh=mesh,
        in_specs=(P("obs", "par"), P("par", None), P("par", None, None, None), P("par", None)),
        out_specs=(P("par", None), P("par", None), P()),
        check_vma=False,
    )
```

time: 178 us -> 167 us (0.938)
  blocking collectives: 59.4 us -> 46.7 us
  Pallas kernels: 38.3 us -> 32.2 us
  local copies, waits for them, and re-layouts: 4.8 us -> 10.2 us
  waiting for transfers between devices: 39.1 us -> 42.2 us
    all_to_all x4 -> x3, blocking collectives: 59.4 us -> 46.7 us  [exchanged(): lax.all_to_all(parts, 'par', 0, 0, axis_index_groups=groups, tiled=True)]
    unnamed x8 -> x26, local copies, waits for them, and re-layouts: 2.2 us -> 10.2 us
    all_to_all x0 -> x1, waiting for transfers between devices: none -> 7.47 us  [exchanged(): lax.all_to_all(parts, 'par', 0, 0, axis_index_groups=groups, tiled=True)]
    all_to_all x0 -> x1, starting transfers between devices: none -> 6.32 us  [exchanged(): lax.all_to_all(parts, 'par', 0, 0, axis_index_groups=groups, tiled=True)]
    ppermute x19 -> x17, starting transfers between devices: 31.9 us -> 26.3 us  [the longest x15 15.2 us: shifted(): lax.ppermute(value, axis, [(i, (i + by) % count) for i in range(count)])]
    ppermute x19 -> x17, waiting for transfers between devices: 35.1 us -> 30.1 us  [the longest x15 29.5 us: shifted(): lax.ppermute(value, axis, [(i, (i + by) % count) for i in range(count)])]
    pallas_call x12, Pallas kernels: 32.7 us -> 28.6 us  [call(): pl.pallas_call(kernel, out_shape=outs, in_specs=specs, out_specs=jax.tree...]
    slice x2 -> x0, local copies, waits for them, and re-layouts: 2.6 us -> none  [the longest x1 1.32 us: body(): coeffs[count - REACH:]]
  transfers between devices with their start and end apart: 23 -> 23, of which waited for: 16 -> 14; matrix products, arithmetic and copies ran while one was open for 0% -> 0% of each run, Pallas kernels for 7% -> 13%
where the time goes in v2:
time: 167 us; the launch traced here: 165 us
  blocking collectives  46.7 us (28%)
  waiting for transfers between devices  42.2 us (25%)
  starting transfers between devices  32.8 us (20%)
  Pallas kernels  32.2 us (19%)
  local copies, waits for them, and re-layouts  10.2 us (6%)
    all_to_all x3, blocking collectives, exchanged(): lax.all_to_all(parts, 'par', 0, 0, axis_index_groups=groups, tiled=True)  46.7 us
    ppermute x15, waiting for transfers between devices, shifted(): lax.ppermute(value, axis, [(i, (i + by) % count) for i in range(count)])  29.5 us
    pallas_call x12, Pallas kernels, call(): pl.pallas_call(kernel, out_shape=outs, in_specs=specs, out_specs=jax.tree...  28.6 us
    ppermute x15, starting transfers between devices, shifted(): lax.ppermute(value, axis, [(i, (i + by) % count) for i in range(count)])  15.2 us
    ppermute x2, starting transfers between devices, to_neighbor(): return lax.ppermute(value, 'par', pairs)  11 us
    unnamed x26, local copies, waits for them, and re-layouts  10.2 us
    all_to_all x1, waiting for transfers between devices, exchanged(): lax.all_to_all(parts, 'par', 0, 0, axis_index_groups=groups, tiled=True)  7.47 us
    all_to_all x1, starting transfers between devices, exchanged(): lax.all_to_all(parts, 'par', 0, 0, axis_index_groups=groups, tiled=True)  6.32 us
  transfers between devices with their start and end apart: 23, of which 14 were waited for; matrix products, arithmetic and copies ran while one was open for 0% of the time, Pallas kernels for 13%

profile of v2, /device:TPU:6, one launch (start us, length us, event | category | flops | bytes accessed | tf_op | source)
XLA Modules:
  0.0 165.3 jit_solution(12502701251788804184)
XLA Ops:
  0.6 1.9 %copy-done = bf16[32,3,128,128]{3,2,1,0:T(8,128)(2,1)S(1)} copy-done((bf16[32,3,128,128]{3,2,1,0:T(8,128)(2,1)S(1)}, bf16[32,3,128,128]{3,2,1,0:T(8,128)(2,1)}, u32[]{:S(2)}) %copy-start) | copy-done | bytes 3145752
  2.5 2.2 %copy-done.5 = bf16[512,4096]{1,0:T(8,128)(2,1)S(1)} copy-done((bf16[512,4096]{1,0:T(8,128)(2,1)S(1)}, bf16[512,4096]{1,0:T(8,128)(2,1)}, u32[]{:S(2)}) %copy-start.5) | copy-done | bytes 4194328
  4.7 0.7 copy-done.10
  5.4 2.2 %shard_map.68 = (bf16[512,512]{1,0:T(8,128)(2,1)S(1)}, bf16[512,512]{1,0:T(8,128)(2,1)S(1)}) custom-call(s32[2,32]{1,0:T(2,128)S(1)} %bitcast.6, bf16[512,4096]{1,0:T(8,128)(2,1)S(1)} %copy-done.5, bf16[32,3,128,128]{3,2,1,0:T(8,128)(2,1)S(1)} %copy-done), custom_call_target="tpu_custom_call" | custom-call | flops 268435456 | tf_op jit(solution)/shard_map/pallas_call | solution.py:27
  7.7 7.7 %collective-permute-start.1 = (bf16[512,512]{1,0:T(8,128)(2,1)S(1)}, bf16[512,512]{1,0:T(8,128)(2,1)S(1)}, u32[]{:S(2)}, u32[]{:S(2)}) collective-permute-start(bf16[512,512]{1,0:T(8,128)(2,1)S(1)} %get-tuple-element.23), channel_id=1, source_target_pairs={{1,2},{2,1},{3,4},{4,3},{5,6},{6,5},{7,8},{8,7},{9,10},{10,9},{11,... | collective-permute-start | bytes 1572872 | tf_op jit(solution)/shard_map/ppermute | solution.py:357
  15.4 7.9 %shard_map.67.own_ref = bf16[512,4096]{1,0:T(8,128)(2,1)S(1)} custom-call(s32[2,32]{1,0:T(2,128)S(1)} %bitcast.7, bf16[512,4096]{1,0:T(8,128)(2,1)S(1)} %copy-done.5, bf16[32,3,128,128]{3,2,1,0:T(8,128)(2,1)S(1)} %copy-done), custom_call_target="tpu_custom_call" | custom-call | flops 4294967296 | tf_op jit(solution)/shard_map/pallas_call | solution.py:27
  23.4 1.6 shard_map.69
  25.1 1.3 collective-permute-done.2.come_ref
  26.5 16.6 %all_to_all.20.parts_ref = bf16[32,8,256]{2,1,0:T(8,128)(2,1)S(1)} all-to-all(bf16[32,8,256]{2,1,0:T(8,128)(2,1)S(1)} %bitcast.5), channel_id=1, replica_groups={{0,2,4,6,8,10,12,14,16,18,20,22,24,26,28,30,32,34,36,38,40,42,44,46,48,..., dimensions={0} | all-to-all | bytes 262144 | tf_op jit(solution)/shard_map/all_to_all | solution.py:370
  43.2 13.9 %all_to_all.21 = bf16[32,8,256]{2,1,0:T(8,128)(2,1)S(1)} all-to-all(bf16[32,8,256]{2,1,0:T(8,128)(2,1)S(1)} %shard_map.71), channel_id=1, replica_groups={{0,2,4,6,8,10,12,14,16,18,20,22,24,26,28,30,32,34,36,38,40,42,44,46,48,..., dimensions={0} | all-to-all | bytes 262144 | tf_op jit(solution)/shard_map/all_to_all | solution.py:370
  57.1 1.3 collective-permute-done.3.other_ref
  58.4 1.4 shard_map.72
  59.9 1.7 %collective-permute-start.4 = (bf16[512,256]{1,0:T(8,128)(2,1)S(1)}, bf16[512,256]{1,0:T(8,128)(2,1)S(1)}, u32[]{:S(2)}, u32[]{:S(2)}) collective-permute-start(bf16[512,256]{1,0:T(8,128)(2,1)S(1)} %get-tuple-element.29), channel_id=1, source_target_pairs={{0,64},{64,128},{128,192},{192,0},{1,65},{65,129},{129,193},{193,1... | collective-permute-start | bytes 786440 | tf_op jit(solution)/shard_map/ppermute | solution.py:351
  61.5 1.6 collective-permute-start.8
  63.2 1.8 %collective-permute-start.6 = (bf16[512,256]{1,0:T(8,128)(2,1)S(1)}, bf16[512,256]{1,0:T(8,128)(2,1)S(1)}, u32[]{:S(2)}, u32[]{:S(2)}) collective-permute-start(bf16[512,256]{1,0:T(8,128)(2,1)S(1)} %get-tuple-element.30), channel_id=1, source_target_pairs={{0,192},{64,0},{128,64},{192,128},{1,193},{65,1},{129,65},{193,129... | collective-permute-start | bytes 786440 | tf_op jit(solution)/shard_map/ppermute | solution.py:351
  65.0 4.6 %collective-permute-done.4 = bf16[512,256]{1,0:T(8,128)(2,1)S(1)} collective-permute-done((bf16[512,256]{1,0:T(8,128)(2,1)S(1)}, bf16[512,256]{1,0:T(8,128)(2,1)S(1)}, u32[]{:S(2)}, u32[]{:S(2)}) %collective-permute-start.4) | collective-permute-done | bytes 262176 | tf_op jit(solution)/shard_map/ppermute | solution.py:351
  70.0 1.6 collective-permute-start.7
  71.7 2.0 %collective-permute-start.9 = (bf16[512,256]{1,0:T(8,128)(2,1)S(1)}, bf16[512,256]{1,0:T(8,128)(2,1)S(1)}, u32[]{:S(2)}, u32[]{:S(2)}) collective-permute-start(bf16[512,256]{1,0:T(8,128)(2,1)S(1)} %add_convert_fusion.1), channel_id=1, source_target_pairs={{0,192},{64,0},{128,64},{192,128},{1,193},{65,1},{129,65},{193,129... | collective-permute-start | bytes 786440 | tf_op jit(solution)/shard_map/ppermute | solution.py:351
  73.7 2.6 %collective-permute-done.6 = bf16[512,256]{1,0:T(8,128)(2,1)S(1)} collective-permute-done((bf16[512,256]{1,0:T(8,128)(2,1)S(1)}, bf16[512,256]{1,0:T(8,128)(2,1)S(1)}, u32[]{:S(2)}, u32[]{:S(2)}) %collective-permute-start.6) | collective-permute-done | bytes 262176 | tf_op jit(solution)/shard_map/ppermute | solution.py:351
  76.3 3.8 %collective-permute-done.5 = bf16[512,256]{1,0:T(8,128)(2,1)S(1)} collective-permute-done((bf16[512,256]{1,0:T(8,128)(2,1)S(1)}, bf16[512,256]{1,0:T(8,128)(2,1)S(1)}, u32[]{:S(2)}, u32[]{:S(2)}) %collective-permute-start.5) | collective-permute-done | bytes 262176 | tf_op jit(solution)/shard_map/ppermute | solution.py:351
  80.3 5.4 %collective-permute-done.7 = bf16[512,256]{1,0:T(8,128)(2,1)S(1)} collective-permute-done((bf16[512,256]{1,0:T(8,128)(2,1)S(1)}, bf16[512,256]{1,0:T(8,128)(2,1)S(1)}, u32[]{:S(2)}, u32[]{:S(2)}) %collective-permute-start.7) | collective-permute-done | bytes 262176 | tf_op jit(solution)/shard_map/ppermute | solution.py:351
  85.8 0.6 collective-permute-start.11
  86.4 0.7 collective-permute-start.10
  87.2 1.3 collective-permute-start.15
  88.5 2.9 %collective-permute-done.12.refs_6_ = bf16[512,256]{1,0:T(8,128)(2,1)S(1)} collective-permute-done((bf16[512,256]{1,0:T(8,128)(2,1)S(1)}, bf16[512,256]{1,0:T(8,128)(2,1)S(1)}, u32[]{:S(2)}, u32[]{:S(2)}) %collective-permute-start.12) | collective-permute-done | bytes 262176 | tf_op jit(solution)/shard_map/ppermute | solution.py:351
  91.4 3.7 %collective-permute-done.11.refs_3_ = bf16[512,256]{1,0:T(8,128)(2,1)S(1)} collective-permute-done((bf16[512,256]{1,0:T(8,128)(2,1)S(1)}, bf16[512,256]{1,0:T(8,128)(2,1)S(1)}, u32[]{:S(2)}, u32[]{:S(2)}) %collective-permute-start.11) | collective-permute-done | bytes 262176 | tf_op jit(solution)/shard_map/ppermute | solution.py:351
  95.1 0.8 collective-permute-start.14
  95.9 3.6 %collective-permute-done.10.refs_2_ = bf16[512,256]{1,0:T(8,128)(2,1)S(1)} collective-permute-done((bf16[512,256]{1,0:T(8,128)(2,1)S(1)}, bf16[512,256]{1,0:T(8,128)(2,1)S(1)}, u32[]{:S(2)}, u32[]{:S(2)}) %collective-permute-start.10) | collective-permute-done | bytes 262176 | tf_op jit(solution)/shard_map/ppermute | solution.py:351
  99.5 1.5 collective-permute-done.13.refs_4_
  101.0 1.3 collective-permute-done.14.refs_5_
  102.3 2.0 %shard_map.73 = (bf16[4096,256]{1,0:T(8,128)(2,1)S(1)}, bf16[512,256]{1,0:T(8,128)(2,1)S(1)}, bf16[512,256]{1,0:T(8,128)(2,1)S(1)}, bf16[1024,256]{1,0:T(8,128)(2,1)S(1)}) custom-call(bf16[512,4096]{1,0:T(8,128)(2,1)S(1)} %get-tuple-element.24.full_ref, bf16[512,256]{1,0:T(8,128)(2,1)S(1)} %add_convert_fusion.2.refs_0_, ...), custom_call_target="tpu_custom_call" | custom-call | flops 1073741824 | tf_op jit(solution)/shard_map/pallas_call | solution.py:27
  104.3 1.3 copy-done.2
  105.6 1.9 %collective-permute-done.16.come_ref = bf16[1024,256]{1,0:T(8,128)(2,1)S(1)} collective-permute-done((bf16[1024,256]{1,0:T(8,128)(2,1)S(1)}, bf16[1024,256]{1,0:T(8,128)(2,1)S(1)}, u32[]{:S(2)}, u32[]{:S(2)}) %collective-permute-start.16) | collective-permute-done | bytes 524320 | tf_op jit(solution)/shard_map/ppermute | solution.py:365
  107.6 0.8 copy-done.7
  108.4 16.2 %all_to_all.22.parts_ref = bf16[32,16,256]{2,1,0:T(8,128)(2,1)S(1)} all-to-all(bf16[32,16,256]{2,1,0:T(8,128)(2,1)S(1)} %shard_map.74), channel_id=1, replica_groups={{0,2,4,6,8,10,12,14,16,18,20,22,24,26,28,30,32,34,36,38,40,42,44,46,48,..., dimensions={0} | all-to-all | bytes 524288 | tf_op jit(solution)/shard_map/all_to_all | solution.py:370
  124.6 0.7 copy-done.9
  125.3 6.3 %all-to-all-start.3 = ((bf16[32,16,256]{2,1,0:T(8,128)(2,1)}), bf16[32,16,256]{2,1,0:T(8,128)(2,1)S(1)}, u32[]{:S(2)}, u32[]{:S(2)}) async-start(bf16[32,16,256]{2,1,0:T(8,128)(2,1)} %copy-done.9), calls=%async_computation.3 | async-start | bytes 524288 | tf_op jit(solution)/shard_map/all_to_all | solution.py:370
  131.6 3.3 %collective-permute-start.18 = (bf16[512,256]{1,0:T(8,128)(2,1)}, bf16[512,256]{1,0:T(8,128)(2,1)}, u32[]{:S(2)}, u32[]{:S(2)}) collective-permute-start(bf16[512,256]{1,0:T(8,128)(2,1)} %copy-done.12), channel_id=1, source_target_pairs={{1,2},{2,1},{3,4},{4,3},{5,6},{6,5},{7,8},{8,7},{9,10},{10,9},{11,... | collective-permute-start | bytes 786440 | tf_op jit(solution)/shard_map/ppermute | solution.py:357
  134.9 7.5 %all-to-all-done.3.mine_ref = bf16[32,16,256]{2,1,0:T(8,128)(2,1)S(1)} async-done(((bf16[32,16,256]{2,1,0:T(8,128)(2,1)}), bf16[32,16,256]{2,1,0:T(8,128)(2,1)S(1)}, u32[]{:S(2)}, u32[]{:S(2)}) %all-to-all-start.3) | async-done | bytes 262176 | tf_op jit(solution)/shard_map/all_to_all | solution.py:370
  142.4 0.7 collective-permute-done.18.neighbor_ref
  143.1 1.6 copy-done.3
  144.7 1.0 copy-done.8
  145.7 4.0 %shard_map.78.image_ref = bf16[4096,256]{1,0:T(8,128)(2,1)S(1)} custom-call(s32[2,32]{1,0:T(2,128)S(1)} %bitcast.8, bf16[32,3,128,128]{3,2,1,0:T(8,128)(2,1)S(1)} %copy-done.1, bf16[4096,256]{1,0:T(8,128)(2,1)S(1)} %copy-done.3, bf16[1024,256]{1,0:T(8,128)(2,1)S(1)} %copy-done.8, bf16[512,256]{1,0:T(8,128)(2,1)} %collective-permute-done.18.neighbor_ref), custom_call_target="tpu_custom_call" | custom-call | flops 1073741824 | tf_op jit(solution)/shard_map/pallas_call | solution.py:27
  149.7 0.4 shard_map.76
  150.2 0.6 collective-permute-start.21
  150.8 1.7 collective-permute-start.20
  152.8 8.8 %shard_map.77.inv_ref.rows_ref = bf16[256,256]{1,0:T(8,128)(2,1)S(1)} custom-call(f32[256,256]{1,0:T(8,128)S(1)} %get-tuple-element.37.gram_ref), custom_call_target="tpu_custom_call" | custom-call | flops 17179869184 | tf_op jit(solution)/shard_map/pallas_call | solution.py:27
  161.7 3.5 %final.1 = (bf16[4096,256]{1,0:T(8,128)(2,1)}, bf16[4096,256]{1,0:T(8,128)(2,1)}, f32[256,256]{1,0:T(8,128)}) custom-call(bf16[256,256]{1,0:T(8,128)(2,1)S(1)} %shard_map.77.inv_ref.rows_ref, bf16[256,256]{1,0:T(8,128)(2,1)S(1)} %shard_map.77.inv_ref.rows_ref, bf16[4096,256]{1,0:T(8,128)(2,1)S(1)} %copy-done.4, bf16[4096,256]{1,0:T(8,128)(2,1)S(1)} %shard_map.78.image_ref, ...), custom_call_target="tpu_custom_call" | custom-call | tf_op jit(solution)/shard_map/final/pallas_call | solution.py:495
  (44 shorter events, 1.6 us)
Async XLA Ops:
  0.6 1.9 %copy-start = (bf16[32,3,128,128]{3,2,1,0:T(8,128)(2,1)S(1)}, bf16[32,3,128,128]{3,2,1,0:T(8,128)(2,1)}, u32[]{:S(2)}) copy-start(bf16[32,3,128,128]{3,2,1,0:T(8,128)(2,1)} %coef_ref.5) | copy-start | bytes 9437188
  2.5 2.2 %copy-start.5 = (bf16[512,4096]{1,0:T(8,128)(2,1)S(1)}, bf16[512,4096]{1,0:T(8,128)(2,1)}, u32[]{:S(2)}) copy-start(bf16[512,4096]{1,0:T(8,128)(2,1)} %jac_ref.3) | copy-start | bytes 12582916
  4.7 0.7 copy-start.10
  7.6 15.8 %collective-permute-start = (bf16[512,512]{1,0:T(8,128)(2,1)S(1)}, bf16[512,512]{1,0:T(8,128)(2,1)S(1)}, u32[]{:S(2)}, u32[]{:S(2)}) collective-permute-start(bf16[512,512]{1,0:T(8,128)(2,1)S(1)} %get-tuple-element.22), channel_id=1, source_target_pairs={{0,1},{1,0},{2,3},{3,2},{4,5},{5,4},{6,7},{7,6},{8,9},{9,8},{10,11... | collective-permute-start | bytes 1572872 | tf_op jit(solution)/shard_map/ppermute | solution.py:365
  7.7 15.7 %copy-start.6 = (bf16[4096,256]{1,0:T(8,128)(2,1)S(1)}, bf16[4096,256]{1,0:T(8,128)(2,1)}, u32[]{:S(2)}) copy-start(bf16[4096,256]{1,0:T(8,128)(2,1)} %probe_ref.1) | copy-start | bytes 6291460
  7.7 15.7 %collective-permute-start.1 = (bf16[512,512]{1,0:T(8,128)(2,1)S(1)}, bf16[512,512]{1,0:T(8,128)(2,1)S(1)}, u32[]{:S(2)}, u32[]{:S(2)}) collective-permute-start(bf16[512,512]{1,0:T(8,128)(2,1)S(1)} %get-tuple-element.23), channel_id=1, source_target_pairs={{1,2},{2,1},{3,4},{4,3},{5,6},{6,5},{7,8},{8,7},{9,10},{10,9},{11,... | collective-permute-start | bytes 1572872 | tf_op jit(solution)/shard_map/ppermute | solution.py:357
  25.0 1.4 collective-permute-start.2
  57.1 1.3 collective-permute-start.3
  59.9 9.7 %collective-permute-start.4 = (bf16[512,256]{1,0:T(8,128)(2,1)S(1)}, bf16[512,256]{1,0:T(8,128)(2,1)S(1)}, u32[]{:S(2)}, u32[]{:S(2)}) collective-permute-start(bf16[512,256]{1,0:T(8,128)(2,1)S(1)} %get-tuple-element.29), channel_id=1, source_target_pairs={{0,64},{64,128},{128,192},{192,0},{1,65},{65,129},{129,193},{193,1... | collective-permute-start | bytes 786440 | tf_op jit(solution)/shard_map/ppermute | solution.py:351
  61.5 10.1 %collective-permute-start.8 = (bf16[512,256]{1,0:T(8,128)(2,1)S(1)}, bf16[512,256]{1,0:T(8,128)(2,1)S(1)}, u32[]{:S(2)}, u32[]{:S(2)}) collective-permute-start(bf16[512,256]{1,0:T(8,128)(2,1)S(1)} %get-tuple-element.34), channel_id=1, source_target_pairs={{0,192},{64,0},{128,64},{192,128},{1,193},{65,1},{129,65},{193,129... | collective-permute-start | bytes 786440 | tf_op jit(solution)/shard_map/ppermute | solution.py:351
  63.2 13.1 %collective-permute-start.6 = (bf16[512,256]{1,0:T(8,128)(2,1)S(1)}, bf16[512,256]{1,0:T(8,128)(2,1)S(1)}, u32[]{:S(2)}, u32[]{:S(2)}) collective-permute-start(bf16[512,256]{1,0:T(8,128)(2,1)S(1)} %get-tuple-element.30), channel_id=1, source_target_pairs={{0,192},{64,0},{128,64},{192,128},{1,193},{65,1},{129,65},{193,129... | collective-permute-start | bytes 786440 | tf_op jit(solution)/shard_map/ppermute | solution.py:351
  69.6 10.5 %collective-permute-start.5 = (bf16[512,256]{1,0:T(8,128)(2,1)S(1)}, bf16[512,256]{1,0:T(8,128)(2,1)S(1)}, u32[]{:S(2)}, u32[]{:S(2)}) collective-permute-start(bf16[512,256]{1,0:T(8,128)(2,1)S(1)} %add_convert_fusion.3), channel_id=1, source_target_pairs={{0,64},{64,128},{128,192},{192,0},{1,65},{65,129},{129,193},{193,1... | collective-permute-start | bytes 786440 | tf_op jit(solution)/shard_map/ppermute | solution.py:351
  70.0 15.7 %collective-permute-start.7 = (bf16[512,256]{1,0:T(8,128)(2,1)S(1)}, bf16[512,256]{1,0:T(8,128)(2,1)S(1)}, u32[]{:S(2)}, u32[]{:S(2)}) collective-permute-start(bf16[512,256]{1,0:T(8,128)(2,1)S(1)} %get-tuple-element.32), channel_id=1, source_target_pairs={{0,64},{64,128},{128,192},{192,0},{1,65},{65,129},{129,193},{193,1... | collective-permute-start | bytes 786440 | tf_op jit(solution)/shard_map/ppermute | solution.py:351
  71.7 14.1 %collective-permute-start.9 = (bf16[512,256]{1,0:T(8,128)(2,1)S(1)}, bf16[512,256]{1,0:T(8,128)(2,1)S(1)}, u32[]{:S(2)}, u32[]{:S(2)}) collective-permute-start(bf16[512,256]{1,0:T(8,128)(2,1)S(1)} %add_convert_fusion.1), channel_id=1, source_target_pairs={{0,192},{64,0},{128,64},{192,128},{1,193},{65,1},{129,65},{193,129... | collective-permute-start | bytes 786440 | tf_op jit(solution)/shard_map/ppermute | solution.py:351
  80.2 11.1 %collective-permute-start.12 = (bf16[512,256]{1,0:T(8,128)(2,1)S(1)}, bf16[512,256]{1,0:T(8,128)(2,1)S(1)}, u32[]{:S(2)}, u32[]{:S(2)}) collective-permute-start(bf16[512,256]{1,0:T(8,128)(2,1)S(1)} %add_convert_fusion.2.refs_0_), channel_id=1, source_target_pairs={{0,64},{64,128},{128,192},{192,0},{1,65},{65,129},{129,193},{193,1... | collective-permute-start | bytes 786440 | tf_op jit(solution)/shard_map/ppermute | solution.py:351
  85.8 9.3 %collective-permute-start.11 = (bf16[512,256]{1,0:T(8,128)(2,1)S(1)}, bf16[512,256]{1,0:T(8,128)(2,1)S(1)}, u32[]{:S(2)}, u32[]{:S(2)}) collective-permute-start(bf16[512,256]{1,0:T(8,128)(2,1)S(1)} %add_convert_fusion.refs_1_), channel_id=1, source_target_pairs={{0,192},{64,0},{128,64},{192,128},{1,193},{65,1},{129,65},{193,129... | collective-permute-start | bytes 786440 | tf_op jit(solution)/shard_map/ppermute | solution.py:351
  86.4 13.0 %collective-permute-start.10 = (bf16[512,256]{1,0:T(8,128)(2,1)S(1)}, bf16[512,256]{1,0:T(8,128)(2,1)S(1)}, u32[]{:S(2)}, u32[]{:S(2)}) collective-permute-start(bf16[512,256]{1,0:T(8,128)(2,1)S(1)} %add_convert_fusion.2.refs_0_), channel_id=1, source_target_pairs={{0,192},{64,0},{128,64},{192,128},{1,193},{65,1},{129,65},{193,129... | collective-permute-start | bytes 786440 | tf_op jit(solution)/shard_map/ppermute | solution.py:351
  87.2 12.3 %collective-permute-start.15 = (bf16[512,256]{1,0:T(8,128)(2,1)S(1)}, bf16[512,256]{1,0:T(8,128)(2,1)S(1)}, u32[]{:S(2)}, u32[]{:S(2)}) collective-permute-start(bf16[512,256]{1,0:T(8,128)(2,1)S(1)} %add_convert_fusion.refs_1_), channel_id=1, source_target_pairs={{0,64},{64,128},{128,192},{192,0},{1,65},{65,129},{129,193},{193,1... | collective-permute-start | bytes 786440 | tf_op jit(solution)/shard_map/ppermute | solution.py:351
  91.3 9.6 %collective-permute-start.13 = (bf16[512,256]{1,0:T(8,128)(2,1)S(1)}, bf16[512,256]{1,0:T(8,128)(2,1)S(1)}, u32[]{:S(2)}, u32[]{:S(2)}) collective-permute-start(bf16[512,256]{1,0:T(8,128)(2,1)S(1)} %collective-permute-done.12.refs_6_), channel_id=1, source_target_pairs={{0,64},{64,128},{128,192},{192,0},{1,65},{65,129},{129,193},{193,1... | collective-permute-start | bytes 786440 | tf_op jit(solution)/shard_map/ppermute | solution.py:351
  95.1 7.2 %collective-permute-start.14 = (bf16[512,256]{1,0:T(8,128)(2,1)S(1)}, bf16[512,256]{1,0:T(8,128)(2,1)S(1)}, u32[]{:S(2)}, u32[]{:S(2)}) collective-permute-start(bf16[512,256]{1,0:T(8,128)(2,1)S(1)} %collective-permute-done.11.refs_3_), channel_id=1, source_target_pairs={{0,192},{64,0},{128,64},{192,128},{1,193},{65,1},{129,65},{193,129... | collective-permute-start | bytes 786440 | tf_op jit(solution)/shard_map/ppermute | solution.py:351
  102.3 40.8 %copy-start.1 = (bf16[32,3,128,128]{3,2,1,0:T(8,128)(2,1)S(1)}, bf16[32,3,128,128]{3,2,1,0:T(8,128)(2,1)}, u32[]{:S(2)}) copy-start(bf16[32,3,128,128]{3,2,1,0:T(8,128)(2,1)} %coef_ref.5) | copy-start | bytes 9437188
  104.3 1.3 copy-start.2
  105.6 19.0 %copy-start.12 = (bf16[512,256]{1,0:T(8,128)(2,1)}, bf16[512,256]{1,0:T(8,128)(2,1)S(1)}, u32[]{:S(2)}) copy-start(bf16[512,256]{1,0:T(8,128)(2,1)S(1)} %get-tuple-element.39) | copy-start | bytes 786436
  105.6 37.5 %copy-start.11 = (s32[32,2]{0,1:T(2,128)S(1)}, s32[32,2]{0,1:T(2,128)}, u32[]{:S(2)}) copy-start(s32[32,2]{0,1:T(2,128)} %param.7) | copy-start | bytes 772
  105.6 1.9 %collective-permute-start.16 = (bf16[1024,256]{1,0:T(8,128)(2,1)S(1)}, bf16[1024,256]{1,0:T(8,128)(2,1)S(1)}, u32[]{:S(2)}, u32[]{:S(2)}) collective-permute-start(bf16[1024,256]{1,0:T(8,128)(2,1)S(1)} %get-tuple-element.36), channel_id=1, source_target_pairs={{0,1},{1,0},{2,3},{3,2},{4,5},{5,4},{6,7},{7,6},{8,9},{9,8},{10,11... | collective-permute-start | bytes 1572872 | tf_op jit(solution)/shard_map/ppermute | solution.py:365
  107.6 0.8 copy-start.7
  124.6 0.7 copy-start.9
  125.3 17.1 %all-to-all-start.3 = ((bf16[32,16,256]{2,1,0:T(8,128)(2,1)}), bf16[32,16,256]{2,1,0:T(8,128)(2,1)S(1)}, u32[]{:S(2)}, u32[]{:S(2)}) async-start(bf16[32,16,256]{2,1,0:T(8,128)(2,1)} %copy-done.9), calls=%async_computation.3 | async-start | bytes 524288 | tf_op jit(solution)/shard_map/all_to_all | solution.py:370
  131.6 11.4 %collective-permute-start.18 = (bf16[512,256]{1,0:T(8,128)(2,1)}, bf16[512,256]{1,0:T(8,128)(2,1)}, u32[]{:S(2)}, u32[]{:S(2)}) collective-permute-start(bf16[512,256]{1,0:T(8,128)(2,1)} %copy-done.12), channel_id=1, source_target_pairs={{1,2},{2,1},{3,4},{4,3},{5,6},{6,5},{7,8},{8,7},{9,10},{10,9},{11,... | collective-permute-start | bytes 786440 | tf_op jit(solution)/shard_map/ppermute | solution.py:357
  142.4 7.4 %collective-permute-start.17 = (bf16[32,16,256]{2,1,0:T(8,128)(2,1)S(1)}, bf16[32,16,256]{2,1,0:T(8,128)(2,1)S(1)}, u32[]{:S(2)}, u32[]{:S(2)}) collective-permute-start(bf16[32,16,256]{2,1,0:T(8,128)(2,1)S(1)} %all-to-all-done.3.mine_ref), channel_id=1, source_target_pairs={{0,1},{1,0},{2,3},{3,2},{4,5},{5,4},{6,7},{7,6},{8,9},{9,8},{10,11... | collective-permute-start | bytes 786440 | tf_op jit(solution)/shard_map/ppermute | solution.py:365
  143.1 1.6 copy-start.3
  144.7 1.0 copy-start.8
  150.2 11.5 %collective-permute-start.21 = (bf16[320,128]{1,0:T(8,128)(2,1)S(1)}, bf16[320,128]{1,0:T(8,128)(2,1)S(1)}, u32[]{:S(2)}, u32[]{:S(2)}) collective-permute-start(bf16[320,128]{1,0:T(8,128)(2,1)S(1)} %get-tuple-element.40.refs_0_), channel_id=1, source_target_pairs={{0,128},{64,192},{128,0},{192,64},{1,129},{65,193},{129,1},{193,65... | collective-permute-start | bytes 245768 | tf_op jit(solution)/shard_map/ppermute | solution.py:351
  150.8 10.9 %collective-permute-start.20 = (bf16[320,128]{1,0:T(8,128)(2,1)S(1)}, bf16[320,128]{1,0:T(8,128)(2,1)S(1)}, u32[]{:S(2)}, u32[]{:S(2)}) collective-permute-start(bf16[320,128]{1,0:T(8,128)(2,1)S(1)} %get-tuple-element.40.refs_0_), channel_id=1, source_target_pairs={{0,192},{64,0},{128,64},{192,128},{1,193},{65,1},{129,65},{193,129... | collective-permute-start | bytes 245768 | tf_op jit(solution)/shard_map/ppermute | solution.py:351
  152.4 9.3 %collective-permute-start.19 = (bf16[320,128]{1,0:T(8,128)(2,1)S(1)}, bf16[320,128]{1,0:T(8,128)(2,1)S(1)}, u32[]{:S(2)}, u32[]{:S(2)}) collective-permute-start(bf16[320,128]{1,0:T(8,128)(2,1)S(1)} %get-tuple-element.40.refs_0_), channel_id=1, source_target_pairs={{0,64},{64,128},{128,192},{192,0},{1,65},{65,129},{129,193},{193,1... | collective-permute-start | bytes 245768 | tf_op jit(solution)/shard_map/ppermute | solution.py:351
  152.8 8.9 %copy-start.4 = (bf16[4096,256]{1,0:T(8,128)(2,1)S(1)}, bf16[4096,256]{1,0:T(8,128)(2,1)}, u32[]{:S(2)}) copy-start(bf16[4096,256]{1,0:T(8,128)(2,1)} %copy-done.2) | copy-start | bytes 6291460

commit v3 on v2

--- a/solution.py
+++ b/solution.py
@@ -51,26 +51,26 @@
     return jax.ShapeDtypeStruct(dims, dtype)
 
 
-def edges_kernel(off_ref, jac_ref, coef_ref, partner_ref, neighbor_ref, acc):
-    count = coef_ref.shape[0]
+def edges_kernel(count, off_ref, jac_ref, coef_ref, partner_ref, neighbor_ref, acc):
+    side = pl.program_id(0)
     acc[...] = jnp.zeros_like(acc)
-    for side in range(2):
-        for i in range(REACH):
-            block = i + side * (count - REACH)
-            columns = jac_ref[:, block * BLK : (block + 1) * BLK]
-            for j in range(2):
-                target = block + off_ref[j, block]
-                place = target + REACH if side == 0 else target - count + REACH
-                outside = target < 0 if side == 0 else target >= count
-
-                @pl.when(outside)
-                def _():
-                    acc[place] += dot(columns, coef_ref[block, j + 1])
-
-    core = core_index()
     for i in range(REACH):
-        partner_ref[:, i * BLK : (i + 1) * BLK] = acc[(1 - core) * REACH + i].astype(BF16)
-        neighbor_ref[:, i * BLK : (i + 1) * BLK] = acc[core * REACH + i].astype(BF16)
+        block = i + side * (count - REACH)
+        columns = jac_ref[:, i * BLK : (i + 1) * BLK]
+        for j in range(2):
+            target = block + off_ref[j, block]
+            place = jnp.where(side == 0, target + REACH, target - count)
+
+            @pl.when((place >= 0) & (place < REACH))
+            def _():
+                acc[place] += dot(columns, coef_ref[i, j + 1])
+
+    for out_ref, wanted in ((partner_ref, 1 - core_index()), (neighbor_ref, core_index())):
+
+        @pl.when(side == wanted)
+        def _():
+            for i in range(REACH):
+                out_ref[:, i * BLK : (i + 1) * BLK] = acc[i].astype(BF16)
 
 
 def own_kernel(off_ref, jac_ref, coef_ref, out_ref, acc):
@@ -84,7 +84,7 @@
         acc[block + REACH] = dot(columns, coef_ref[block, 0])
         return carry
 
-    lax.fori_loop(0, count, diagonal, 0, unroll=4)
+    lax.fori_loop(0, count, diagonal, 0, unroll=8)
 
     def band(block, carry):
         columns = jac_ref[:, pl.ds(pl.multiple_of(block * BLK, BLK), BLK)]
@@ -92,7 +92,7 @@
             acc[block + REACH + off_ref[j, block]] += dot(columns, coef_ref[block, j + 1])
         return carry
 
-    lax.fori_loop(0, count, band, 0, unroll=4)
+    lax.fori_loop(0, count, band, 0, unroll=8)
     for block in range(count):
         out_ref[:, block * BLK : (block + 1) * BLK] = acc[block + REACH].astype(BF16)
 
@@ -201,21 +201,26 @@
     give_ref[2 * rows :] = sample_ref[pl.ds(pl.multiple_of((1 - core) * last, EDGE), EDGE), :]
 
 
-def prior_kernel(off_ref, coef_ref, sample_ref, come_ref, neighbor_ref, out_ref, ext):
+def prior_block(block, off_ref, coefs, ext, base):
+    total = dot(coefs[0], ext[pl.ds(pl.multiple_of(base + block * BLK, BLK), BLK), :])
+    for j in range(2):
+        start = base + (block + off_ref[j, block]) * BLK
+        total += dot(coefs[j + 1], ext[pl.ds(pl.multiple_of(start, BLK), BLK), :])
+    return total.astype(BF16)
+
+
+def outer_kernel(off_ref, coef_ref, sample_ref, come_ref, neighbor_ref, inv_ref, out_ref, ext):
     count, rows = coef_ref.shape[0], sample_ref.shape[0]
     core = core_index()
-    far = EDGE + rows
-    ext[EDGE : EDGE + rows] = sample_ref[...]
-    ext[pl.ds(pl.multiple_of((1 - core) * far, EDGE), EDGE)] = come_ref[come_ref.shape[0] - EDGE :]
-    ext[pl.ds(pl.multiple_of(core * far, EDGE), EDGE)] = neighbor_ref[...]
-
-    def apply(block, carry):
-        starts = [(block + REACH) * BLK] + [(block + REACH + off_ref[j, block]) * BLK for j in range(2)]
-        result = sum(dot(coef_ref[block, j], ext[pl.ds(pl.multiple_of(starts[j], BLK), BLK), :]) for j in range(3))
-        out_ref[pl.ds(pl.multiple_of(block * BLK, BLK), BLK), :] = result.astype(BF16)
-        return carry
-
-    lax.fori_loop(0, count, apply, 0, unroll=4)
+    ext[EDGE : 3 * EDGE] = sample_ref[: 2 * EDGE]
+    ext[3 * EDGE : 5 * EDGE] = sample_ref[rows - 2 * EDGE :]
+    ext[pl.ds(pl.multiple_of((1 - core) * (5 * EDGE), EDGE), EDGE)] = come_ref[come_ref.shape[0] - EDGE :]
+    ext[pl.ds(pl.multiple_of(core * (5 * EDGE), EDGE), EDGE)] = neighbor_ref[...]
+    for i in range(REACH):
+        for side, base in ((0, EDGE), (1, 5 * EDGE - rows)):
+            block = i + side * (count - REACH)
+            coefs = [coef_ref[block, j] for j in range(3)]
+            out_ref[side, i * BLK : (i + 1) * BLK] = prior_block(block, off_ref, coefs, ext, base)
 
 
 def packed(full):
@@ -306,8 +311,10 @@
     return dot_nt(a, b, HI) if nt else jnp.dot(a, b, precision=HI, preferred_element_type=F32)
 
 
-def factor_kernel(scale, gram_ref, out_ref, a_ref, m_ref, inv_ref):
+def factor_kernel(scale, gram_ref, off_ref, coef_ref, sample_ref, out_ref, image_ref, a_ref, m_ref, inv_ref):
     n = out_ref.shape[0]
+    count = coef_ref.shape[0]
+    inner = (count - 2 * REACH) * NB // n
     gram = gram_ref[...] * scale
     index = [lax.broadcasted_iota(jnp.int32, (n, n), d) for d in (0, 1)]
     diagonal = jnp.where(index[0] == index[1], gram, 0.0)
@@ -319,6 +326,10 @@
         hi, nx = lo + NB, lo + 2 * NB
         inverse = factor_inverse(a_ref[lo:hi, lo:hi])
         inv_ref[lo:hi, lo:hi] = inverse
+        first = REACH + lo // NB * inner
+        for block in range(first, first + inner):
+            coefs = [coef_ref[block, j] for j in range(3)]
+            image_ref[block * BLK : (block + 1) * BLK] = prior_block(block, off_ref, coefs, sample_ref, 0)
         if hi < n:
             upper = exact(inverse, a_ref[lo:hi, hi:])
             lower = exact(a_ref[hi:, lo:hi], inverse, nt=True)
@@ -333,11 +344,16 @@
     out_ref[...] = (inv_ref[...] * across).astype(BF16)
 
 
-def final_kernel(scale, inv_ref, rows_ref, sample_ref, image_ref, *refs):
+def final_kernel(scale, inv_ref, rows_ref, sample_ref, image_ref, outer_ref, *refs):
     seconds, (basis_ref, mapped_ref, ritz_ref) = refs[:-3], refs[-3:]
     inverse = inv_ref[...]
     basis_ref[...] = dot_nt(sample_ref[...], inverse).astype(BF16)
-    mapped_ref[...] = dot_nt(image_ref[...], inverse).astype(BF16)
+    step, last = pl.program_id(0), pl.num_programs(0) - 1
+    rows = image_ref.shape[0]
+    top = jnp.where(step == 0, outer_ref[0], image_ref[:EDGE])
+    bottom = jnp.where(step == last, outer_ref[1], image_ref[rows - EDGE :])
+    mapped_ref[:EDGE] = dot_nt(top, inverse).astype(BF16)
+    mapped_ref[rows - EDGE :] = dot_nt(bottom, inverse).astype(BF16)
     total = seconds[0][...].astype(F32)
     for part in seconds[1:]:
         total += part[...].astype(F32)
@@ -379,14 +395,23 @@
     offsets = offsets.T
     flops = 2 * nobs * npar * width
 
-    partner, neighbor = call(
-        edges_kernel,
-        [shape(nobs, EDGE)] * 2,
-        [SMEM, VMEM, VMEM],
-        [offsets, jacobian, coeffs],
-        [pltpu.VMEM((2 * REACH, nobs, BLK), F32)],
-        flops=flops // 4,
-    )
+    whole = lambda *dims: pl.BlockSpec(dims, lambda i: (0,) * len(dims))
+    last = npar // EDGE - 1
+    partner, neighbor = pl.pallas_call(
+        functools.partial(edges_kernel, count),
+        name="edges",
+        grid=(2,),
+        out_shape=[shape(nobs, EDGE)] * 2,
+        in_specs=[
+            SMEM,
+            pl.BlockSpec((nobs, EDGE), lambda i: (0, i * last)),
+            pl.BlockSpec((REACH, *coeffs.shape[1:]), lambda i: (i * last, 0, 0, 0)),
+        ],
+        out_specs=[whole(nobs, EDGE)] * 2,
+        scratch_shapes=[pltpu.VMEM((REACH, nobs, BLK), F32)],
+        compiler_params=pltpu.CompilerParams(vmem_limit_bytes=50 * 2**20),
+        cost_estimate=pl.CostEstimate(flops=flops // 4, bytes_accessed=0, transcendentals=0),
+    )(offsets, jacobian, coeffs)
     from_neighbor = to_neighbor(neighbor)
     from_partner = swapped(partner)
     own = call(
@@ -453,12 +478,12 @@
         flops=flops,
     )
     come = swapped(give)
-    from_neighbor = to_neighbor(neighbor)
     both = shape(chips, 16, width)
     part = call(pair_gram_kernel, both, [VMEM] * 2, [keep, come], mib=4)
     total = call(total_gram_kernel, both, [VMEM], [exchanged(part)], mib=4)
     mine = exchanged(total)
     other = swapped(mine)
+    from_neighbor = to_neighbor(neighbor)
     gram, second = call(
         moments_kernel,
         [shape(width, width, dtype=F32), shape(5 * NB, 2 * NB)],
@@ -469,27 +494,26 @@
         flops=flops // 8,
     )
     seconds = [second] + [shifted(second, "obs", by) for by in (1, -1, 2)]
-    image = call(
-        prior_kernel,
-        shape(npar, width),
-        [SMEM] + [VMEM] * 4,
-        [offsets, coeffs, sample, come, from_neighbor],
-        [pltpu.VMEM((npar + 2 * EDGE, width), BF16)],
-        mib=8,
-        flops=flops,
-    )
     total_par = npar * lax.axis_size("par")
-    inverse = call(
+    inverse, image = call(
         functools.partial(factor_kernel, 1.0 / total_par),
-        shape(width, width),
-        [VMEM],
-        [gram],
+        [shape(width, width), shape(npar, width)],
+        [VMEM, SMEM, VMEM, VMEM],
+        [gram, offsets, coeffs, sample],
         [pltpu.VMEM((width, width), F32)] * 3,
-        mib=8,
+        mib=16,
         flops=16 * flops,
     )
+    outer = call(
+        outer_kernel,
+        shape(2, EDGE, width),
+        [SMEM] + [VMEM] * 5,
+        [offsets, coeffs, sample, come, from_neighbor, inverse],
+        [pltpu.VMEM((6 * EDGE, width), BF16)],
+        mib=16,
+        flops=flops // 4,
+    )
     steps = 4
-    whole = lambda *dims: pl.BlockSpec(dims, lambda i: (0, 0))
     by_rows = pl.BlockSpec((npar // steps, width), lambda i: (i, 0))
     few = pl.BlockSpec((width // steps, width), lambda i: (i, 0))
     return pl.pallas_call(
@@ -497,10 +521,10 @@
         name="final",
         grid=(steps,),
         out_shape=[shape(npar, width), shape(npar, width), shape(width, width, dtype=F32)],
-        in_specs=[whole(width, width), few, by_rows, by_rows] + [whole(*second.shape)] * len(seconds),
+        in_specs=[whole(width, width), few, by_rows, by_rows, whole(2, EDGE, width)] + [whole(*second.shape)] * len(seconds),
         out_specs=[by_rows, by_rows, few],
         compiler_params=pltpu.CompilerParams(vmem_limit_bytes=12 * 2**20),
-    )(inverse, inverse, sample, image, *seconds)
+    )(inverse, inverse, sample, image, outer, *seconds)
 
 
 def solution(mesh):

time: 167 us -> 159 us (0.952)
  blocking collectives: 46.7 us -> 64 us
  local copies, waits for them, and re-layouts: 10.2 us -> 0.69 us
  waiting for transfers between devices: 42.2 us -> 34.2 us
  starting transfers between devices: 32.8 us -> 26.7 us
  Pallas kernels: 32.2 us -> 29.5 us
    all_to_all x3 -> x4, blocking collectives: 46.7 us -> 64 us  [exchanged(): lax.all_to_all(parts, 'par', 0, 0, axis_index_groups=groups, tiled=True)]
    unnamed x26 -> x8, local copies, waits for them, and re-layouts: 10.2 us -> 0.69 us
    all_to_all x1 -> x0, waiting for transfers between devices: 7.47 us -> none  [exchanged(): lax.all_to_all(parts, 'par', 0, 0, axis_index_groups=groups, tiled=True)]
    all_to_all x1 -> x0, starting transfers between devices: 6.32 us -> none  [exchanged(): lax.all_to_all(parts, 'par', 0, 0, axis_index_groups=groups, tiled=True)]
    pallas_call x12 -> x11, Pallas kernels: 28.6 us -> 23 us  [call(): pl.pallas_call(kernel, out_shape=outs, in_specs=specs, out_specs=jax.tree...]
    pallas_call x0 -> x1, Pallas kernels: none -> 2.89 us  [body(): pl.pallas_call(functools.partial(edges_kernel, count), name='edges', grid...]
  transfers between devices with their start and end apart: 23 -> 22, of which waited for: 14 -> 13; matrix products, arithmetic and copies ran while one was open for 0% -> 0% of each run, Pallas kernels for 13% -> 11%
where the time goes in v3:
time: 159 us; the launch traced here: 156 us
  blocking collectives  64 us (40%)
  waiting for transfers between devices  34.2 us (22%)
  Pallas kernels  29.5 us (19%)
  starting transfers between devices  26.7 us (17%)
    all_to_all x4, blocking collectives, exchanged(): lax.all_to_all(parts, 'par', 0, 0, axis_index_groups=groups, tiled=True)  64 us
    ppermute x15, waiting for transfers between devices, shifted(): lax.ppermute(value, axis, [(i, (i + by) % count) for i in range(count)])  29.4 us
    pallas_call x11, Pallas kernels, call(): pl.pallas_call(kernel, out_shape=outs, in_specs=specs, out_specs=jax.tree...  23 us
    ppermute x15, starting transfers between devices, shifted(): lax.ppermute(value, axis, [(i, (i + by) % count) for i in range(count)])  15.3 us
    ppermute x2, starting transfers between devices, to_neighbor(): return lax.ppermute(value, 'par', pairs)  11.2 us
    ppermute x5, waiting for transfers between devices, swapped(): lax.ppermute(value, 'par', [(i, i ^ 1) for i in range(lax.axis_size('par'...  4.58 us
    pallas_call x1, Pallas kernels, body(): pl.pallas_call(functools.partial(final_kernel, 1.0 / (nobs * ranks)), nam...  3.55 us
  transfers between devices with their start and end apart: 22, of which 13 were waited for; matrix products, arithmetic and copies ran while one was open for 0% of the time, Pallas kernels for 11%

profile of v3, /device:TPU:6, one launch (start us, length us, event | category | flops | bytes accessed | tf_op | source)
XLA Modules:
  0.0 156.2 jit_solution(8518784150456686730)
XLA Ops:
  0.6 0.7 copy-done.3
  1.3 2.9 %edges.1 = (bf16[512,512]{1,0:T(8,128)(2,1)S(1)}, bf16[512,512]{1,0:T(8,128)(2,1)S(1)}) custom-call(s32[2,32]{1,0:T(2,128)S(1)} %bitcast.6, bf16[512,4096]{1,0:T(8,128)(2,1)} %jac_ref.3, bf16[32,3,128,128]{3,2,1,0:T(8,128)(2,1)} %coef_ref.7), custom_call_target="tpu_custom_call" | custom-call | flops 268435456 | tf_op jit(solution)/shard_map/edges/pallas_call | solution.py:400
  4.2 0.1 collective-permute-start
  4.3 7.8 %collective-permute-start.1 = (bf16[512,512]{1,0:T(8,128)(2,1)S(1)}, bf16[512,512]{1,0:T(8,128)(2,1)S(1)}, u32[]{:S(2)}, u32[]{:S(2)}) collective-permute-start(bf16[512,512]{1,0:T(8,128)(2,1)S(1)} %get-tuple-element.25), channel_id=1, source_target_pairs={{1,2},{2,1},{3,4},{4,3},{5,6},{6,5},{7,8},{8,7},{9,10},{10,9},{11,... | collective-permute-start | bytes 1572872 | tf_op jit(solution)/shard_map/ppermute | solution.py:373
  12.1 6.6 %shard_map.67.own_ref = bf16[512,4096]{1,0:T(8,128)(2,1)S(1)} custom-call(s32[2,32]{1,0:T(2,128)S(1)} %bitcast.7, bf16[512,4096]{1,0:T(8,128)(2,1)S(1)} %copy-done.1, bf16[32,3,128,128]{3,2,1,0:T(8,128)(2,1)S(1)} %copy-done), custom_call_target="tpu_custom_call" | custom-call | flops 4294967296 | tf_op jit(solution)/shard_map/pallas_call | solution.py:27
  18.8 0.2 collective-permute-done.1.neighbor_ref
  18.9 1.7 %shard_map.68 = (bf16[512,4096]{1,0:T(8,128)(2,1)S(1)}, bf16[256,256]{1,0:T(8,128)(2,1)S(1)}, bf16[256,256]{1,0:T(8,128)(2,1)S(1)}) custom-call(bf16[512,4096]{1,0:T(8,128)(2,1)S(1)} %shard_map.67.own_ref, bf16[512,512]{1,0:T(8,128)(2,1)S(1)} %collective-permute-done.partner_ref, bf16[512,512]{1,0:T(8,128)(2,1)S(1)} %collective-permute-done.1.neighbor_ref, ...), custom_call_target="tpu_custom_call" | custom-call | flops 1073741824 | tf_op jit(solution)/shard_map/pallas_call | solution.py:27
  20.6 0.1 collective-permute-start.2
  20.7 1.3 collective-permute-done.2.come_ref
  22.1 17.7 %all_to_all.20.parts_ref = bf16[32,8,256]{2,1,0:T(8,128)(2,1)S(1)} all-to-all(bf16[32,8,256]{2,1,0:T(8,128)(2,1)S(1)} %bitcast.5), channel_id=1, replica_groups={{0,2,4,6,8,10,12,14,16,18,20,22,24,26,28,30,32,34,36,38,40,42,44,46,48,..., dimensions={0} | all-to-all | bytes 262144 | tf_op jit(solution)/shard_map/all_to_all | solution.py:386
  39.8 13.9 %all_to_all.21 = bf16[32,8,256]{2,1,0:T(8,128)(2,1)S(1)} all-to-all(bf16[32,8,256]{2,1,0:T(8,128)(2,1)S(1)} %shard_map.70), channel_id=1, replica_groups={{0,2,4,6,8,10,12,14,16,18,20,22,24,26,28,30,32,34,36,38,40,42,44,46,48,..., dimensions={0} | all-to-all | bytes 262144 | tf_op jit(solution)/shard_map/all_to_all | solution.py:386
  53.8 1.3 collective-permute-done.3.other_ref
  55.1 1.4 shard_map.71
  56.5 1.7 %collective-permute-start.4 = (bf16[512,256]{1,0:T(8,128)(2,1)S(1)}, bf16[512,256]{1,0:T(8,128)(2,1)S(1)}, u32[]{:S(2)}, u32[]{:S(2)}) collective-permute-start(bf16[512,256]{1,0:T(8,128)(2,1)S(1)} %get-tuple-element.31), channel_id=1, source_target_pairs={{0,64},{64,128},{128,192},{192,0},{1,65},{65,129},{129,193},{193,1... | collective-permute-start | bytes 786440 | tf_op jit(solution)/shard_map/ppermute | solution.py:367
  58.2 1.7 %collective-permute-start.8 = (bf16[512,256]{1,0:T(8,128)(2,1)S(1)}, bf16[512,256]{1,0:T(8,128)(2,1)S(1)}, u32[]{:S(2)}, u32[]{:S(2)}) collective-permute-start(bf16[512,256]{1,0:T(8,128)(2,1)S(1)} %get-tuple-element.36), channel_id=1, source_target_pairs={{0,192},{64,0},{128,64},{192,128},{1,193},{65,1},{129,65},{193,129... | collective-permute-start | bytes 786440 | tf_op jit(solution)/shard_map/ppermute | solution.py:367
  59.8 1.8 %collective-permute-start.6 = (bf16[512,256]{1,0:T(8,128)(2,1)S(1)}, bf16[512,256]{1,0:T(8,128)(2,1)S(1)}, u32[]{:S(2)}, u32[]{:S(2)}) collective-permute-start(bf16[512,256]{1,0:T(8,128)(2,1)S(1)} %get-tuple-element.32), channel_id=1, source_target_pairs={{0,192},{64,0},{128,64},{192,128},{1,193},{65,1},{129,65},{193,129... | collective-permute-start | bytes 786440 | tf_op jit(solution)/shard_map/ppermute | solution.py:367
  61.6 4.6 %collective-permute-done.4 = bf16[512,256]{1,0:T(8,128)(2,1)S(1)} collective-permute-done((bf16[512,256]{1,0:T(8,128)(2,1)S(1)}, bf16[512,256]{1,0:T(8,128)(2,1)S(1)}, u32[]{:S(2)}, u32[]{:S(2)}) %collective-permute-start.4) | collective-permute-done | bytes 262176 | tf_op jit(solution)/shard_map/ppermute | solution.py:367
  66.3 0.4 collective-permute-start.5
  66.7 1.6 %collective-permute-start.7 = (bf16[512,256]{1,0:T(8,128)(2,1)S(1)}, bf16[512,256]{1,0:T(8,128)(2,1)S(1)}, u32[]{:S(2)}, u32[]{:S(2)}) collective-permute-start(bf16[512,256]{1,0:T(8,128)(2,1)S(1)} %get-tuple-element.34), channel_id=1, source_target_pairs={{0,64},{64,128},{128,192},{192,0},{1,65},{65,129},{129,193},{193,1... | collective-permute-start | bytes 786440 | tf_op jit(solution)/shard_map/ppermute | solution.py:367
  68.3 2.0 %collective-permute-start.9 = (bf16[512,256]{1,0:T(8,128)(2,1)S(1)}, bf16[512,256]{1,0:T(8,128)(2,1)S(1)}, u32[]{:S(2)}, u32[]{:S(2)}) collective-permute-start(bf16[512,256]{1,0:T(8,128)(2,1)S(1)} %add_convert_fusion.1), channel_id=1, source_target_pairs={{0,192},{64,0},{128,64},{192,128},{1,193},{65,1},{129,65},{193,129... | collective-permute-start | bytes 786440 | tf_op jit(solution)/shard_map/ppermute | solution.py:367
  70.4 2.6 %collective-permute-done.6 = bf16[512,256]{1,0:T(8,128)(2,1)S(1)} collective-permute-done((bf16[512,256]{1,0:T(8,128)(2,1)S(1)}, bf16[512,256]{1,0:T(8,128)(2,1)S(1)}, u32[]{:S(2)}, u32[]{:S(2)}) %collective-permute-start.6) | collective-permute-done | bytes 262176 | tf_op jit(solution)/shard_map/ppermute | solution.py:367
  73.0 3.8 %collective-permute-done.5 = bf16[512,256]{1,0:T(8,128)(2,1)S(1)} collective-permute-done((bf16[512,256]{1,0:T(8,128)(2,1)S(1)}, bf16[512,256]{1,0:T(8,128)(2,1)S(1)}, u32[]{:S(2)}, u32[]{:S(2)}) %collective-permute-start.5) | collective-permute-done | bytes 262176 | tf_op jit(solution)/shard_map/ppermute | solution.py:367
  76.8 0.1 add_convert_fusion.2.refs_0_
  77.0 5.4 %collective-permute-done.7 = bf16[512,256]{1,0:T(8,128)(2,1)S(1)} collective-permute-done((bf16[512,256]{1,0:T(8,128)(2,1)S(1)}, bf16[512,256]{1,0:T(8,128)(2,1)S(1)}, u32[]{:S(2)}, u32[]{:S(2)}) %collective-permute-start.7) | collective-permute-done | bytes 262176 | tf_op jit(solution)/shard_map/ppermute | solution.py:367
  82.4 0.1 add_convert_fusion.refs_1_
  82.5 0.6 collective-permute-start.11
  83.1 0.7 collective-permute-start.10
  83.9 1.3 collective-permute-start.15
  85.1 2.9 %collective-permute-done.12.refs_6_ = bf16[512,256]{1,0:T(8,128)(2,1)S(1)} collective-permute-done((bf16[512,256]{1,0:T(8,128)(2,1)S(1)}, bf16[512,256]{1,0:T(8,128)(2,1)S(1)}, u32[]{:S(2)}, u32[]{:S(2)}) %collective-permute-start.12) | collective-permute-done | bytes 262176 | tf_op jit(solution)/shard_map/ppermute | solution.py:367
  88.0 3.8 %collective-permute-done.11.refs_3_ = bf16[512,256]{1,0:T(8,128)(2,1)S(1)} collective-permute-done((bf16[512,256]{1,0:T(8,128)(2,1)S(1)}, bf16[512,256]{1,0:T(8,128)(2,1)S(1)}, u32[]{:S(2)}, u32[]{:S(2)}) %collective-permute-start.11) | collective-permute-done | bytes 262176 | tf_op jit(solution)/shard_map/ppermute | solution.py:367
  91.8 0.8 collective-permute-start.14
  92.5 3.6 %collective-permute-done.10.refs_2_ = bf16[512,256]{1,0:T(8,128)(2,1)S(1)} collective-permute-done((bf16[512,256]{1,0:T(8,128)(2,1)S(1)}, bf16[512,256]{1,0:T(8,128)(2,1)S(1)}, u32[]{:S(2)}, u32[]{:S(2)}) %collective-permute-start.10) | collective-permute-done | bytes 262176 | tf_op jit(solution)/shard_map/ppermute | solution.py:367
  96.1 1.5 collective-permute-done.13.refs_4_
  97.6 1.3 collective-permute-done.14.refs_5_
  98.9 2.0 %shard_map.72 = (bf16[4096,256]{1,0:T(8,128)(2,1)S(1)}, bf16[512,256]{1,0:T(8,128)(2,1)S(1)}, bf16[512,256]{1,0:T(8,128)(2,1)S(1)}, bf16[1024,256]{1,0:T(8,128)(2,1)S(1)}) custom-call(bf16[512,4096]{1,0:T(8,128)(2,1)S(1)} %get-tuple-element.26.full_ref, bf16[512,256]{1,0:T(8,128)(2,1)S(1)} %add_convert_fusion.2.refs_0_, ...), custom_call_target="tpu_custom_call" | custom-call | flops 1073741824 | tf_op jit(solution)/shard_map/pallas_call | solution.py:27
  100.9 0.1 collective-permute-start.16
  101.0 1.9 %collective-permute-done.16.come_ref = bf16[1024,256]{1,0:T(8,128)(2,1)S(1)} collective-permute-done((bf16[1024,256]{1,0:T(8,128)(2,1)S(1)}, bf16[1024,256]{1,0:T(8,128)(2,1)S(1)}, u32[]{:S(2)}, u32[]{:S(2)}) %collective-permute-start.16) | collective-permute-done | bytes 524320 | tf_op jit(solution)/shard_map/ppermute | solution.py:381
  102.9 0.1 shard_map.73
  103.0 16.2 %all_to_all.22.parts_ref = bf16[32,16,256]{2,1,0:T(8,128)(2,1)S(1)} all-to-all(bf16[32,16,256]{2,1,0:T(8,128)(2,1)S(1)} %shard_map.73), channel_id=1, replica_groups={{0,2,4,6,8,10,12,14,16,18,20,22,24,26,28,30,32,34,36,38,40,42,44,46,48,..., dimensions={0} | all-to-all | bytes 524288 | tf_op jit(solution)/shard_map/all_to_all | solution.py:386
  119.2 16.2 %all_to_all.23.mine_ref = bf16[32,16,256]{2,1,0:T(8,128)(2,1)S(1)} all-to-all(bf16[32,16,256]{2,1,0:T(8,128)(2,1)S(1)} %shard_map.74), channel_id=1, replica_groups={{0,2,4,6,8,10,12,14,16,18,20,22,24,26,28,30,32,34,36,38,40,42,44,46,48,..., dimensions={0} | all-to-all | bytes 524288 | tf_op jit(solution)/shard_map/all_to_all | solution.py:386
  135.4 3.4 %collective-permute-start.18 = (bf16[512,256]{1,0:T(8,128)(2,1)S(1)}, bf16[512,256]{1,0:T(8,128)(2,1)S(1)}, u32[]{:S(2)}, u32[]{:S(2)}) collective-permute-start(bf16[512,256]{1,0:T(8,128)(2,1)S(1)} %get-tuple-element.43), channel_id=1, source_target_pairs={{1,2},{2,1},{3,4},{4,3},{5,6},{6,5},{7,8},{8,7},{9,10},{10,9},{11,... | collective-permute-start | bytes 786440 | tf_op jit(solution)/shard_map/ppermute | solution.py:373
  138.8 0.4 shard_map.75
  139.3 0.6 collective-permute-start.21
  139.9 1.6 %collective-permute-start.20 = (bf16[320,128]{1,0:T(8,128)(2,1)S(1)}, bf16[320,128]{1,0:T(8,128)(2,1)S(1)}, u32[]{:S(2)}, u32[]{:S(2)}) collective-permute-start(bf16[320,128]{1,0:T(8,128)(2,1)S(1)} %get-tuple-element.44.refs_0_), channel_id=1, source_target_pairs={{0,192},{64,0},{128,64},{192,128},{1,193},{65,1},{129,65},{193,129... | collective-permute-start | bytes 245768 | tf_op jit(solution)/shard_map/ppermute | solution.py:367
  141.5 0.4 collective-permute-start.19
  141.9 9.5 %shard_map.76 = (bf16[256,256]{1,0:T(8,128)(2,1)S(1)}, bf16[4096,256]{1,0:T(8,128)(2,1)S(1)}) custom-call(f32[256,256]{1,0:T(8,128)S(1)} %get-tuple-element.39.gram_ref, s32[2,32]{1,0:T(2,128)S(1)} %bitcast.8, bf16[32,3,128,128]{3,2,1,0:T(8,128)(2,1)S(1)} %copy-done, bf16[4096,256]{1,0:T(8,128)(2,1)S(1)} %get-tuple-element.40.sample_ref), custom_call_target="tpu_custom_call" | custom-call | flops 17179869184 | tf_op jit(solution)/shard_map/pallas_call | solution.py:27
  151.4 1.2 shard_map.77.outer_ref
  152.7 3.5 %final.1 = (bf16[4096,256]{1,0:T(8,128)(2,1)}, bf16[4096,256]{1,0:T(8,128)(2,1)}, f32[256,256]{1,0:T(8,128)}) custom-call(bf16[256,256]{1,0:T(8,128)(2,1)S(1)} %get-tuple-element.41.inv_ref.rows_ref, bf16[256,256]{1,0:T(8,128)(2,1)S(1)} %get-tuple-element.41.inv_ref.rows_ref, bf16[4096,256]{1,0:T(8,128)(2,1)S(1)} %get-tuple-element.40.sample_ref, ...), custom_call_target="tpu_custom_call" | custom-call | tf_op jit(solution)/shard_map/final/pallas_call | solution.py:519
  (25 shorter events, 0.4 us)
Async XLA Ops:
  0.6 0.7 copy-start.3
  1.3 10.8 %copy-start = (bf16[32,3,128,128]{3,2,1,0:T(8,128)(2,1)S(1)}, bf16[32,3,128,128]{3,2,1,0:T(8,128)(2,1)}, u32[]{:S(2)}) copy-start(bf16[32,3,128,128]{3,2,1,0:T(8,128)(2,1)} %coef_ref.7) | copy-start | bytes 9437188
  1.3 10.8 %copy-start.1 = (bf16[512,4096]{1,0:T(8,128)(2,1)S(1)}, bf16[512,4096]{1,0:T(8,128)(2,1)}, u32[]{:S(2)}) copy-start(bf16[512,4096]{1,0:T(8,128)(2,1)} %jac_ref.3) | copy-start | bytes 12582916
  4.2 14.5 %collective-permute-start = (bf16[512,512]{1,0:T(8,128)(2,1)S(1)}, bf16[512,512]{1,0:T(8,128)(2,1)S(1)}, u32[]{:S(2)}, u32[]{:S(2)}) collective-permute-start(bf16[512,512]{1,0:T(8,128)(2,1)S(1)} %get-tuple-element.24), channel_id=1, source_target_pairs={{0,1},{1,0},{2,3},{3,2},{4,5},{5,4},{6,7},{7,6},{8,9},{9,8},{10,11... | collective-permute-start | bytes 1572872 | tf_op jit(solution)/shard_map/ppermute | solution.py:381
  4.3 14.6 %copy-start.2 = (bf16[4096,256]{1,0:T(8,128)(2,1)S(1)}, bf16[4096,256]{1,0:T(8,128)(2,1)}, u32[]{:S(2)}) copy-start(bf16[4096,256]{1,0:T(8,128)(2,1)} %probe_ref.1) | copy-start | bytes 6291460
  4.3 14.6 %collective-permute-start.1 = (bf16[512,512]{1,0:T(8,128)(2,1)S(1)}, bf16[512,512]{1,0:T(8,128)(2,1)S(1)}, u32[]{:S(2)}, u32[]{:S(2)}) collective-permute-start(bf16[512,512]{1,0:T(8,128)(2,1)S(1)} %get-tuple-element.25), channel_id=1, source_target_pairs={{1,2},{2,1},{3,4},{4,3},{5,6},{6,5},{7,8},{8,7},{9,10},{10,9},{11,... | collective-permute-start | bytes 1572872 | tf_op jit(solution)/shard_map/ppermute | solution.py:373
  20.6 1.4 collective-permute-start.2
  53.8 1.3 collective-permute-start.3
  56.5 9.7 %collective-permute-start.4 = (bf16[512,256]{1,0:T(8,128)(2,1)S(1)}, bf16[512,256]{1,0:T(8,128)(2,1)S(1)}, u32[]{:S(2)}, u32[]{:S(2)}) collective-permute-start(bf16[512,256]{1,0:T(8,128)(2,1)S(1)} %get-tuple-element.31), channel_id=1, source_target_pairs={{0,64},{64,128},{128,192},{192,0},{1,65},{65,129},{129,193},{193,1... | collective-permute-start | bytes 786440 | tf_op jit(solution)/shard_map/ppermute | solution.py:367
  58.2 10.1 %collective-permute-start.8 = (bf16[512,256]{1,0:T(8,128)(2,1)S(1)}, bf16[512,256]{1,0:T(8,128)(2,1)S(1)}, u32[]{:S(2)}, u32[]{:S(2)}) collective-permute-start(bf16[512,256]{1,0:T(8,128)(2,1)S(1)} %get-tuple-element.36), channel_id=1, source_target_pairs={{0,192},{64,0},{128,64},{192,128},{1,193},{65,1},{129,65},{193,129... | collective-permute-start | bytes 786440 | tf_op jit(solution)/shard_map/ppermute | solution.py:367
  59.8 13.1 %collective-permute-start.6 = (bf16[512,256]{1,0:T(8,128)(2,1)S(1)}, bf16[512,256]{1,0:T(8,128)(2,1)S(1)}, u32[]{:S(2)}, u32[]{:S(2)}) collective-permute-start(bf16[512,256]{1,0:T(8,128)(2,1)S(1)} %get-tuple-element.32), channel_id=1, source_target_pairs={{0,192},{64,0},{128,64},{192,128},{1,193},{65,1},{129,65},{193,129... | collective-permute-start | bytes 786440 | tf_op jit(solution)/shard_map/ppermute | solution.py:367
  66.3 10.5 %collective-permute-start.5 = (bf16[512,256]{1,0:T(8,128)(2,1)S(1)}, bf16[512,256]{1,0:T(8,128)(2,1)S(1)}, u32[]{:S(2)}, u32[]{:S(2)}) collective-permute-start(bf16[512,256]{1,0:T(8,128)(2,1)S(1)} %add_convert_fusion.3), channel_id=1, source_target_pairs={{0,64},{64,128},{128,192},{192,0},{1,65},{65,129},{129,193},{193,1... | collective-permute-start | bytes 786440 | tf_op jit(solution)/shard_map/ppermute | solution.py:367
  66.7 15.7 %collective-permute-start.7 = (bf16[512,256]{1,0:T(8,128)(2,1)S(1)}, bf16[512,256]{1,0:T(8,128)(2,1)S(1)}, u32[]{:S(2)}, u32[]{:S(2)}) collective-permute-start(bf16[512,256]{1,0:T(8,128)(2,1)S(1)} %get-tuple-element.34), channel_id=1, source_target_pairs={{0,64},{64,128},{128,192},{192,0},{1,65},{65,129},{129,193},{193,1... | collective-permute-start | bytes 786440 | tf_op jit(solution)/shard_map/ppermute | solution.py:367
  68.3 14.0 %collective-permute-start.9 = (bf16[512,256]{1,0:T(8,128)(2,1)S(1)}, bf16[512,256]{1,0:T(8,128)(2,1)S(1)}, u32[]{:S(2)}, u32[]{:S(2)}) collective-permute-start(bf16[512,256]{1,0:T(8,128)(2,1)S(1)} %add_convert_fusion.1), channel_id=1, source_target_pairs={{0,192},{64,0},{128,64},{192,128},{1,193},{65,1},{129,65},{193,129... | collective-permute-start | bytes 786440 | tf_op jit(solution)/shard_map/ppermute | solution.py:367
  76.9 11.1 %collective-permute-start.12 = (bf16[512,256]{1,0:T(8,128)(2,1)S(1)}, bf16[512,256]{1,0:T(8,128)(2,1)S(1)}, u32[]{:S(2)}, u32[]{:S(2)}) collective-permute-start(bf16[512,256]{1,0:T(8,128)(2,1)S(1)} %add_convert_fusion.2.refs_0_), channel_id=1, source_target_pairs={{0,64},{64,128},{128,192},{192,0},{1,65},{65,129},{129,193},{193,1... | collective-permute-start | bytes 786440 | tf_op jit(solution)/shard_map/ppermute | solution.py:367
  82.5 9.3 %collective-permute-start.11 = (bf16[512,256]{1,0:T(8,128)(2,1)S(1)}, bf16[512,256]{1,0:T(8,128)(2,1)S(1)}, u32[]{:S(2)}, u32[]{:S(2)}) collective-permute-start(bf16[512,256]{1,0:T(8,128)(2,1)S(1)} %add_convert_fusion.refs_1_), channel_id=1, source_target_pairs={{0,192},{64,0},{128,64},{192,128},{1,193},{65,1},{129,65},{193,129... | collective-permute-start | bytes 786440 | tf_op jit(solution)/shard_map/ppermute | solution.py:367
  83.1 13.0 %collective-permute-start.10 = (bf16[512,256]{1,0:T(8,128)(2,1)S(1)}, bf16[512,256]{1,0:T(8,128)(2,1)S(1)}, u32[]{:S(2)}, u32[]{:S(2)}) collective-permute-start(bf16[512,256]{1,0:T(8,128)(2,1)S(1)} %add_convert_fusion.2.refs_0_), channel_id=1, source_target_pairs={{0,192},{64,0},{128,64},{192,128},{1,193},{65,1},{129,65},{193,129... | collective-permute-start | bytes 786440 | tf_op jit(solution)/shard_map/ppermute | solution.py:367
  83.9 12.3 %collective-permute-start.15 = (bf16[512,256]{1,0:T(8,128)(2,1)S(1)}, bf16[512,256]{1,0:T(8,128)(2,1)S(1)}, u32[]{:S(2)}, u32[]{:S(2)}) collective-permute-start(bf16[512,256]{1,0:T(8,128)(2,1)S(1)} %add_convert_fusion.refs_1_), channel_id=1, source_target_pairs={{0,64},{64,128},{128,192},{192,0},{1,65},{65,129},{129,193},{193,1... | collective-permute-start | bytes 786440 | tf_op jit(solution)/shard_map/ppermute | solution.py:367
  88.0 9.6 %collective-permute-start.13 = (bf16[512,256]{1,0:T(8,128)(2,1)S(1)}, bf16[512,256]{1,0:T(8,128)(2,1)S(1)}, u32[]{:S(2)}, u32[]{:S(2)}) collective-permute-start(bf16[512,256]{1,0:T(8,128)(2,1)S(1)} %collective-permute-done.12.refs_6_), channel_id=1, source_target_pairs={{0,64},{64,128},{128,192},{192,0},{1,65},{65,129},{129,193},{193,1... | collective-permute-start | bytes 786440 | tf_op jit(solution)/shard_map/ppermute | solution.py:367
  91.8 7.2 %collective-permute-start.14 = (bf16[512,256]{1,0:T(8,128)(2,1)S(1)}, bf16[512,256]{1,0:T(8,128)(2,1)S(1)}, u32[]{:S(2)}, u32[]{:S(2)}) collective-permute-start(bf16[512,256]{1,0:T(8,128)(2,1)S(1)} %collective-permute-done.11.refs_3_), channel_id=1, source_target_pairs={{0,192},{64,0},{128,64},{192,128},{1,193},{65,1},{129,65},{193,129... | collective-permute-start | bytes 786440 | tf_op jit(solution)/shard_map/ppermute | solution.py:367
  100.9 2.0 %collective-permute-start.16 = (bf16[1024,256]{1,0:T(8,128)(2,1)S(1)}, bf16[1024,256]{1,0:T(8,128)(2,1)S(1)}, u32[]{:S(2)}, u32[]{:S(2)}) collective-permute-start(bf16[1024,256]{1,0:T(8,128)(2,1)S(1)} %get-tuple-element.38), channel_id=1, source_target_pairs={{0,1},{1,0},{2,3},{3,2},{4,5},{5,4},{6,7},{7,6},{8,9},{9,8},{10,11... | collective-permute-start | bytes 1572872 | tf_op jit(solution)/shard_map/ppermute | solution.py:381
  135.4 3.4 %collective-permute-start.17 = (bf16[32,16,256]{2,1,0:T(8,128)(2,1)S(1)}, bf16[32,16,256]{2,1,0:T(8,128)(2,1)S(1)}, u32[]{:S(2)}, u32[]{:S(2)}) collective-permute-start(bf16[32,16,256]{2,1,0:T(8,128)(2,1)S(1)} %all_to_all.23.mine_ref), channel_id=1, source_target_pairs={{0,1},{1,0},{2,3},{3,2},{4,5},{5,4},{6,7},{7,6},{8,9},{9,8},{10,11... | collective-permute-start | bytes 786440 | tf_op jit(solution)/shard_map/ppermute | solution.py:381
  135.4 16.0 %collective-permute-start.18 = (bf16[512,256]{1,0:T(8,128)(2,1)S(1)}, bf16[512,256]{1,0:T(8,128)(2,1)S(1)}, u32[]{:S(2)}, u32[]{:S(2)}) collective-permute-start(bf16[512,256]{1,0:T(8,128)(2,1)S(1)} %get-tuple-element.43), channel_id=1, source_target_pairs={{1,2},{2,1},{3,4},{4,3},{5,6},{6,5},{7,8},{8,7},{9,10},{10,9},{11,... | collective-permute-start | bytes 786440 | tf_op jit(solution)/shard_map/ppermute | solution.py:373
  139.3 13.4 %collective-permute-start.21 = (bf16[320,128]{1,0:T(8,128)(2,1)S(1)}, bf16[320,128]{1,0:T(8,128)(2,1)S(1)}, u32[]{:S(2)}, u32[]{:S(2)}) collective-permute-start(bf16[320,128]{1,0:T(8,128)(2,1)S(1)} %get-tuple-element.44.refs_0_), channel_id=1, source_target_pairs={{0,128},{64,192},{128,0},{192,64},{1,129},{65,193},{129,1},{193,65... | collective-permute-start | bytes 245768 | tf_op jit(solution)/shard_map/ppermute | solution.py:367
  139.9 12.8 %collective-permute-start.20 = (bf16[320,128]{1,0:T(8,128)(2,1)S(1)}, bf16[320,128]{1,0:T(8,128)(2,1)S(1)}, u32[]{:S(2)}, u32[]{:S(2)}) collective-permute-start(bf16[320,128]{1,0:T(8,128)(2,1)S(1)} %get-tuple-element.44.refs_0_), channel_id=1, source_target_pairs={{0,192},{64,0},{128,64},{192,128},{1,193},{65,1},{129,65},{193,129... | collective-permute-start | bytes 245768 | tf_op jit(solution)/shard_map/ppermute | solution.py:367
  141.5 11.1 %collective-permute-start.19 = (bf16[320,128]{1,0:T(8,128)(2,1)S(1)}, bf16[320,128]{1,0:T(8,128)(2,1)S(1)}, u32[]{:S(2)}, u32[]{:S(2)}) collective-permute-start(bf16[320,128]{1,0:T(8,128)(2,1)S(1)} %get-tuple-element.44.refs_0_), channel_id=1, source_target_pairs={{0,64},{64,128},{128,192},{192,0},{1,65},{65,129},{129,193},{193,1... | collective-permute-start | bytes 245768 | tf_op jit(solution)/shard_map/ppermute | solution.py:367

commit v4 on v3

--- a/solution.py
+++ b/solution.py
@@ -94,7 +94,13 @@
 
     lax.fori_loop(0, count, band, 0, unroll=8)
     for block in range(count):
-        out_ref[:, block * BLK : (block + 1) * BLK] = acc[block + REACH].astype(BF16)
+        place = block % REACH
+        out_ref[block // REACH, :, place * BLK : (place + 1) * BLK] = acc[block + REACH].astype(BF16)
+
+
+def inner_kernel(own_ref, probe_ref, out_ref):
+    chunks = own_ref.shape[0]
+    out_ref[...] = sum(dot(own_ref[i], probe_ref[i * EDGE : (i + 1) * EDGE, :]) for i in range(1, chunks - 1))
 
 
 def halves(rows):
@@ -102,17 +108,23 @@
     return [pl.ds(pl.multiple_of(i * rows, rows), rows) for i in (core, 1 - core)]
 
 
-def forward_kernel(own_ref, partner_ref, neighbor_ref, probe_ref, full_ref, keep_ref, give_ref, acc):
-    width = own_ref.shape[1]
-    core = core_index()
-    full_ref[...] = own_ref[...]
-    for come, side in ((partner_ref, 1 - core), (neighbor_ref, core)):
-        here = pl.ds(pl.multiple_of(side * (width - EDGE), EDGE), EDGE)
-        full_ref[:, here] = (own_ref[:, here].astype(F32) + come[...].astype(F32)).astype(BF16)
-    acc[...] = dot(full_ref[...], probe_ref[...])
-    mine, other = halves(keep_ref.shape[0])
-    keep_ref[...] = acc[mine, :].astype(BF16)
-    give_ref[...] = acc[other, :].astype(BF16)
+def forward_kernel(own_ref, partner_ref, neighbor_ref, probe_ref, inner_ref, full_ref, keep_ref, give_ref, acc):
+    side = pl.program_id(0)
+    come = jnp.where(side == 1 - core_index(), partner_ref[...], neighbor_ref[...])
+    chunk = (own_ref[0].astype(F32) + come.astype(F32)).astype(BF16)
+    full_ref[0] = chunk
+    product = dot(chunk, probe_ref[...])
+
+    @pl.when(side == 0)
+    def _():
+        acc[...] = inner_ref[...] + product
+
+    @pl.when(side == 1)
+    def _():
+        acc[...] += product
+        mine, other = halves(keep_ref.shape[0])
+        keep_ref[...] = acc[mine, :].astype(BF16)
+        give_ref[...] = acc[other, :].astype(BF16)
 
 
 def pair_kernel(keep_ref, come_ref, out_ref):
@@ -165,13 +177,11 @@
 
 def sample_kernel(ranks, full_ref, mine_ref, other_ref, *refs):
     outs, fwd = refs[:-1], refs[-1]
-    rows = full_ref.shape[1] // ranks // 2
     in_order(mine_ref, other_ref, fwd)
     for rel in range(ranks):
         owner = lax.rem(lax.axis_index("obs") + rel, ranks)
         for half in range(2):
-            start = pl.multiple_of(owner * (2 * rows) + half * rows, rows)
-            outs[2 * rel + half][...] = dot_tn(full_ref[:, pl.ds(start, rows)], fwd[...]).astype(BF16)
+            outs[2 * rel + half][...] = dot_tn(full_ref[2 * owner + half], fwd[...]).astype(BF16)
 
 
 def project_kernel(ranks, full_ref, *refs):
@@ -186,7 +196,7 @@
             piece = pieces[2 * rel + half][...]
             start = pl.multiple_of(owner * (2 * rows) + half * rows, rows)
             sample_ref[pl.ds(start, rows), :] = piece
-            total += dot(full_ref[:, pl.ds(start, rows)], piece)
+            total += dot(full_ref[2 * owner + half], piece)
             square += dot_tn(piece, piece)
     acc[...] = total
     gram[...] = square
@@ -209,18 +219,13 @@
     return total.astype(BF16)
 
 
-def outer_kernel(off_ref, coef_ref, sample_ref, come_ref, neighbor_ref, inv_ref, out_ref, ext):
-    count, rows = coef_ref.shape[0], sample_ref.shape[0]
+def fill_ends(sample_ref, come_ref, neighbor_ref, ext):
+    rows = sample_ref.shape[0]
     core = core_index()
     ext[EDGE : 3 * EDGE] = sample_ref[: 2 * EDGE]
     ext[3 * EDGE : 5 * EDGE] = sample_ref[rows - 2 * EDGE :]
     ext[pl.ds(pl.multiple_of((1 - core) * (5 * EDGE), EDGE), EDGE)] = come_ref[come_ref.shape[0] - EDGE :]
     ext[pl.ds(pl.multiple_of(core * (5 * EDGE), EDGE), EDGE)] = neighbor_ref[...]
-    for i in range(REACH):
-        for side, base in ((0, EDGE), (1, 5 * EDGE - rows)):
-            block = i + side * (count - REACH)
-            coefs = [coef_ref[block, j] for j in range(3)]
-            out_ref[side, i * BLK : (i + 1) * BLK] = prior_block(block, off_ref, coefs, ext, base)
 
 
 def packed(full):
@@ -311,10 +316,13 @@
     return dot_nt(a, b, HI) if nt else jnp.dot(a, b, precision=HI, preferred_element_type=F32)
 
 
-def factor_kernel(scale, gram_ref, off_ref, coef_ref, sample_ref, out_ref, image_ref, a_ref, m_ref, inv_ref):
+def factor_kernel(
+    scale, gram_ref, off_ref, coef_ref, sample_ref, come_ref, neighbor_ref, out_ref, image_ref, a_ref, m_ref, inv_ref, ext
+):
     n = out_ref.shape[0]
-    count = coef_ref.shape[0]
-    inner = (count - 2 * REACH) * NB // n
+    count, rows = coef_ref.shape[0], sample_ref.shape[0]
+    share = count * NB // n
+    fill_ends(sample_ref, come_ref, neighbor_ref, ext)
     gram = gram_ref[...] * scale
     index = [lax.broadcasted_iota(jnp.int32, (n, n), d) for d in (0, 1)]
     diagonal = jnp.where(index[0] == index[1], gram, 0.0)
@@ -326,10 +334,15 @@
         hi, nx = lo + NB, lo + 2 * NB
         inverse = factor_inverse(a_ref[lo:hi, lo:hi])
         inv_ref[lo:hi, lo:hi] = inverse
-        first = REACH + lo // NB * inner
-        for block in range(first, first + inner):
+        first = lo // NB * share
+        for block in range(first, first + share):
             coefs = [coef_ref[block, j] for j in range(3)]
-            image_ref[block * BLK : (block + 1) * BLK] = prior_block(block, off_ref, coefs, sample_ref, 0)
+            source, base = sample_ref, 0
+            if block < REACH:
+                source, base = ext, EDGE
+            elif block >= count - REACH:
+                source, base = ext, 5 * EDGE - rows
+            image_ref[block * BLK : (block + 1) * BLK] = prior_block(block, off_ref, coefs, source, base)
         if hi < n:
             upper = exact(inverse, a_ref[lo:hi, hi:])
             lower = exact(a_ref[hi:, lo:hi], inverse, nt=True)
@@ -344,16 +357,11 @@
     out_ref[...] = (inv_ref[...] * across).astype(BF16)
 
 
-def final_kernel(scale, inv_ref, rows_ref, sample_ref, image_ref, outer_ref, *refs):
+def final_kernel(scale, inv_ref, rows_ref, sample_ref, image_ref, *refs):
     seconds, (basis_ref, mapped_ref, ritz_ref) = refs[:-3], refs[-3:]
     inverse = inv_ref[...]
     basis_ref[...] = dot_nt(sample_ref[...], inverse).astype(BF16)
-    step, last = pl.program_id(0), pl.num_programs(0) - 1
-    rows = image_ref.shape[0]
-    top = jnp.where(step == 0, outer_ref[0], image_ref[:EDGE])
-    bottom = jnp.where(step == last, outer_ref[1], image_ref[rows - EDGE :])
-    mapped_ref[:EDGE] = dot_nt(top, inverse).astype(BF16)
-    mapped_ref[rows - EDGE :] = dot_nt(bottom, inverse).astype(BF16)
+    mapped_ref[...] = dot_nt(image_ref[...], inverse).astype(BF16)
     total = seconds[0][...].astype(F32)
     for part in seconds[1:]:
         total += part[...].astype(F32)
@@ -396,7 +404,8 @@
     flops = 2 * nobs * npar * width
 
     whole = lambda *dims: pl.BlockSpec(dims, lambda i: (0,) * len(dims))
-    last = npar // EDGE - 1
+    chunks = npar // EDGE
+    last = chunks - 1
     partner, neighbor = pl.pallas_call(
         functools.partial(edges_kernel, count),
         name="edges",
@@ -416,22 +425,32 @@
     from_partner = swapped(partner)
     own = call(
         own_kernel,
-        shape(nobs, npar),
+        shape(chunks, nobs, EDGE),
         [SMEM, VMEM, VMEM],
         [offsets, jacobian, coeffs],
         [pltpu.VMEM((count + 2 * REACH, nobs, BLK), F32)],
         flops=4 * flops,
     )
     half = shape(nobs // 2, width)
-    full, keep, give = call(
+    inner = call(inner_kernel, shape(nobs, width, dtype=F32), [VMEM] * 2, [own, probes], flops=flops)
+    edge_chunk = pl.BlockSpec((1, nobs, EDGE), lambda i: (i * last, 0, 0))
+    full, keep, give = pl.pallas_call(
         forward_kernel,
-        [shape(nobs, npar), half, half],
-        [VMEM] * 4,
-        [own, from_partner, from_neighbor, probes],
-        [pltpu.VMEM((nobs, width), F32)],
-        mib=16,
-        flops=flops,
-    )
+        name="forward",
+        grid=(2,),
+        out_shape=[shape(chunks, nobs, EDGE), half, half],
+        in_specs=[
+            edge_chunk,
+            whole(nobs, EDGE),
+            whole(nobs, EDGE),
+            pl.BlockSpec((EDGE, width), lambda i: (i * last, 0)),
+            whole(nobs, width),
+        ],
+        out_specs=[edge_chunk, whole(*half.shape), whole(*half.shape)],
+        scratch_shapes=[pltpu.VMEM((nobs, width), F32)],
+        input_output_aliases={0: 0},
+        compiler_params=pltpu.CompilerParams(vmem_limit_bytes=24 * 2**20),
+    )(own, from_partner, from_neighbor, probes, inner)
     part = call(pair_kernel, half, [VMEM] * 2, [keep, swapped(give)], mib=4)
     parts = exchanged(part.reshape(chips, nobs // 2 // chips, width))
     total = call(total_kernel, shape(*parts.shape), [VMEM], [parts], mib=4)
@@ -498,20 +517,11 @@
     inverse, image = call(
         functools.partial(factor_kernel, 1.0 / total_par),
         [shape(width, width), shape(npar, width)],
-        [VMEM, SMEM, VMEM, VMEM],
-        [gram, offsets, coeffs, sample],
-        [pltpu.VMEM((width, width), F32)] * 3,
+        [VMEM, SMEM] + [VMEM] * 4,
+        [gram, offsets, coeffs, sample, come, from_neighbor],
+        [pltpu.VMEM((width, width), F32)] * 3 + [pltpu.VMEM((6 * EDGE, width), BF16)],
         mib=16,
         flops=16 * flops,
-    )
-    outer = call(
-        outer_kernel,
-        shape(2, EDGE, width),
-        [SMEM] + [VMEM] * 5,
-        [offsets, coeffs, sample, come, from_neighbor, inverse],
-        [pltpu.VMEM((6 * EDGE, width), BF16)],
-        mib=16,
-        flops=flops // 4,
     )
     steps = 4
     by_rows = pl.BlockSpec((npar // steps, width), lambda i: (i, 0))
@@ -521,10 +531,10 @@
         name="final",
         grid=(steps,),
         out_shape=[shape(npar, width), shape(npar, width), shape(width, width, dtype=F32)],
-        in_specs=[whole(width, width), few, by_rows, by_rows, whole(2, EDGE, width)] + [whole(*second.shape)] * len(seconds),
+        in_specs=[whole(width, width), few, by_rows, by_rows] + [whole(*second.shape)] * len(seconds),
         out_specs=[by_rows, by_rows, few],
         compiler_params=pltpu.CompilerParams(vmem_limit_bytes=12 * 2**20),
-    )(inverse, inverse, sample, image, outer, *seconds)
+    )(inverse, inverse, sample, image, *seconds)
 
 
 def solution(mesh):

time: 159 us -> 159 us (level)
  waiting for transfers between devices: 34.2 us -> 37.1 us
  Pallas kernels: 29.5 us -> 27.9 us
    ppermute x2, waiting for transfers between devices: 0.18 us -> 3.24 us  [to_neighbor(): return lax.ppermute(value, 'par', pairs)]
    pallas_call x11 -> x10, Pallas kernels: 23 us -> 20.6 us  [call(): pl.pallas_call(kernel, out_shape=outs, in_specs=specs, out_specs=jax.tree...]
where the time goes in v4:
time: 159 us; the launch traced here: 157 us
  blocking collectives  63.6 us (40%)
  waiting for transfers between devices  37.1 us (23%)
  Pallas kernels  27.9 us (18%)
  starting transfers between devices  26.9 us (17%)
    all_to_all x4, blocking collectives, exchanged(): lax.all_to_all(parts, 'par', 0, 0, axis_index_groups=groups, tiled=True)  63.6 us
    ppermute x15, waiting for transfers between devices, shifted(): lax.ppermute(value, axis, [(i, (i + by) % count) for i in range(count)])  29.3 us
    pallas_call x10, Pallas kernels, call(): pl.pallas_call(kernel, out_shape=outs, in_specs=specs, out_specs=jax.tree...  20.6 us
    ppermute x15, starting transfers between devices, shifted(): lax.ppermute(value, axis, [(i, (i + by) % count) for i in range(count)])  15.5 us
    ppermute x2, starting transfers between devices, to_neighbor(): return lax.ppermute(value, 'par', pairs)  11.2 us
    ppermute x5, waiting for transfers between devices, swapped(): lax.ppermute(value, 'par', [(i, i ^ 1) for i in range(lax.axis_size('par'...  4.58 us
    pallas_call x1, Pallas kernels, body(): pl.pallas_call(functools.partial(final_kernel, 1.0 / (nobs * ranks)), nam...  3.55 us
    ppermute x2, waiting for transfers between devices, to_neighbor(): return lax.ppermute(value, 'par', pairs)  3.24 us
  transfers between devices with their start and end apart: 22, of which 13 were waited for; matrix products, arithmetic and copies ran while one was open for 0% of the time, Pallas kernels for 11%

profile of v4, /device:TPU:6, one launch (start us, length us, event | category | flops | bytes accessed | tf_op | source)
XLA Modules:
  0.0 157.4 jit_solution(9220840794770259986)
XLA Ops:
  0.6 0.7 copy-done.3
  1.3 2.9 %edges.1 = (bf16[512,512]{1,0:T(8,128)(2,1)S(1)}, bf16[512,512]{1,0:T(8,128)(2,1)S(1)}) custom-call(s32[2,32]{1,0:T(2,128)S(1)} %bitcast.6, bf16[512,4096]{1,0:T(8,128)(2,1)} %jac_ref.3, bf16[32,3,128,128]{3,2,1,0:T(8,128)(2,1)} %coef_ref.5), custom_call_target="tpu_custom_call" | custom-call | flops 268435456 | tf_op jit(solution)/shard_map/edges/pallas_call | solution.py:409
  4.2 0.1 collective-permute-start
  4.3 7.8 %collective-permute-start.1 = (bf16[512,512]{1,0:T(8,128)(2,1)S(1)}, bf16[512,512]{1,0:T(8,128)(2,1)S(1)}, u32[]{:S(2)}, u32[]{:S(2)}) collective-permute-start(bf16[512,512]{1,0:T(8,128)(2,1)S(1)} %get-tuple-element.25), channel_id=1, source_target_pairs={{1,2},{2,1},{3,4},{4,3},{5,6},{6,5},{7,8},{8,7},{9,10},{10,9},{11,... | collective-permute-start | bytes 1572872 | tf_op jit(solution)/shard_map/ppermute | solution.py:381
  12.1 6.1 %shard_map.67.own_ref = bf16[8,512,512]{2,1,0:T(8,128)(2,1)S(1)} custom-call(s32[2,32]{1,0:T(2,128)S(1)} %bitcast.7, bf16[512,4096]{1,0:T(8,128)(2,1)S(1)} %copy-done.1, bf16[32,3,128,128]{3,2,1,0:T(8,128)(2,1)S(1)} %copy-done.2), custom_call_target="tpu_custom_call" | custom-call | flops 4294967296 | tf_op jit(solution)/shard_map/pallas_call | solution.py:27
  18.3 1.0 shard_map.68.inner_ref
  19.3 0.9 forward.1
  20.2 0.1 collective-permute-start.2
  20.3 1.3 collective-permute-done.2.come_ref
  21.6 17.4 %all_to_all.20.parts_ref = bf16[32,8,256]{2,1,0:T(8,128)(2,1)S(1)} all-to-all(bf16[32,8,256]{2,1,0:T(8,128)(2,1)S(1)} %bitcast.5), channel_id=1, replica_groups={{0,2,4,6,8,10,12,14,16,18,20,22,24,26,28,30,32,34,36,38,40,42,44,46,48,..., dimensions={0} | all-to-all | bytes 262144 | tf_op jit(solution)/shard_map/all_to_all | solution.py:394
  39.0 13.9 %all_to_all.21 = bf16[32,8,256]{2,1,0:T(8,128)(2,1)S(1)} all-to-all(bf16[32,8,256]{2,1,0:T(8,128)(2,1)S(1)} %shard_map.70), channel_id=1, replica_groups={{0,2,4,6,8,10,12,14,16,18,20,22,24,26,28,30,32,34,36,38,40,42,44,46,48,..., dimensions={0} | all-to-all | bytes 262144 | tf_op jit(solution)/shard_map/all_to_all | solution.py:394
  53.0 1.3 collective-permute-done.3.other_ref
  54.3 1.3 shard_map.71
  55.7 1.7 %collective-permute-start.4 = (bf16[512,256]{1,0:T(8,128)(2,1)S(1)}, bf16[512,256]{1,0:T(8,128)(2,1)S(1)}, u32[]{:S(2)}, u32[]{:S(2)}) collective-permute-start(bf16[512,256]{1,0:T(8,128)(2,1)S(1)} %get-tuple-element.31), channel_id=1, source_target_pairs={{0,64},{64,128},{128,192},{192,0},{1,65},{65,129},{129,193},{193,1... | collective-permute-start | bytes 786440 | tf_op jit(solution)/shard_map/ppermute | solution.py:375
  57.3 1.7 %collective-permute-start.8 = (bf16[512,256]{1,0:T(8,128)(2,1)S(1)}, bf16[512,256]{1,0:T(8,128)(2,1)S(1)}, u32[]{:S(2)}, u32[]{:S(2)}) collective-permute-start(bf16[512,256]{1,0:T(8,128)(2,1)S(1)} %get-tuple-element.36), channel_id=1, source_target_pairs={{0,192},{64,0},{128,64},{192,128},{1,193},{65,1},{129,65},{193,129... | collective-permute-start | bytes 786440 | tf_op jit(solution)/shard_map/ppermute | solution.py:375
  59.0 1.8 %collective-permute-start.6 = (bf16[512,256]{1,0:T(8,128)(2,1)S(1)}, bf16[512,256]{1,0:T(8,128)(2,1)S(1)}, u32[]{:S(2)}, u32[]{:S(2)}) collective-permute-start(bf16[512,256]{1,0:T(8,128)(2,1)S(1)} %get-tuple-element.32), channel_id=1, source_target_pairs={{0,192},{64,0},{128,64},{192,128},{1,193},{65,1},{129,65},{193,129... | collective-permute-start | bytes 786440 | tf_op jit(solution)/shard_map/ppermute | solution.py:375
  60.8 4.6 %collective-permute-done.4 = bf16[512,256]{1,0:T(8,128)(2,1)S(1)} collective-permute-done((bf16[512,256]{1,0:T(8,128)(2,1)S(1)}, bf16[512,256]{1,0:T(8,128)(2,1)S(1)}, u32[]{:S(2)}, u32[]{:S(2)}) %collective-permute-start.4) | collective-permute-done | bytes 262176 | tf_op jit(solution)/shard_map/ppermute | solution.py:375
  65.4 0.4 collective-permute-start.5
  65.8 1.6 collective-permute-start.7
  67.5 2.2 %collective-permute-start.9 = (bf16[512,256]{1,0:T(8,128)(2,1)S(1)}, bf16[512,256]{1,0:T(8,128)(2,1)S(1)}, u32[]{:S(2)}, u32[]{:S(2)}) collective-permute-start(bf16[512,256]{1,0:T(8,128)(2,1)S(1)} %add_convert_fusion.1), channel_id=1, source_target_pairs={{0,192},{64,0},{128,64},{192,128},{1,193},{65,1},{129,65},{193,129... | collective-permute-start | bytes 786440 | tf_op jit(solution)/shard_map/ppermute | solution.py:375
  69.7 2.4 %collective-permute-done.6 = bf16[512,256]{1,0:T(8,128)(2,1)S(1)} collective-permute-done((bf16[512,256]{1,0:T(8,128)(2,1)S(1)}, bf16[512,256]{1,0:T(8,128)(2,1)S(1)}, u32[]{:S(2)}, u32[]{:S(2)}) %collective-permute-start.6) | collective-permute-done | bytes 262176 | tf_op jit(solution)/shard_map/ppermute | solution.py:375
  72.1 3.8 %collective-permute-done.5 = bf16[512,256]{1,0:T(8,128)(2,1)S(1)} collective-permute-done((bf16[512,256]{1,0:T(8,128)(2,1)S(1)}, bf16[512,256]{1,0:T(8,128)(2,1)S(1)}, u32[]{:S(2)}, u32[]{:S(2)}) %collective-permute-start.5) | collective-permute-done | bytes 262176 | tf_op jit(solution)/shard_map/ppermute | solution.py:375
  75.9 0.1 add_convert_fusion.2.refs_0_
  76.0 0.1 collective-permute-start.12
  76.1 5.4 %collective-permute-done.7 = bf16[512,256]{1,0:T(8,128)(2,1)S(1)} collective-permute-done((bf16[512,256]{1,0:T(8,128)(2,1)S(1)}, bf16[512,256]{1,0:T(8,128)(2,1)S(1)}, u32[]{:S(2)}, u32[]{:S(2)}) %collective-permute-start.7) | collective-permute-done | bytes 262176 | tf_op jit(solution)/shard_map/ppermute | solution.py:375
  81.5 0.1 add_convert_fusion.refs_1_
  81.6 0.6 collective-permute-start.11
  82.2 0.7 collective-permute-start.10
  83.0 1.3 collective-permute-start.15
  84.3 2.9 %collective-permute-done.12.refs_6_ = bf16[512,256]{1,0:T(8,128)(2,1)S(1)} collective-permute-done((bf16[512,256]{1,0:T(8,128)(2,1)S(1)}, bf16[512,256]{1,0:T(8,128)(2,1)S(1)}, u32[]{:S(2)}, u32[]{:S(2)}) %collective-permute-start.12) | collective-permute-done | bytes 262176 | tf_op jit(solution)/shard_map/ppermute | solution.py:375
  87.1 3.7 %collective-permute-done.11.refs_3_ = bf16[512,256]{1,0:T(8,128)(2,1)S(1)} collective-permute-done((bf16[512,256]{1,0:T(8,128)(2,1)S(1)}, bf16[512,256]{1,0:T(8,128)(2,1)S(1)}, u32[]{:S(2)}, u32[]{:S(2)}) %collective-permute-start.11) | collective-permute-done | bytes 262176 | tf_op jit(solution)/shard_map/ppermute | solution.py:375
  90.9 0.8 collective-permute-start.14
  91.7 3.6 %collective-permute-done.10.refs_2_ = bf16[512,256]{1,0:T(8,128)(2,1)S(1)} collective-permute-done((bf16[512,256]{1,0:T(8,128)(2,1)S(1)}, bf16[512,256]{1,0:T(8,128)(2,1)S(1)}, u32[]{:S(2)}, u32[]{:S(2)}) %collective-permute-start.10) | collective-permute-done | bytes 262176 | tf_op jit(solution)/shard_map/ppermute | solution.py:375
  95.2 1.5 collective-permute-done.13.refs_4_
  96.8 1.3 collective-permute-done.14.refs_5_
  98.0 1.9 %shard_map.72 = (bf16[4096,256]{1,0:T(8,128)(2,1)S(1)}, bf16[512,256]{1,0:T(8,128)(2,1)S(1)}, bf16[512,256]{1,0:T(8,128)(2,1)S(1)}, bf16[1024,256]{1,0:T(8,128)(2,1)S(1)}) custom-call(bf16[8,512,512]{2,1,0:T(8,128)(2,1)S(1)} %get-tuple-element.26.full_ref, bf16[512,256]{1,0:T(8,128)(2,1)S(1)} %add_convert_fusion.2.refs_0_, ...), custom_call_target="tpu_custom_call" | custom-call | flops 1073741824 | tf_op jit(solution)/shard_map/pallas_call | solution.py:27
  100.0 0.1 collective-permute-start.16
  100.1 1.9 %collective-permute-done.16.come_ref = bf16[1024,256]{1,0:T(8,128)(2,1)S(1)} collective-permute-done((bf16[1024,256]{1,0:T(8,128)(2,1)S(1)}, bf16[1024,256]{1,0:T(8,128)(2,1)S(1)}, u32[]{:S(2)}, u32[]{:S(2)}) %collective-permute-start.16) | collective-permute-done | bytes 524320 | tf_op jit(solution)/shard_map/ppermute | solution.py:389
  102.1 16.2 %all_to_all.22.parts_ref = bf16[32,16,256]{2,1,0:T(8,128)(2,1)S(1)} all-to-all(bf16[32,16,256]{2,1,0:T(8,128)(2,1)S(1)} %shard_map.73), channel_id=1, replica_groups={{0,2,4,6,8,10,12,14,16,18,20,22,24,26,28,30,32,34,36,38,40,42,44,46,48,..., dimensions={0} | all-to-all | bytes 524288 | tf_op jit(solution)/shard_map/all_to_all | solution.py:394
  118.3 16.2 %all_to_all.23.mine_ref = bf16[32,16,256]{2,1,0:T(8,128)(2,1)S(1)} all-to-all(bf16[32,16,256]{2,1,0:T(8,128)(2,1)S(1)} %shard_map.74), channel_id=1, replica_groups={{0,2,4,6,8,10,12,14,16,18,20,22,24,26,28,30,32,34,36,38,40,42,44,46,48,..., dimensions={0} | all-to-all | bytes 524288 | tf_op jit(solution)/shard_map/all_to_all | solution.py:394
  134.5 3.4 %collective-permute-start.18 = (bf16[512,256]{1,0:T(8,128)(2,1)S(1)}, bf16[512,256]{1,0:T(8,128)(2,1)S(1)}, u32[]{:S(2)}, u32[]{:S(2)}) collective-permute-start(bf16[512,256]{1,0:T(8,128)(2,1)S(1)} %get-tuple-element.41), channel_id=1, source_target_pairs={{1,2},{2,1},{3,4},{4,3},{5,6},{6,5},{7,8},{8,7},{9,10},{10,9},{11,... | collective-permute-start | bytes 786440 | tf_op jit(solution)/shard_map/ppermute | solution.py:381
  137.9 0.4 shard_map.75
  138.4 0.6 collective-permute-start.21
  139.0 1.6 %collective-permute-start.20 = (bf16[320,128]{1,0:T(8,128)(2,1)S(1)}, bf16[320,128]{1,0:T(8,128)(2,1)S(1)}, u32[]{:S(2)}, u32[]{:S(2)}) collective-permute-start(bf16[320,128]{1,0:T(8,128)(2,1)S(1)} %get-tuple-element.44.refs_0_), channel_id=1, source_target_pairs={{0,192},{64,0},{128,64},{192,128},{1,193},{65,1},{129,65},{193,129... | collective-permute-start | bytes 245768 | tf_op jit(solution)/shard_map/ppermute | solution.py:375
  140.6 0.4 collective-permute-start.19
  141.0 3.2 %collective-permute-done.18.neighbor_ref = bf16[512,256]{1,0:T(8,128)(2,1)S(1)} collective-permute-done((bf16[512,256]{1,0:T(8,128)(2,1)S(1)}, bf16[512,256]{1,0:T(8,128)(2,1)S(1)}, u32[]{:S(2)}, u32[]{:S(2)}) %collective-permute-start.18) | collective-permute-done | bytes 262176 | tf_op jit(solution)/shard_map/ppermute | solution.py:381
  144.3 9.5 %shard_map.76 = (bf16[256,256]{1,0:T(8,128)(2,1)S(1)}, bf16[4096,256]{1,0:T(8,128)(2,1)S(1)}) custom-call(f32[256,256]{1,0:T(8,128)S(1)} %get-tuple-element.39.gram_ref, s32[2,32]{1,0:T(2,128)S(1)} %bitcast.8, bf16[32,3,128,128]{3,2,1,0:T(8,128)(2,1)S(1)} %copy-done.2, bf16[4096,256]{1,0:T(8,128)(2,1)S(1)} %get-tuple-element.40.sample_ref, ...), custom_call_target="tpu_custom_call" | custom-call | flops 17179869184 | tf_op jit(solution)/shard_map/pallas_call | solution.py:27
  153.8 3.6 %final.1 = (bf16[4096,256]{1,0:T(8,128)(2,1)}, bf16[4096,256]{1,0:T(8,128)(2,1)}, f32[256,256]{1,0:T(8,128)}) custom-call(bf16[256,256]{1,0:T(8,128)(2,1)S(1)} %get-tuple-element.42.inv_ref.rows_ref, bf16[256,256]{1,0:T(8,128)(2,1)S(1)} %get-tuple-element.42.inv_ref.rows_ref, bf16[4096,256]{1,0:T(8,128)(2,1)S(1)} %get-tuple-element.40.sample_ref, ...), custom_call_target="tpu_custom_call" | custom-call | tf_op jit(solution)/shard_map/final/pallas_call | solution.py:529
  (25 shorter events, 0.4 us)
Async XLA Ops:
  0.6 0.7 copy-start.3
  1.3 10.8 %copy-start.1 = (bf16[512,4096]{1,0:T(8,128)(2,1)S(1)}, bf16[512,4096]{1,0:T(8,128)(2,1)}, u32[]{:S(2)}) copy-start(bf16[512,4096]{1,0:T(8,128)(2,1)} %jac_ref.3) | copy-start | bytes 12582916
  1.3 10.8 %copy-start.2 = (bf16[32,3,128,128]{3,2,1,0:T(8,128)(2,1)S(1)}, bf16[32,3,128,128]{3,2,1,0:T(8,128)(2,1)}, u32[]{:S(2)}) copy-start(bf16[32,3,128,128]{3,2,1,0:T(8,128)(2,1)} %coef_ref.5) | copy-start | bytes 9437188
  4.2 15.0 %collective-permute-start = (bf16[512,512]{1,0:T(8,128)(2,1)S(1)}, bf16[512,512]{1,0:T(8,128)(2,1)S(1)}, u32[]{:S(2)}, u32[]{:S(2)}) collective-permute-start(bf16[512,512]{1,0:T(8,128)(2,1)S(1)} %get-tuple-element.24), channel_id=1, source_target_pairs={{0,1},{1,0},{2,3},{3,2},{4,5},{5,4},{6,7},{7,6},{8,9},{9,8},{10,11... | collective-permute-start | bytes 1572872 | tf_op jit(solution)/shard_map/ppermute | solution.py:389
  4.3 13.9 %copy-start = (bf16[4096,256]{1,0:T(8,128)(2,1)S(1)}, bf16[4096,256]{1,0:T(8,128)(2,1)}, u32[]{:S(2)}) copy-start(bf16[4096,256]{1,0:T(8,128)(2,1)} %probe_ref.3) | copy-start | bytes 6291460
  4.3 14.9 %collective-permute-start.1 = (bf16[512,512]{1,0:T(8,128)(2,1)S(1)}, bf16[512,512]{1,0:T(8,128)(2,1)S(1)}, u32[]{:S(2)}, u32[]{:S(2)}) collective-permute-start(bf16[512,512]{1,0:T(8,128)(2,1)S(1)} %get-tuple-element.25), channel_id=1, source_target_pairs={{1,2},{2,1},{3,4},{4,3},{5,6},{6,5},{7,8},{8,7},{9,10},{10,9},{11,... | collective-permute-start | bytes 1572872 | tf_op jit(solution)/shard_map/ppermute | solution.py:381
  20.2 1.4 collective-permute-start.2
  53.0 1.3 collective-permute-start.3
  55.7 9.7 %collective-permute-start.4 = (bf16[512,256]{1,0:T(8,128)(2,1)S(1)}, bf16[512,256]{1,0:T(8,128)(2,1)S(1)}, u32[]{:S(2)}, u32[]{:S(2)}) collective-permute-start(bf16[512,256]{1,0:T(8,128)(2,1)S(1)} %get-tuple-element.31), channel_id=1, source_target_pairs={{0,64},{64,128},{128,192},{192,0},{1,65},{65,129},{129,193},{193,1... | collective-permute-start | bytes 786440 | tf_op jit(solution)/shard_map/ppermute | solution.py:375
  57.3 10.1 %collective-permute-start.8 = (bf16[512,256]{1,0:T(8,128)(2,1)S(1)}, bf16[512,256]{1,0:T(8,128)(2,1)S(1)}, u32[]{:S(2)}, u32[]{:S(2)}) collective-permute-start(bf16[512,256]{1,0:T(8,128)(2,1)S(1)} %get-tuple-element.36), channel_id=1, source_target_pairs={{0,192},{64,0},{128,64},{192,128},{1,193},{65,1},{129,65},{193,129... | collective-permute-start | bytes 786440 | tf_op jit(solution)/shard_map/ppermute | solution.py:375
  59.0 13.1 %collective-permute-start.6 = (bf16[512,256]{1,0:T(8,128)(2,1)S(1)}, bf16[512,256]{1,0:T(8,128)(2,1)S(1)}, u32[]{:S(2)}, u32[]{:S(2)}) collective-permute-start(bf16[512,256]{1,0:T(8,128)(2,1)S(1)} %get-tuple-element.32), channel_id=1, source_target_pairs={{0,192},{64,0},{128,64},{192,128},{1,193},{65,1},{129,65},{193,129... | collective-permute-start | bytes 786440 | tf_op jit(solution)/shard_map/ppermute | solution.py:375
  65.4 10.5 %collective-permute-start.5 = (bf16[512,256]{1,0:T(8,128)(2,1)S(1)}, bf16[512,256]{1,0:T(8,128)(2,1)S(1)}, u32[]{:S(2)}, u32[]{:S(2)}) collective-permute-start(bf16[512,256]{1,0:T(8,128)(2,1)S(1)} %add_convert_fusion.3), channel_id=1, source_target_pairs={{0,64},{64,128},{128,192},{192,0},{1,65},{65,129},{129,193},{193,1... | collective-permute-start | bytes 786440 | tf_op jit(solution)/shard_map/ppermute | solution.py:375
  65.8 15.7 %collective-permute-start.7 = (bf16[512,256]{1,0:T(8,128)(2,1)S(1)}, bf16[512,256]{1,0:T(8,128)(2,1)S(1)}, u32[]{:S(2)}, u32[]{:S(2)}) collective-permute-start(bf16[512,256]{1,0:T(8,128)(2,1)S(1)} %get-tuple-element.34), channel_id=1, source_target_pairs={{0,64},{64,128},{128,192},{192,0},{1,65},{65,129},{129,193},{193,1... | collective-permute-start | bytes 786440 | tf_op jit(solution)/shard_map/ppermute | solution.py:375
  67.5 14.1 %collective-permute-start.9 = (bf16[512,256]{1,0:T(8,128)(2,1)S(1)}, bf16[512,256]{1,0:T(8,128)(2,1)S(1)}, u32[]{:S(2)}, u32[]{:S(2)}) collective-permute-start(bf16[512,256]{1,0:T(8,128)(2,1)S(1)} %add_convert_fusion.1), channel_id=1, source_target_pairs={{0,192},{64,0},{128,64},{192,128},{1,193},{65,1},{129,65},{193,129... | collective-permute-start | bytes 786440 | tf_op jit(solution)/shard_map/ppermute | solution.py:375
  76.0 11.1 %collective-permute-start.12 = (bf16[512,256]{1,0:T(8,128)(2,1)S(1)}, bf16[512,256]{1,0:T(8,128)(2,1)S(1)}, u32[]{:S(2)}, u32[]{:S(2)}) collective-permute-start(bf16[512,256]{1,0:T(8,128)(2,1)S(1)} %add_convert_fusion.2.refs_0_), channel_id=1, source_target_pairs={{0,64},{64,128},{128,192},{192,0},{1,65},{65,129},{129,193},{193,1... | collective-permute-start | bytes 786440 | tf_op jit(solution)/shard_map/ppermute | solution.py:375
  81.6 9.3 %collective-permute-start.11 = (bf16[512,256]{1,0:T(8,128)(2,1)S(1)}, bf16[512,256]{1,0:T(8,128)(2,1)S(1)}, u32[]{:S(2)}, u32[]{:S(2)}) collective-permute-start(bf16[512,256]{1,0:T(8,128)(2,1)S(1)} %add_convert_fusion.refs_1_), channel_id=1, source_target_pairs={{0,192},{64,0},{128,64},{192,128},{1,193},{65,1},{129,65},{193,129... | collective-permute-start | bytes 786440 | tf_op jit(solution)/shard_map/ppermute | solution.py:375
  82.2 13.0 %collective-permute-start.10 = (bf16[512,256]{1,0:T(8,128)(2,1)S(1)}, bf16[512,256]{1,0:T(8,128)(2,1)S(1)}, u32[]{:S(2)}, u32[]{:S(2)}) collective-permute-start(bf16[512,256]{1,0:T(8,128)(2,1)S(1)} %add_convert_fusion.2.refs_0_), channel_id=1, source_target_pairs={{0,192},{64,0},{128,64},{192,128},{1,193},{65,1},{129,65},{193,129... | collective-permute-start | bytes 786440 | tf_op jit(solution)/shard_map/ppermute | solution.py:375
  83.0 12.3 %collective-permute-start.15 = (bf16[512,256]{1,0:T(8,128)(2,1)S(1)}, bf16[512,256]{1,0:T(8,128)(2,1)S(1)}, u32[]{:S(2)}, u32[]{:S(2)}) collective-permute-start(bf16[512,256]{1,0:T(8,128)(2,1)S(1)} %add_convert_fusion.refs_1_), channel_id=1, source_target_pairs={{0,64},{64,128},{128,192},{192,0},{1,65},{65,129},{129,193},{193,1... | collective-permute-start | bytes 786440 | tf_op jit(solution)/shard_map/ppermute | solution.py:375
  87.1 9.6 %collective-permute-start.13 = (bf16[512,256]{1,0:T(8,128)(2,1)S(1)}, bf16[512,256]{1,0:T(8,128)(2,1)S(1)}, u32[]{:S(2)}, u32[]{:S(2)}) collective-permute-start(bf16[512,256]{1,0:T(8,128)(2,1)S(1)} %collective-permute-done.12.refs_6_), channel_id=1, source_target_pairs={{0,64},{64,128},{128,192},{192,0},{1,65},{65,129},{129,193},{193,1... | collective-permute-start | bytes 786440 | tf_op jit(solution)/shard_map/ppermute | solution.py:375
  90.9 7.2 %collective-permute-start.14 = (bf16[512,256]{1,0:T(8,128)(2,1)S(1)}, bf16[512,256]{1,0:T(8,128)(2,1)S(1)}, u32[]{:S(2)}, u32[]{:S(2)}) collective-permute-start(bf16[512,256]{1,0:T(8,128)(2,1)S(1)} %collective-permute-done.11.refs_3_), channel_id=1, source_target_pairs={{0,192},{64,0},{128,64},{192,128},{1,193},{65,1},{129,65},{193,129... | collective-permute-start | bytes 786440 | tf_op jit(solution)/shard_map/ppermute | solution.py:375
  100.0 2.0 %collective-permute-start.16 = (bf16[1024,256]{1,0:T(8,128)(2,1)S(1)}, bf16[1024,256]{1,0:T(8,128)(2,1)S(1)}, u32[]{:S(2)}, u32[]{:S(2)}) collective-permute-start(bf16[1024,256]{1,0:T(8,128)(2,1)S(1)} %get-tuple-element.38), channel_id=1, source_target_pairs={{0,1},{1,0},{2,3},{3,2},{4,5},{5,4},{6,7},{7,6},{8,9},{9,8},{10,11... | collective-permute-start | bytes 1572872 | tf_op jit(solution)/shard_map/ppermute | solution.py:389
  134.5 3.4 %collective-permute-start.17 = (bf16[32,16,256]{2,1,0:T(8,128)(2,1)S(1)}, bf16[32,16,256]{2,1,0:T(8,128)(2,1)S(1)}, u32[]{:S(2)}, u32[]{:S(2)}) collective-permute-start(bf16[32,16,256]{2,1,0:T(8,128)(2,1)S(1)} %all_to_all.23.mine_ref), channel_id=1, source_target_pairs={{0,1},{1,0},{2,3},{3,2},{4,5},{5,4},{6,7},{7,6},{8,9},{9,8},{10,11... | collective-permute-start | bytes 786440 | tf_op jit(solution)/shard_map/ppermute | solution.py:389
  134.5 9.8 %collective-permute-start.18 = (bf16[512,256]{1,0:T(8,128)(2,1)S(1)}, bf16[512,256]{1,0:T(8,128)(2,1)S(1)}, u32[]{:S(2)}, u32[]{:S(2)}) collective-permute-start(bf16[512,256]{1,0:T(8,128)(2,1)S(1)} %get-tuple-element.41), channel_id=1, source_target_pairs={{1,2},{2,1},{3,4},{4,3},{5,6},{6,5},{7,8},{8,7},{9,10},{10,9},{11,... | collective-permute-start | bytes 786440 | tf_op jit(solution)/shard_map/ppermute | solution.py:381
  138.4 15.5 %collective-permute-start.21 = (bf16[320,128]{1,0:T(8,128)(2,1)S(1)}, bf16[320,128]{1,0:T(8,128)(2,1)S(1)}, u32[]{:S(2)}, u32[]{:S(2)}) collective-permute-start(bf16[320,128]{1,0:T(8,128)(2,1)S(1)} %get-tuple-element.44.refs_0_), channel_id=1, source_target_pairs={{0,128},{64,192},{128,0},{192,64},{1,129},{65,193},{129,1},{193,65... | collective-permute-start | bytes 245768 | tf_op jit(solution)/shard_map/ppermute | solution.py:375
  139.0 14.8 %collective-permute-start.20 = (bf16[320,128]{1,0:T(8,128)(2,1)S(1)}, bf16[320,128]{1,0:T(8,128)(2,1)S(1)}, u32[]{:S(2)}, u32[]{:S(2)}) collective-permute-start(bf16[320,128]{1,0:T(8,128)(2,1)S(1)} %get-tuple-element.44.refs_0_), channel_id=1, source_target_pairs={{0,192},{64,0},{128,64},{192,128},{1,193},{65,1},{129,65},{193,129... | collective-permute-start | bytes 245768 | tf_op jit(solution)/shard_map/ppermute | solution.py:375
  140.6 13.2 %collective-permute-start.19 = (bf16[320,128]{1,0:T(8,128)(2,1)S(1)}, bf16[320,128]{1,0:T(8,128)(2,1)S(1)}, u32[]{:S(2)}, u32[]{:S(2)}) collective-permute-start(bf16[320,128]{1,0:T(8,128)(2,1)S(1)} %get-tuple-element.44.refs_0_), channel_id=1, source_target_pairs={{0,64},{64,128},{128,192},{192,0},{1,65},{65,129},{129,193},{193,1... | collective-permute-start | bytes 245768 | tf_op jit(solution)/shard_map/ppermute | solution.py:375

commit v5 on v4

--- a/solution.py
+++ b/solution.py
@@ -131,6 +131,15 @@
     out_ref[...] = (keep_ref[...].astype(F32) + come_ref[...].astype(F32)).astype(BF16)
 
 
+def add_kernel(start, count, *refs):
+    rows = refs[-1].shape[0]
+    cut = slice(start, start + rows)
+    total = sum(ref[cut].astype(F32) for ref in refs[:count])
+    for ref in refs[count:-1]:
+        total += ref[...].astype(F32)
+    refs[-1][...] = total.astype(BF16)
+
+
 def total_kernel(parts_ref, out_ref):
     total = parts_ref[0].astype(F32)
     for i in range(1, parts_ref.shape[0]):
@@ -175,28 +184,46 @@
         out[rows, :] = part[...]
 
 
+def half_of(role):
+    core = core_index()
+    return role + core - 2 * role * core
+
+
 def sample_kernel(ranks, full_ref, mine_ref, other_ref, *refs):
     outs, fwd = refs[:-1], refs[-1]
     in_order(mine_ref, other_ref, fwd)
     for rel in range(ranks):
         owner = lax.rem(lax.axis_index("obs") + rel, ranks)
         for half in range(2):
-            outs[2 * rel + half][...] = dot_tn(full_ref[2 * owner + half], fwd[...]).astype(BF16)
+            outs[2 * rel + half][...] = dot_tn(full_ref[2 * owner + half_of(half)], fwd[...]).astype(BF16)
+
+
+def pick_kernel(ranks, *refs):
+    pieces, out_ref = refs[:-1], refs[-1]
+    rel = lax.rem(core_index() * (ranks - 1) + ranks - lax.axis_index("obs"), ranks)
+    for i in range(ranks):
+
+        @pl.when(rel == i)
+        def _():
+            rows = pieces[2 * i].shape[0]
+            out_ref[:rows] = pieces[2 * i][...]
+            out_ref[rows:] = pieces[2 * i + 1][...]
 
 
 def project_kernel(ranks, full_ref, *refs):
-    pieces = refs[: 2 * ranks]
-    sample_ref, neighbor_ref, keep_ref, give_ref, acc, gram = refs[2 * ranks :]
-    rows = pieces[0].shape[0]
+    pieces = refs[: 3 * ranks]
+    sample_ref, keep_ref, give_ref, acc, gram = refs[3 * ranks :]
+    rows = pieces[2].shape[0]
     total = jnp.zeros(acc.shape, F32)
     square = jnp.zeros(gram.shape, F32)
     for rel in range(ranks):
         owner = lax.rem(lax.axis_index("obs") + rel, ranks)
         for half in range(2):
-            piece = pieces[2 * rel + half][...]
-            start = pl.multiple_of(owner * (2 * rows) + half * rows, rows)
-            sample_ref[pl.ds(start, rows), :] = piece
-            total += dot(full_ref[2 * owner + half], piece)
+            parts = pieces[3 * rel : 3 * rel + 2] if half == 0 else pieces[3 * rel + 2 : 3 * rel + 3]
+            piece = jnp.concatenate([part[...] for part in parts], axis=0)
+            chunk = 2 * owner + half_of(half)
+            sample_ref[pl.ds(pl.multiple_of(chunk * rows, rows), rows), :] = piece
+            total += dot(full_ref[chunk], piece)
             square += dot_tn(piece, piece)
     acc[...] = total
     gram[...] = square
@@ -207,7 +234,6 @@
         out_ref[rows : 2 * rows, :BLK], out_ref[rows : 2 * rows, BLK:] = split(gram[:, mine])
     core = core_index()
     last = sample_ref.shape[0] - EDGE
-    neighbor_ref[...] = sample_ref[pl.ds(pl.multiple_of(core * last, EDGE), EDGE), :]
     give_ref[2 * rows :] = sample_ref[pl.ds(pl.multiple_of((1 - core) * last, EDGE), EDGE), :]
 
 
@@ -381,10 +407,6 @@
     return lax.ppermute(value, "par", pairs)
 
 
-def added(*values):
-    return sum(v.astype(F32) for v in values).astype(BF16)
-
-
 def swapped(value):
     return lax.ppermute(value, "par", [(i, i ^ 1) for i in range(lax.axis_size("par"))])
 
@@ -471,27 +493,35 @@
     def ring(value, by):
         return shifted(value, "obs", by)
 
+    def add(start, rows, whole, parts=()):
+        kernel = functools.partial(add_kernel, start, len(whole))
+        return call(kernel, shape(rows, width), [VMEM] * (len(whole) + len(parts)), [*whole, *parts], mib=4)
+
     via_left = ring(far0, 1)
     via_right = ring(far1, -1)
-    a1 = ring(right1, 1)
-    b0 = ring(left0, -1)
-    a0 = ring(added(right0, via_left), 1)
-    b1 = ring(added(left1, via_right), -1)
-    sum0 = added(here0, a0, b0)
-    sum1 = added(here1, a1, b1)
-
-    l0 = ring(sum0, 1)
+    own_up = ring(right1, 1)
+    own_down = ring(left0, -1)
+    rows = EDGE // 2
+    sums_up = [ring(add(i * rows, rows, [right0, via_left]), 1) for i in range(2)]
+    sum_down = ring(add(0, EDGE, [left1, via_right]), -1)
+    sums0 = [add(i * rows, rows, [here0, own_down], [sums_up[i]]) for i in range(2)]
+    sum1 = add(0, EDGE, [here1, own_up, sum_down])
+    l0 = [ring(sums0[i], 1) for i in range(2)]
+    r0 = [ring(sums0[i], -1) for i in range(2)]
+    f0 = [ring(l0[i], 1) for i in range(2)]
+    l1 = ring(sum1, 1)
     r1 = ring(sum1, -1)
-    l1 = ring(sum1, 1)
-    r0 = ring(sum0, -1)
-    f0 = ring(l0, 1)
     f1 = ring(r1, -1)
 
-    sample, neighbor, keep, give = call(
+    neighbor = call(
+        functools.partial(pick_kernel, ranks), shape(EDGE, width), [VMEM] * (2 * ranks), [*sums0, *r0, *f0, *l0], mib=4
+    )
+    from_neighbor = to_neighbor(neighbor)
+    sample, keep, give = call(
         functools.partial(project_kernel, ranks),
-        [shape(npar, width), shape(EDGE, width), shape(nobs, width), shape(nobs + EDGE, width)],
-        [VMEM] * (1 + 2 * ranks),
-        [full, sum0, sum1, r0, r1, f0, f1, l0, l1],
+        [shape(npar, width), shape(nobs, width), shape(nobs + EDGE, width)],
+        [VMEM] * (1 + 3 * ranks),
+        [full, *sums0, sum1, *r0, r1, *f0, f1, *l0, l1],
         [pltpu.VMEM((nobs, width), F32), pltpu.VMEM((width, width), F32)],
         mib=16,
         flops=flops,
@@ -502,7 +532,6 @@
     total = call(total_gram_kernel, both, [VMEM], [exchanged(part)], mib=4)
     mine = exchanged(total)
     other = swapped(mine)
-    from_neighbor = to_neighbor(neighbor)
     gram, second = call(
         moments_kernel,
         [shape(width, width, dtype=F32), shape(5 * NB, 2 * NB)],

time: 159 us -> 165 us (1.038)
  starting transfers between devices: 26.9 us -> 36.8 us
  waiting for transfers between devices: 37.1 us -> 32.9 us
    ppermute x15 -> x19, starting transfers between devices: 15.5 us -> 25.1 us  [shifted(): lax.ppermute(value, axis, [(i, (i + by) % count) for i in range(count)])]
    ppermute x15 -> x19, waiting for transfers between devices: 29.3 us -> 24.8 us  [shifted(): lax.ppermute(value, axis, [(i, (i + by) % count) for i in range(count)])]
    pallas_call x10 -> x17, Pallas kernels: 20.6 us -> 20.9 us  [call(): pl.pallas_call(kernel, out_shape=outs, in_specs=specs, out_specs=jax.tree...]
  transfers between devices with their start and end apart: 22 -> 26, of which waited for: 13 -> 13; matrix products, arithmetic and copies ran while one was open for 0% -> 0% of each run, Pallas kernels for 11% -> 11%
where the time goes in v5:
time: 165 us; the launch traced here: 163 us
  blocking collectives  63.6 us (39%)
  starting transfers between devices  36.8 us (22%)
  waiting for transfers between devices  32.9 us (20%)
  Pallas kernels  28.3 us (17%)
    all_to_all x4, blocking collectives, exchanged(): lax.all_to_all(parts, 'par', 0, 0, axis_index_groups=groups, tiled=True)  63.6 us
    ppermute x19, starting transfers between devices, shifted(): lax.ppermute(value, axis, [(i, (i + by) % count) for i in range(count)])  25.1 us
    ppermute x19, waiting for transfers between devices, shifted(): lax.ppermute(value, axis, [(i, (i + by) % count) for i in range(count)])  24.8 us
    pallas_call x17, Pallas kernels, call(): pl.pallas_call(kernel, out_shape=outs, in_specs=specs, out_specs=jax.tree...  20.9 us
    ppermute x2, starting transfers between devices, to_neighbor(): return lax.ppermute(value, 'par', pairs)  11.4 us
    ppermute x5, waiting for transfers between devices, swapped(): lax.ppermute(value, 'par', [(i, i ^ 1) for i in range(lax.axis_size('par'...  4.58 us
    pallas_call x1, Pallas kernels, body(): pl.pallas_call(functools.partial(final_kernel, 1.0 / (nobs * ranks)), nam...  3.55 us
    ppermute x2, waiting for transfers between devices, to_neighbor(): return lax.ppermute(value, 'par', pairs)  3.5 us
  transfers between devices with their start and end apart: 26, of which 13 were waited for; matrix products, arithmetic and copies ran while one was open for 0% of the time, Pallas kernels for 11%

profile of v5, /device:TPU:6, one launch (start us, length us, event | category | flops | bytes accessed | tf_op | source)
XLA Modules:
  0.0 163.2 jit_solution(14400808233322567913)
XLA Ops:
  0.6 0.7 copy-done.3
  1.3 2.9 %edges.1 = (bf16[512,512]{1,0:T(8,128)(2,1)S(1)}, bf16[512,512]{1,0:T(8,128)(2,1)S(1)}) custom-call(s32[2,32]{1,0:T(2,128)S(1)} %bitcast.6, bf16[512,4096]{1,0:T(8,128)(2,1)} %jac_ref.3, bf16[32,3,128,128]{3,2,1,0:T(8,128)(2,1)} %coef_ref.5), custom_call_target="tpu_custom_call" | custom-call | flops 268435456 | tf_op jit(solution)/shard_map/edges/pallas_call | solution.py:431
  4.2 0.1 collective-permute-start
  4.3 7.8 %collective-permute-start.1 = (bf16[512,512]{1,0:T(8,128)(2,1)S(1)}, bf16[512,512]{1,0:T(8,128)(2,1)S(1)}, u32[]{:S(2)}, u32[]{:S(2)}) collective-permute-start(bf16[512,512]{1,0:T(8,128)(2,1)S(1)} %get-tuple-element.24), channel_id=1, source_target_pairs={{1,2},{2,1},{3,4},{4,3},{5,6},{6,5},{7,8},{8,7},{9,10},{10,9},{11,... | collective-permute-start | bytes 1572872 | tf_op jit(solution)/shard_map/ppermute | solution.py:407
  12.1 6.1 %shard_map.67.own_ref = bf16[8,512,512]{2,1,0:T(8,128)(2,1)S(1)} custom-call(s32[2,32]{1,0:T(2,128)S(1)} %bitcast.7, bf16[512,4096]{1,0:T(8,128)(2,1)S(1)} %copy-done.1, bf16[32,3,128,128]{3,2,1,0:T(8,128)(2,1)S(1)} %copy-done.2), custom_call_target="tpu_custom_call" | custom-call | flops 4294967296 | tf_op jit(solution)/shard_map/pallas_call | solution.py:27
  18.3 1.0 shard_map.68.inner_ref
  19.3 0.9 forward.1
  20.2 0.1 collective-permute-start.2
  20.3 1.3 collective-permute-done.2.come_ref
  21.6 17.4 %all_to_all.20.parts_ref = bf16[32,8,256]{2,1,0:T(8,128)(2,1)S(1)} all-to-all(bf16[32,8,256]{2,1,0:T(8,128)(2,1)S(1)} %bitcast.5), channel_id=1, replica_groups={{0,2,4,6,8,10,12,14,16,18,20,22,24,26,28,30,32,34,36,38,40,42,44,46,48,..., dimensions={0} | all-to-all | bytes 262144 | tf_op jit(solution)/shard_map/all_to_all | solution.py:416
  39.0 13.9 %all_to_all.21 = bf16[32,8,256]{2,1,0:T(8,128)(2,1)S(1)} all-to-all(bf16[32,8,256]{2,1,0:T(8,128)(2,1)S(1)} %shard_map.70), channel_id=1, replica_groups={{0,2,4,6,8,10,12,14,16,18,20,22,24,26,28,30,32,34,36,38,40,42,44,46,48,..., dimensions={0} | all-to-all | bytes 262144 | tf_op jit(solution)/shard_map/all_to_all | solution.py:416
  53.0 1.3 collective-permute-done.3.other_ref
  54.3 1.3 shard_map.71
  55.7 3.1 %collective-permute-start.9 = (bf16[512,256]{1,0:T(8,128)(2,1)S(1)}, bf16[512,256]{1,0:T(8,128)(2,1)S(1)}, u32[]{:S(2)}, u32[]{:S(2)}) collective-permute-start(bf16[512,256]{1,0:T(8,128)(2,1)S(1)} %get-tuple-element.35), channel_id=1, source_target_pairs={{0,192},{64,0},{128,64},{192,128},{1,193},{65,1},{129,65},{193,129... | collective-permute-start | bytes 786440 | tf_op jit(solution)/shard_map/ppermute | solution.py:401
  58.8 5.9 %collective-permute-done.9.refs_1_ = bf16[512,256]{1,0:T(8,128)(2,1)S(1)} collective-permute-done((bf16[512,256]{1,0:T(8,128)(2,1)S(1)}, bf16[512,256]{1,0:T(8,128)(2,1)S(1)}, u32[]{:S(2)}, u32[]{:S(2)}) %collective-permute-start.9) | collective-permute-done | bytes 262176 | tf_op jit(solution)/shard_map/ppermute | solution.py:401
  64.7 3.8 %collective-permute-start.10 = (bf16[512,256]{1,0:T(8,128)(2,1)S(1)}, bf16[512,256]{1,0:T(8,128)(2,1)S(1)}, u32[]{:S(2)}, u32[]{:S(2)}) collective-permute-start(bf16[512,256]{1,0:T(8,128)(2,1)S(1)} %shard_map.76), channel_id=1, source_target_pairs={{0,192},{64,0},{128,64},{192,128},{1,193},{65,1},{129,65},{193,129... | collective-permute-start | bytes 786440 | tf_op jit(solution)/shard_map/ppermute | solution.py:401
  68.5 3.2 %collective-permute-start.4 = (bf16[512,256]{1,0:T(8,128)(2,1)S(1)}, bf16[512,256]{1,0:T(8,128)(2,1)S(1)}, u32[]{:S(2)}, u32[]{:S(2)}) collective-permute-start(bf16[512,256]{1,0:T(8,128)(2,1)S(1)} %get-tuple-element.29), channel_id=1, source_target_pairs={{0,192},{64,0},{128,64},{192,128},{1,193},{65,1},{129,65},{193,129... | collective-permute-start | bytes 786440 | tf_op jit(solution)/shard_map/ppermute | solution.py:401
  71.7 3.5 %collective-permute-done.10.refs_2_ = bf16[512,256]{1,0:T(8,128)(2,1)S(1)} collective-permute-done((bf16[512,256]{1,0:T(8,128)(2,1)S(1)}, bf16[512,256]{1,0:T(8,128)(2,1)S(1)}, u32[]{:S(2)}, u32[]{:S(2)}) %collective-permute-start.10) | collective-permute-done | bytes 262176 | tf_op jit(solution)/shard_map/ppermute | solution.py:401
  75.2 0.1 shard_map.77.refs_2_
  75.3 4.0 %collective-permute-start.13 = (bf16[512,256]{1,0:T(8,128)(2,1)S(1)}, bf16[512,256]{1,0:T(8,128)(2,1)S(1)}, u32[]{:S(2)}, u32[]{:S(2)}) collective-permute-start(bf16[512,256]{1,0:T(8,128)(2,1)S(1)} %shard_map.77.refs_2_), channel_id=1, source_target_pairs={{0,192},{64,0},{128,64},{192,128},{1,193},{65,1},{129,65},{193,129... | collective-permute-start | bytes 786440 | tf_op jit(solution)/shard_map/ppermute | solution.py:401
  79.3 0.1 collective-permute-start.6
  79.4 0.1 collective-permute-start.7
  79.5 1.3 collective-permute-done.4.refs_1_
  80.8 5.5 %collective-permute-done.6.refs_2_ = bf16[256,256]{1,0:T(8,128)(2,1)S(1)} collective-permute-done((bf16[256,256]{1,0:T(8,128)(2,1)S(1)}, bf16[256,256]{1,0:T(8,128)(2,1)S(1)}, u32[]{:S(2)}, u32[]{:S(2)}) %collective-permute-start.6) | collective-permute-done | bytes 131104 | tf_op jit(solution)/shard_map/ppermute | solution.py:401
  86.3 0.1 collective-permute-start.14
  86.4 3.2 %collective-permute-start.11 = (bf16[256,256]{1,0:T(8,128)(2,1)S(1)}, bf16[256,256]{1,0:T(8,128)(2,1)S(1)}, u32[]{:S(2)}, u32[]{:S(2)}) collective-permute-start(bf16[256,256]{1,0:T(8,128)(2,1)S(1)} %shard_map.73.refs_0_), channel_id=1, source_target_pairs={{0,192},{64,0},{128,64},{192,128},{1,193},{65,1},{129,65},{193,129... | collective-permute-start | bytes 393224 | tf_op jit(solution)/shard_map/ppermute | solution.py:401
  89.8 0.1 collective-permute-start.19
  89.9 3.2 %collective-permute-start.18 = (bf16[512,256]{1,0:T(8,128)(2,1)S(1)}, bf16[512,256]{1,0:T(8,128)(2,1)S(1)}, u32[]{:S(2)}, u32[]{:S(2)}) collective-permute-start(bf16[512,256]{1,0:T(8,128)(2,1)S(1)} %collective-permute-done.13.refs_5_), channel_id=1, source_target_pairs={{0,192},{64,0},{128,64},{192,128},{1,193},{65,1},{129,65},{193,129... | collective-permute-start | bytes 786440 | tf_op jit(solution)/shard_map/ppermute | solution.py:401
  93.1 0.9 collective-permute-done.14.refs_9_.refs_6_
  94.0 1.1 collective-permute-start.12
  95.0 1.0 collective-permute-start.15
  96.0 1.3 collective-permute-done.16.refs_10_.refs_7_
  97.3 1.6 collective-permute-done.12.refs_4_.refs_3_
  98.9 3.4 %collective-permute-done.15.refs_6_.refs_4_ = bf16[256,256]{1,0:T(8,128)(2,1)S(1)} collective-permute-done((bf16[256,256]{1,0:T(8,128)(2,1)S(1)}, bf16[256,256]{1,0:T(8,128)(2,1)S(1)}, u32[]{:S(2)}, u32[]{:S(2)}) %collective-permute-start.15) | collective-permute-done | bytes 131104 | tf_op jit(solution)/shard_map/ppermute | solution.py:401
  102.4 1.4 collective-permute-done.17.refs_7_.refs_5_
  103.8 2.0 %shard_map.78 = (bf16[4096,256]{1,0:T(8,128)(2,1)S(1)}, bf16[512,256]{1,0:T(8,128)(2,1)S(1)}, bf16[1024,256]{1,0:T(8,128)(2,1)S(1)}) custom-call(bf16[8,512,512]{2,1,0:T(8,128)(2,1)S(1)} %get-tuple-element.25.full_ref, bf16[256,256]{1,0:T(8,128)(2,1)S(1)} %shard_map.73.refs_0_, bf16[256,256]{1,0:T(8,128)(2,1)S(1)} %shard_map.75.refs_1_, ...), custom_call_target="tpu_custom_call" | custom-call | flops 1073741824 | tf_op jit(solution)/shard_map/pallas_call | solution.py:27
  105.8 0.1 collective-permute-start.20
  105.9 1.9 %collective-permute-done.20.come_ref = bf16[1024,256]{1,0:T(8,128)(2,1)S(1)} collective-permute-done((bf16[1024,256]{1,0:T(8,128)(2,1)S(1)}, bf16[1024,256]{1,0:T(8,128)(2,1)S(1)}, u32[]{:S(2)}, u32[]{:S(2)}) %collective-permute-start.20) | collective-permute-done | bytes 524320 | tf_op jit(solution)/shard_map/ppermute | solution.py:411
  107.8 16.2 %all_to_all.22.parts_ref = bf16[32,16,256]{2,1,0:T(8,128)(2,1)S(1)} all-to-all(bf16[32,16,256]{2,1,0:T(8,128)(2,1)S(1)} %shard_map.79), channel_id=1, replica_groups={{0,2,4,6,8,10,12,14,16,18,20,22,24,26,28,30,32,34,36,38,40,42,44,46,48,..., dimensions={0} | all-to-all | bytes 524288 | tf_op jit(solution)/shard_map/all_to_all | solution.py:416
  124.1 16.2 %all_to_all.23.mine_ref = bf16[32,16,256]{2,1,0:T(8,128)(2,1)S(1)} all-to-all(bf16[32,16,256]{2,1,0:T(8,128)(2,1)S(1)} %shard_map.80), channel_id=1, replica_groups={{0,2,4,6,8,10,12,14,16,18,20,22,24,26,28,30,32,34,36,38,40,42,44,46,48,..., dimensions={0} | all-to-all | bytes 524288 | tf_op jit(solution)/shard_map/all_to_all | solution.py:416
  140.3 3.7 %collective-permute-start.22 = (bf16[512,256]{1,0:T(8,128)(2,1)S(1)}, bf16[512,256]{1,0:T(8,128)(2,1)S(1)}, u32[]{:S(2)}, u32[]{:S(2)}) collective-permute-start(bf16[512,256]{1,0:T(8,128)(2,1)S(1)} %shard_map.82), channel_id=1, source_target_pairs={{1,2},{2,1},{3,4},{4,3},{5,6},{6,5},{7,8},{8,7},{9,10},{10,9},{11,... | collective-permute-start | bytes 786440 | tf_op jit(solution)/shard_map/ppermute | solution.py:407
  143.9 0.4 shard_map.81
  144.4 0.1 collective-permute-start.25
  144.5 1.5 collective-permute-start.24
  145.9 0.6 collective-permute-start.23
  146.6 3.5 %collective-permute-done.22.neighbor_ref = bf16[512,256]{1,0:T(8,128)(2,1)S(1)} collective-permute-done((bf16[512,256]{1,0:T(8,128)(2,1)S(1)}, bf16[512,256]{1,0:T(8,128)(2,1)S(1)}, u32[]{:S(2)}, u32[]{:S(2)}) %collective-permute-start.22) | collective-permute-done | bytes 262176 | tf_op jit(solution)/shard_map/ppermute | solution.py:407
  150.1 9.5 %shard_map.83 = (bf16[256,256]{1,0:T(8,128)(2,1)S(1)}, bf16[4096,256]{1,0:T(8,128)(2,1)S(1)}) custom-call(f32[256,256]{1,0:T(8,128)S(1)} %get-tuple-element.38.gram_ref, s32[2,32]{1,0:T(2,128)S(1)} %bitcast.8, bf16[32,3,128,128]{3,2,1,0:T(8,128)(2,1)S(1)} %copy-done.2, bf16[4096,256]{1,0:T(8,128)(2,1)S(1)} %get-tuple-element.39.sample_ref, ...), custom_call_target="tpu_custom_call" | custom-call | flops 17179869184 | tf_op jit(solution)/shard_map/pallas_call | solution.py:27
  159.6 3.6 %final.1 = (bf16[4096,256]{1,0:T(8,128)(2,1)}, bf16[4096,256]{1,0:T(8,128)(2,1)}, f32[256,256]{1,0:T(8,128)}) custom-call(bf16[256,256]{1,0:T(8,128)(2,1)S(1)} %get-tuple-element.40.inv_ref.rows_ref, bf16[256,256]{1,0:T(8,128)(2,1)S(1)} %get-tuple-element.40.inv_ref.rows_ref, bf16[4096,256]{1,0:T(8,128)(2,1)S(1)} %get-tuple-element.39.sample_ref, ...), custom_call_target="tpu_custom_call" | custom-call | tf_op jit(solution)/shard_map/final/pallas_call | solution.py:558
  (36 shorter events, 0.6 us)
Async XLA Ops:
  0.6 0.7 copy-start.3
  1.3 10.8 %copy-start.1 = (bf16[512,4096]{1,0:T(8,128)(2,1)S(1)}, bf16[512,4096]{1,0:T(8,128)(2,1)}, u32[]{:S(2)}) copy-start(bf16[512,4096]{1,0:T(8,128)(2,1)} %jac_ref.3) | copy-start | bytes 12582916
  1.3 10.8 %copy-start.2 = (bf16[32,3,128,128]{3,2,1,0:T(8,128)(2,1)S(1)}, bf16[32,3,128,128]{3,2,1,0:T(8,128)(2,1)}, u32[]{:S(2)}) copy-start(bf16[32,3,128,128]{3,2,1,0:T(8,128)(2,1)} %coef_ref.5) | copy-start | bytes 9437188
  4.2 15.0 %collective-permute-start = (bf16[512,512]{1,0:T(8,128)(2,1)S(1)}, bf16[512,512]{1,0:T(8,128)(2,1)S(1)}, u32[]{:S(2)}, u32[]{:S(2)}) collective-permute-start(bf16[512,512]{1,0:T(8,128)(2,1)S(1)} %get-tuple-element.23), channel_id=1, source_target_pairs={{0,1},{1,0},{2,3},{3,2},{4,5},{5,4},{6,7},{7,6},{8,9},{9,8},{10,11... | collective-permute-start | bytes 1572872 | tf_op jit(solution)/shard_map/ppermute | solution.py:411
  4.3 13.9 %copy-start = (bf16[4096,256]{1,0:T(8,128)(2,1)S(1)}, bf16[4096,256]{1,0:T(8,128)(2,1)}, u32[]{:S(2)}) copy-start(bf16[4096,256]{1,0:T(8,128)(2,1)} %probe_ref.3) | copy-start | bytes 6291460
  4.3 14.9 %collective-permute-start.1 = (bf16[512,512]{1,0:T(8,128)(2,1)S(1)}, bf16[512,512]{1,0:T(8,128)(2,1)S(1)}, u32[]{:S(2)}, u32[]{:S(2)}) collective-permute-start(bf16[512,512]{1,0:T(8,128)(2,1)S(1)} %get-tuple-element.24), channel_id=1, source_target_pairs={{1,2},{2,1},{3,4},{4,3},{5,6},{6,5},{7,8},{8,7},{9,10},{10,9},{11,... | collective-permute-start | bytes 1572872 | tf_op jit(solution)/shard_map/ppermute | solution.py:407
  20.2 1.4 collective-permute-start.2
  53.0 1.3 collective-permute-start.3
  55.7 9.0 %collective-permute-start.9 = (bf16[512,256]{1,0:T(8,128)(2,1)S(1)}, bf16[512,256]{1,0:T(8,128)(2,1)S(1)}, u32[]{:S(2)}, u32[]{:S(2)}) collective-permute-start(bf16[512,256]{1,0:T(8,128)(2,1)S(1)} %get-tuple-element.35), channel_id=1, source_target_pairs={{0,192},{64,0},{128,64},{192,128},{1,193},{65,1},{129,65},{193,129... | collective-permute-start | bytes 786440 | tf_op jit(solution)/shard_map/ppermute | solution.py:401
  58.8 13.0 %collective-permute-start.8 = (bf16[512,256]{1,0:T(8,128)(2,1)S(1)}, bf16[512,256]{1,0:T(8,128)(2,1)S(1)}, u32[]{:S(2)}, u32[]{:S(2)}) collective-permute-start(bf16[512,256]{1,0:T(8,128)(2,1)S(1)} %get-tuple-element.33), channel_id=1, source_target_pairs={{0,64},{64,128},{128,192},{192,0},{1,65},{65,129},{129,193},{193,1... | collective-permute-start | bytes 786440 | tf_op jit(solution)/shard_map/ppermute | solution.py:401
  64.7 10.5 %collective-permute-start.10 = (bf16[512,256]{1,0:T(8,128)(2,1)S(1)}, bf16[512,256]{1,0:T(8,128)(2,1)S(1)}, u32[]{:S(2)}, u32[]{:S(2)}) collective-permute-start(bf16[512,256]{1,0:T(8,128)(2,1)S(1)} %shard_map.76), channel_id=1, source_target_pairs={{0,192},{64,0},{128,64},{192,128},{1,193},{65,1},{129,65},{193,129... | collective-permute-start | bytes 786440 | tf_op jit(solution)/shard_map/ppermute | solution.py:401
  68.5 10.7 %collective-permute-start.5 = (bf16[512,256]{1,0:T(8,128)(2,1)S(1)}, bf16[512,256]{1,0:T(8,128)(2,1)S(1)}, u32[]{:S(2)}, u32[]{:S(2)}) collective-permute-start(bf16[512,256]{1,0:T(8,128)(2,1)S(1)} %get-tuple-element.31), channel_id=1, source_target_pairs={{0,64},{64,128},{128,192},{192,0},{1,65},{65,129},{129,193},{193,1... | collective-permute-start | bytes 786440 | tf_op jit(solution)/shard_map/ppermute | solution.py:401
  68.5 12.3 %collective-permute-start.4 = (bf16[512,256]{1,0:T(8,128)(2,1)S(1)}, bf16[512,256]{1,0:T(8,128)(2,1)S(1)}, u32[]{:S(2)}, u32[]{:S(2)}) collective-permute-start(bf16[512,256]{1,0:T(8,128)(2,1)S(1)} %get-tuple-element.29), channel_id=1, source_target_pairs={{0,192},{64,0},{128,64},{192,128},{1,193},{65,1},{129,65},{193,129... | collective-permute-start | bytes 786440 | tf_op jit(solution)/shard_map/ppermute | solution.py:401
  75.3 14.6 %collective-permute-start.13 = (bf16[512,256]{1,0:T(8,128)(2,1)S(1)}, bf16[512,256]{1,0:T(8,128)(2,1)S(1)}, u32[]{:S(2)}, u32[]{:S(2)}) collective-permute-start(bf16[512,256]{1,0:T(8,128)(2,1)S(1)} %shard_map.77.refs_2_), channel_id=1, source_target_pairs={{0,192},{64,0},{128,64},{192,128},{1,193},{65,1},{129,65},{193,129... | collective-permute-start | bytes 786440 | tf_op jit(solution)/shard_map/ppermute | solution.py:401
  79.3 7.0 %collective-permute-start.6 = (bf16[256,256]{1,0:T(8,128)(2,1)S(1)}, bf16[256,256]{1,0:T(8,128)(2,1)S(1)}, u32[]{:S(2)}, u32[]{:S(2)}) collective-permute-start(bf16[256,256]{1,0:T(8,128)(2,1)S(1)} %shard_map.72), channel_id=1, source_target_pairs={{0,64},{64,128},{128,192},{192,0},{1,65},{65,129},{129,193},{193,1... | collective-permute-start | bytes 393224 | tf_op jit(solution)/shard_map/ppermute | solution.py:401
  79.4 10.2 %collective-permute-start.7 = (bf16[256,256]{1,0:T(8,128)(2,1)S(1)}, bf16[256,256]{1,0:T(8,128)(2,1)S(1)}, u32[]{:S(2)}, u32[]{:S(2)}) collective-permute-start(bf16[256,256]{1,0:T(8,128)(2,1)S(1)} %shard_map.74), channel_id=1, source_target_pairs={{0,64},{64,128},{128,192},{192,0},{1,65},{65,129},{129,193},{193,1... | collective-permute-start | bytes 393224 | tf_op jit(solution)/shard_map/ppermute | solution.py:401
  86.3 7.7 %collective-permute-start.14 = (bf16[256,256]{1,0:T(8,128)(2,1)S(1)}, bf16[256,256]{1,0:T(8,128)(2,1)S(1)}, u32[]{:S(2)}, u32[]{:S(2)}) collective-permute-start(bf16[256,256]{1,0:T(8,128)(2,1)S(1)} %shard_map.73.refs_0_), channel_id=1, source_target_pairs={{0,64},{64,128},{128,192},{192,0},{1,65},{65,129},{129,193},{193,1... | collective-permute-start | bytes 393224 | tf_op jit(solution)/shard_map/ppermute | solution.py:401
  86.4 8.6 %collective-permute-start.11 = (bf16[256,256]{1,0:T(8,128)(2,1)S(1)}, bf16[256,256]{1,0:T(8,128)(2,1)S(1)}, u32[]{:S(2)}, u32[]{:S(2)}) collective-permute-start(bf16[256,256]{1,0:T(8,128)(2,1)S(1)} %shard_map.73.refs_0_), channel_id=1, source_target_pairs={{0,192},{64,0},{128,64},{192,128},{1,193},{65,1},{129,65},{193,129... | collective-permute-start | bytes 393224 | tf_op jit(solution)/shard_map/ppermute | solution.py:401
  89.7 7.7 %collective-permute-start.16 = (bf16[256,256]{1,0:T(8,128)(2,1)S(1)}, bf16[256,256]{1,0:T(8,128)(2,1)S(1)}, u32[]{:S(2)}, u32[]{:S(2)}) collective-permute-start(bf16[256,256]{1,0:T(8,128)(2,1)S(1)} %shard_map.75.refs_1_), channel_id=1, source_target_pairs={{0,64},{64,128},{128,192},{192,0},{1,65},{65,129},{129,193},{193,1... | collective-permute-start | bytes 393224 | tf_op jit(solution)/shard_map/ppermute | solution.py:401
  89.8 14.0 %collective-permute-start.19 = (bf16[512,256]{1,0:T(8,128)(2,1)S(1)}, bf16[512,256]{1,0:T(8,128)(2,1)S(1)}, u32[]{:S(2)}, u32[]{:S(2)}) collective-permute-start(bf16[512,256]{1,0:T(8,128)(2,1)S(1)} %shard_map.77.refs_2_), channel_id=1, source_target_pairs={{0,64},{64,128},{128,192},{192,0},{1,65},{65,129},{129,193},{193,1... | collective-permute-start | bytes 786440 | tf_op jit(solution)/shard_map/ppermute | solution.py:401
  89.9 13.9 %collective-permute-start.18 = (bf16[512,256]{1,0:T(8,128)(2,1)S(1)}, bf16[512,256]{1,0:T(8,128)(2,1)S(1)}, u32[]{:S(2)}, u32[]{:S(2)}) collective-permute-start(bf16[512,256]{1,0:T(8,128)(2,1)S(1)} %collective-permute-done.13.refs_5_), channel_id=1, source_target_pairs={{0,192},{64,0},{128,64},{192,128},{1,193},{65,1},{129,65},{193,129... | collective-permute-start | bytes 786440 | tf_op jit(solution)/shard_map/ppermute | solution.py:401
  94.0 5.0 %collective-permute-start.12 = (bf16[256,256]{1,0:T(8,128)(2,1)S(1)}, bf16[256,256]{1,0:T(8,128)(2,1)S(1)}, u32[]{:S(2)}, u32[]{:S(2)}) collective-permute-start(bf16[256,256]{1,0:T(8,128)(2,1)S(1)} %shard_map.75.refs_1_), channel_id=1, source_target_pairs={{0,192},{64,0},{128,64},{192,128},{1,193},{65,1},{129,65},{193,129... | collective-permute-start | bytes 393224 | tf_op jit(solution)/shard_map/ppermute | solution.py:401
  95.0 7.3 %collective-permute-start.15 = (bf16[256,256]{1,0:T(8,128)(2,1)S(1)}, bf16[256,256]{1,0:T(8,128)(2,1)S(1)}, u32[]{:S(2)}, u32[]{:S(2)}) collective-permute-start(bf16[256,256]{1,0:T(8,128)(2,1)S(1)} %collective-permute-done.14.refs_9_.refs_6_), channel_id=1, source_target_pairs={{0,64},{64,128},{128,192},{192,0},{1,65},{65,129},{129,193},{193,1... | collective-permute-start | bytes 393224 | tf_op jit(solution)/shard_map/ppermute | solution.py:401
  97.3 6.4 %collective-permute-start.17 = (bf16[256,256]{1,0:T(8,128)(2,1)S(1)}, bf16[256,256]{1,0:T(8,128)(2,1)S(1)}, u32[]{:S(2)}, u32[]{:S(2)}) collective-permute-start(bf16[256,256]{1,0:T(8,128)(2,1)S(1)} %collective-permute-done.16.refs_10_.refs_7_), channel_id=1, source_target_pairs={{0,64},{64,128},{128,192},{192,0},{1,65},{65,129},{129,193},{193,1... | collective-permute-start | bytes 393224 | tf_op jit(solution)/shard_map/ppermute | solution.py:401
  105.8 2.0 %collective-permute-start.20 = (bf16[1024,256]{1,0:T(8,128)(2,1)S(1)}, bf16[1024,256]{1,0:T(8,128)(2,1)S(1)}, u32[]{:S(2)}, u32[]{:S(2)}) collective-permute-start(bf16[1024,256]{1,0:T(8,128)(2,1)S(1)} %get-tuple-element.37), channel_id=1, source_target_pairs={{0,1},{1,0},{2,3},{3,2},{4,5},{5,4},{6,7},{7,6},{8,9},{9,8},{10,11... | collective-permute-start | bytes 1572872 | tf_op jit(solution)/shard_map/ppermute | solution.py:411
  140.2 3.7 %collective-permute-start.21 = (bf16[32,16,256]{2,1,0:T(8,128)(2,1)S(1)}, bf16[32,16,256]{2,1,0:T(8,128)(2,1)S(1)}, u32[]{:S(2)}, u32[]{:S(2)}) collective-permute-start(bf16[32,16,256]{2,1,0:T(8,128)(2,1)S(1)} %all_to_all.23.mine_ref), channel_id=1, source_target_pairs={{0,1},{1,0},{2,3},{3,2},{4,5},{5,4},{6,7},{7,6},{8,9},{9,8},{10,11... | collective-permute-start | bytes 786440 | tf_op jit(solution)/shard_map/ppermute | solution.py:411
  140.3 9.8 %collective-permute-start.22 = (bf16[512,256]{1,0:T(8,128)(2,1)S(1)}, bf16[512,256]{1,0:T(8,128)(2,1)S(1)}, u32[]{:S(2)}, u32[]{:S(2)}) collective-permute-start(bf16[512,256]{1,0:T(8,128)(2,1)S(1)} %shard_map.82), channel_id=1, source_target_pairs={{1,2},{2,1},{3,4},{4,3},{5,6},{6,5},{7,8},{8,7},{9,10},{10,9},{11,... | collective-permute-start | bytes 786440 | tf_op jit(solution)/shard_map/ppermute | solution.py:407
  144.4 15.2 %collective-permute-start.25 = (bf16[320,128]{1,0:T(8,128)(2,1)S(1)}, bf16[320,128]{1,0:T(8,128)(2,1)S(1)}, u32[]{:S(2)}, u32[]{:S(2)}) collective-permute-start(bf16[320,128]{1,0:T(8,128)(2,1)S(1)} %get-tuple-element.42.refs_0_), channel_id=1, source_target_pairs={{0,128},{64,192},{128,0},{192,64},{1,129},{65,193},{129,1},{193,65... | collective-permute-start | bytes 245768 | tf_op jit(solution)/shard_map/ppermute | solution.py:401
  144.5 15.2 %collective-permute-start.24 = (bf16[320,128]{1,0:T(8,128)(2,1)S(1)}, bf16[320,128]{1,0:T(8,128)(2,1)S(1)}, u32[]{:S(2)}, u32[]{:S(2)}) collective-permute-start(bf16[320,128]{1,0:T(8,128)(2,1)S(1)} %get-tuple-element.42.refs_0_), channel_id=1, source_target_pairs={{0,192},{64,0},{128,64},{192,128},{1,193},{65,1},{129,65},{193,129... | collective-permute-start | bytes 245768 | tf_op jit(solution)/shard_map/ppermute | solution.py:401
  145.9 13.7 %collective-permute-start.23 = (bf16[320,128]{1,0:T(8,128)(2,1)S(1)}, bf16[320,128]{1,0:T(8,128)(2,1)S(1)}, u32[]{:S(2)}, u32[]{:S(2)}) collective-permute-start(bf16[320,128]{1,0:T(8,128)(2,1)S(1)} %get-tuple-element.42.refs_0_), channel_id=1, source_target_pairs={{0,64},{64,128},{128,192},{192,0},{1,65},{65,129},{129,193},{193,1... | collective-permute-start | bytes 245768 | tf_op jit(solution)/shard_map/ppermute | solution.py:401

commit v6 on v5

--- a/solution.py
+++ b/solution.py
@@ -210,7 +210,7 @@
             out_ref[rows:] = pieces[2 * i + 1][...]
 
 
-def project_kernel(ranks, full_ref, *refs):
+def project_kernel(ranks, full_ref, passed_ref, *refs):
     pieces = refs[: 3 * ranks]
     sample_ref, keep_ref, give_ref, acc, gram = refs[3 * ranks :]
     rows = pieces[2].shape[0]
@@ -234,7 +234,8 @@
         out_ref[rows : 2 * rows, :BLK], out_ref[rows : 2 * rows, BLK:] = split(gram[:, mine])
     core = core_index()
     last = sample_ref.shape[0] - EDGE
-    give_ref[2 * rows :] = sample_ref[pl.ds(pl.multiple_of((1 - core) * last, EDGE), EDGE), :]
+    give_ref[2 * rows + EDGE :] = passed_ref[...]
+    give_ref[2 * rows : 2 * rows + EDGE] = sample_ref[pl.ds(pl.multiple_of((1 - core) * last, EDGE), EDGE), :]
 
 
 def prior_block(block, off_ref, coefs, ext, base):
@@ -250,8 +251,10 @@
     core = core_index()
     ext[EDGE : 3 * EDGE] = sample_ref[: 2 * EDGE]
     ext[3 * EDGE : 5 * EDGE] = sample_ref[rows - 2 * EDGE :]
-    ext[pl.ds(pl.multiple_of((1 - core) * (5 * EDGE), EDGE), EDGE)] = come_ref[come_ref.shape[0] - EDGE :]
-    ext[pl.ds(pl.multiple_of(core * (5 * EDGE), EDGE), EDGE)] = neighbor_ref[...]
+    near = come_ref.shape[0] - 2 * EDGE
+    ext[pl.ds(pl.multiple_of((1 - core) * (5 * EDGE), EDGE), EDGE)] = come_ref[near : near + EDGE]
+    far = jnp.where(core == 0, come_ref[near + EDGE :], neighbor_ref[...])
+    ext[pl.ds(pl.multiple_of(core * (5 * EDGE), EDGE), EDGE)] = far
 
 
 def packed(full):
@@ -516,12 +519,14 @@
     neighbor = call(
         functools.partial(pick_kernel, ranks), shape(EDGE, width), [VMEM] * (2 * ranks), [*sums0, *r0, *f0, *l0], mib=4
     )
-    from_neighbor = to_neighbor(neighbor)
+    cores = lax.axis_size("par")
+    passed = lax.ppermute(neighbor, "par", [(i, i + 2) for i in range(1, cores - 2, 2)])
+    from_neighbor = lax.ppermute(neighbor, "par", [(i, i - 1) for i in range(2, cores, 2)])
     sample, keep, give = call(
         functools.partial(project_kernel, ranks),
-        [shape(npar, width), shape(nobs, width), shape(nobs + EDGE, width)],
-        [VMEM] * (1 + 3 * ranks),
-        [full, *sums0, sum1, *r0, r1, *f0, f1, *l0, l1],
+        [shape(npar, width), shape(nobs, width), shape(nobs + 2 * EDGE, width)],
+        [VMEM] * (2 + 3 * ranks),
+        [full, passed, *sums0, sum1, *r0, r1, *f0, f1, *l0, l1],
         [pltpu.VMEM((nobs, width), F32), pltpu.VMEM((width, width), F32)],
         mib=16,
         flops=flops,
@@ -552,7 +557,7 @@
         mib=16,
         flops=16 * flops,
     )
-    steps = 4
+    steps = 2
     by_rows = pl.BlockSpec((npar // steps, width), lambda i: (i, 0))
     few = pl.BlockSpec((width // steps, width), lambda i: (i, 0))
     return pl.pallas_call(
@@ -562,7 +567,7 @@
         out_shape=[shape(npar, width), shape(npar, width), shape(width, width, dtype=F32)],
         in_specs=[whole(width, width), few, by_rows, by_rows] + [whole(*second.shape)] * len(seconds),
         out_specs=[by_rows, by_rows, few],
-        compiler_params=pltpu.CompilerParams(vmem_limit_bytes=12 * 2**20),
+        compiler_params=pltpu.CompilerParams(vmem_limit_bytes=16 * 2**20),
     )(inverse, inverse, sample, image, *seconds)
 
 

time: 165 us -> 164 us (level)
  starting transfers between devices: 36.8 us -> 33.2 us
  waiting for transfers between devices: 32.9 us -> 34.8 us
    ppermute x19, waiting for transfers between devices: 24.8 us -> 29.9 us  [shifted(): lax.ppermute(value, axis, [(i, (i + by) % count) for i in range(count)])]
    ppermute x0 -> x2, starting transfers between devices: none -> 4.12 us  [the longest x1 3.45 us: body(): lax.ppermute(neighbor, 'par', [(i, i - 1) for i in range(2, cores, 2)])]
    ppermute x19, starting transfers between devices: 25.1 us -> 21 us  [shifted(): lax.ppermute(value, axis, [(i, (i + by) % count) for i in range(count)])]
    ppermute x2 -> x1, starting transfers between devices: 11.4 us -> 7.76 us  [to_neighbor(): return lax.ppermute(value, 'par', pairs)]
    ppermute x2 -> x1, waiting for transfers between devices: 3.5 us -> 0.01 us  [to_neighbor(): return lax.ppermute(value, 'par', pairs)]
  transfers between devices with their start and end apart: 26 -> 27, of which waited for: 13 -> 14; matrix products, arithmetic and copies ran while one was open for 0% -> 0% of each run, Pallas kernels for 11% -> 11%
where the time goes in v6:
time: 164 us; the launch traced here: 162 us
  blocking collectives  64.1 us (39%)
  waiting for transfers between devices  34.8 us (21%)
  starting transfers between devices  33.2 us (20%)
  Pallas kernels  27.8 us (17%)
    all_to_all x4, blocking collectives, exchanged(): lax.all_to_all(parts, 'par', 0, 0, axis_index_groups=groups, tiled=True)  64.1 us
    ppermute x19, waiting for transfers between devices, shifted(): lax.ppermute(value, axis, [(i, (i + by) % count) for i in range(count)])  29.9 us
    ppermute x19, starting transfers between devices, shifted(): lax.ppermute(value, axis, [(i, (i + by) % count) for i in range(count)])  21 us
    pallas_call x17, Pallas kernels, call(): pl.pallas_call(kernel, out_shape=outs, in_specs=specs, out_specs=jax.tree...  21 us
    ppermute x1, starting transfers between devices, to_neighbor(): return lax.ppermute(value, 'par', pairs)  7.76 us
    ppermute x5, waiting for transfers between devices, swapped(): lax.ppermute(value, 'par', [(i, i ^ 1) for i in range(lax.axis_size('par'...  4.96 us
    ppermute x1, starting transfers between devices, body(): lax.ppermute(neighbor, 'par', [(i, i - 1) for i in range(2, cores, 2)])  3.45 us
  transfers between devices with their start and end apart: 27, of which 14 were waited for; matrix products, arithmetic and copies ran while one was open for 0% of the time, Pallas kernels for 11%

profile of v6, /device:TPU:6, one launch (start us, length us, event | category | flops | bytes accessed | tf_op | source)
XLA Modules:
  0.0 161.6 jit_solution(8332346043278375500)
XLA Ops:
  0.6 0.7 copy-done.3
  1.3 2.9 %edges.1 = (bf16[512,512]{1,0:T(8,128)(2,1)S(1)}, bf16[512,512]{1,0:T(8,128)(2,1)S(1)}) custom-call(s32[2,32]{1,0:T(2,128)S(1)} %bitcast.6, bf16[512,4096]{1,0:T(8,128)(2,1)} %jac_ref.3, bf16[32,3,128,128]{3,2,1,0:T(8,128)(2,1)} %coef_ref.5), custom_call_target="tpu_custom_call" | custom-call | flops 268435456 | tf_op jit(solution)/shard_map/edges/pallas_call | solution.py:434
  4.2 0.1 collective-permute-start
  4.3 7.8 %collective-permute-start.1 = (bf16[512,512]{1,0:T(8,128)(2,1)S(1)}, bf16[512,512]{1,0:T(8,128)(2,1)S(1)}, u32[]{:S(2)}, u32[]{:S(2)}) collective-permute-start(bf16[512,512]{1,0:T(8,128)(2,1)S(1)} %get-tuple-element.24), channel_id=1, source_target_pairs={{1,2},{2,1},{3,4},{4,3},{5,6},{6,5},{7,8},{8,7},{9,10},{10,9},{11,... | collective-permute-start | bytes 1572872 | tf_op jit(solution)/shard_map/ppermute | solution.py:410
  12.1 6.1 %shard_map.67.own_ref = bf16[8,512,512]{2,1,0:T(8,128)(2,1)S(1)} custom-call(s32[2,32]{1,0:T(2,128)S(1)} %bitcast.7, bf16[512,4096]{1,0:T(8,128)(2,1)S(1)} %copy-done.1, bf16[32,3,128,128]{3,2,1,0:T(8,128)(2,1)S(1)} %copy-done.2), custom_call_target="tpu_custom_call" | custom-call | flops 4294967296 | tf_op jit(solution)/shard_map/pallas_call | solution.py:27
  18.3 1.0 shard_map.68.inner_ref
  19.3 0.9 forward.1
  20.2 0.1 collective-permute-start.2
  20.3 1.3 collective-permute-done.2.come_ref
  21.6 17.4 %all_to_all.20.parts_ref = bf16[32,8,256]{2,1,0:T(8,128)(2,1)S(1)} all-to-all(bf16[32,8,256]{2,1,0:T(8,128)(2,1)S(1)} %bitcast.5), channel_id=1, replica_groups={{0,2,4,6,8,10,12,14,16,18,20,22,24,26,28,30,32,34,36,38,40,42,44,46,48,..., dimensions={0} | all-to-all | bytes 262144 | tf_op jit(solution)/shard_map/all_to_all | solution.py:419
  39.0 13.9 %all_to_all.21 = bf16[32,8,256]{2,1,0:T(8,128)(2,1)S(1)} all-to-all(bf16[32,8,256]{2,1,0:T(8,128)(2,1)S(1)} %shard_map.70), channel_id=1, replica_groups={{0,2,4,6,8,10,12,14,16,18,20,22,24,26,28,30,32,34,36,38,40,42,44,46,48,..., dimensions={0} | all-to-all | bytes 262144 | tf_op jit(solution)/shard_map/all_to_all | solution.py:419
  53.0 1.3 collective-permute-done.3.other_ref
  54.3 1.3 shard_map.71
  55.7 3.1 %collective-permute-start.16 = (bf16[512,256]{1,0:T(8,128)(2,1)S(1)}, bf16[512,256]{1,0:T(8,128)(2,1)S(1)}, u32[]{:S(2)}, u32[]{:S(2)}) collective-permute-start(bf16[512,256]{1,0:T(8,128)(2,1)S(1)} %get-tuple-element.35), channel_id=1, source_target_pairs={{0,192},{64,0},{128,64},{192,128},{1,193},{65,1},{129,65},{193,129... | collective-permute-start | bytes 786440 | tf_op jit(solution)/shard_map/ppermute | solution.py:404
  58.8 3.2 %collective-permute-start.4 = (bf16[512,256]{1,0:T(8,128)(2,1)S(1)}, bf16[512,256]{1,0:T(8,128)(2,1)S(1)}, u32[]{:S(2)}, u32[]{:S(2)}) collective-permute-start(bf16[512,256]{1,0:T(8,128)(2,1)S(1)} %get-tuple-element.29), channel_id=1, source_target_pairs={{0,192},{64,0},{128,64},{192,128},{1,193},{65,1},{129,65},{193,129... | collective-permute-start | bytes 786440 | tf_op jit(solution)/shard_map/ppermute | solution.py:404
  62.0 3.5 %collective-permute-done.16.refs_1_ = bf16[512,256]{1,0:T(8,128)(2,1)S(1)} collective-permute-done((bf16[512,256]{1,0:T(8,128)(2,1)S(1)}, bf16[512,256]{1,0:T(8,128)(2,1)S(1)}, u32[]{:S(2)}, u32[]{:S(2)}) %collective-permute-start.16) | collective-permute-done | bytes 262176 | tf_op jit(solution)/shard_map/ppermute | solution.py:404
  65.5 3.8 %collective-permute-start.17 = (bf16[512,256]{1,0:T(8,128)(2,1)S(1)}, bf16[512,256]{1,0:T(8,128)(2,1)S(1)}, u32[]{:S(2)}, u32[]{:S(2)}) collective-permute-start(bf16[512,256]{1,0:T(8,128)(2,1)S(1)} %shard_map.77), channel_id=1, source_target_pairs={{0,192},{64,0},{128,64},{192,128},{1,193},{65,1},{129,65},{193,129... | collective-permute-start | bytes 786440 | tf_op jit(solution)/shard_map/ppermute | solution.py:404
  69.3 0.3 collective-permute-start.6
  69.6 0.1 collective-permute-start.7
  69.7 1.3 collective-permute-done.4.refs_1_
  71.1 6.5 %collective-permute-done.6.refs_2_ = bf16[256,256]{1,0:T(8,128)(2,1)S(1)} collective-permute-done((bf16[256,256]{1,0:T(8,128)(2,1)S(1)}, bf16[256,256]{1,0:T(8,128)(2,1)S(1)}, u32[]{:S(2)}, u32[]{:S(2)}) %collective-permute-start.6) | collective-permute-done | bytes 131104 | tf_op jit(solution)/shard_map/ppermute | solution.py:404
  77.7 1.6 collective-permute-done.7.refs_2_
  79.4 0.1 shard_map.78.refs_2_
  79.6 3.3 %collective-permute-start.18 = (bf16[512,256]{1,0:T(8,128)(2,1)S(1)}, bf16[512,256]{1,0:T(8,128)(2,1)S(1)}, u32[]{:S(2)}, u32[]{:S(2)}) collective-permute-start(bf16[512,256]{1,0:T(8,128)(2,1)S(1)} %shard_map.78.refs_2_), channel_id=1, source_target_pairs={{0,192},{64,0},{128,64},{192,128},{1,193},{65,1},{129,65},{193,129... | collective-permute-start | bytes 786440 | tf_op jit(solution)/shard_map/ppermute | solution.py:404
  82.8 0.4 collective-permute-start.8
  83.3 0.1 collective-permute-start.9
  83.4 1.7 %collective-permute-done.10.refs_6_.refs_9_ = bf16[256,256]{1,0:T(8,128)(2,1)S(1)} collective-permute-done((bf16[256,256]{1,0:T(8,128)(2,1)S(1)}, bf16[256,256]{1,0:T(8,128)(2,1)S(1)}, u32[]{:S(2)}, u32[]{:S(2)}) %collective-permute-start.10) | collective-permute-done | bytes 131104 | tf_op jit(solution)/shard_map/ppermute | solution.py:404
  85.0 0.3 collective-permute-start.11
  85.3 2.3 %collective-permute-done.12.refs_7_.refs_10_ = bf16[256,256]{1,0:T(8,128)(2,1)S(1)} collective-permute-done((bf16[256,256]{1,0:T(8,128)(2,1)S(1)}, bf16[256,256]{1,0:T(8,128)(2,1)S(1)}, u32[]{:S(2)}, u32[]{:S(2)}) %collective-permute-start.12) | collective-permute-done | bytes 131104 | tf_op jit(solution)/shard_map/ppermute | solution.py:404
  87.6 3.9 %collective-permute-done.8.refs_2_.refs_3_ = bf16[256,256]{1,0:T(8,128)(2,1)S(1)} collective-permute-done((bf16[256,256]{1,0:T(8,128)(2,1)S(1)}, bf16[256,256]{1,0:T(8,128)(2,1)S(1)}, u32[]{:S(2)}, u32[]{:S(2)}) %collective-permute-start.8) | collective-permute-done | bytes 131104 | tf_op jit(solution)/shard_map/ppermute | solution.py:404
  91.5 1.4 collective-permute-done.9.refs_3_.refs_4_
  92.9 2.1 %collective-permute-done.13.refs_5_.refs_7_ = bf16[256,256]{1,0:T(8,128)(2,1)S(1)} collective-permute-done((bf16[256,256]{1,0:T(8,128)(2,1)S(1)}, bf16[256,256]{1,0:T(8,128)(2,1)S(1)}, u32[]{:S(2)}, u32[]{:S(2)}) %collective-permute-start.13) | collective-permute-done | bytes 131104 | tf_op jit(solution)/shard_map/ppermute | solution.py:404
  95.1 0.7 collective-permute-start.14
  95.8 1.6 %collective-permute-start.19 = (bf16[512,256]{1,0:T(8,128)(2,1)S(1)}, bf16[512,256]{1,0:T(8,128)(2,1)S(1)}, u32[]{:S(2)}, u32[]{:S(2)}) collective-permute-start(bf16[512,256]{1,0:T(8,128)(2,1)S(1)} %collective-permute-done.18.refs_5_), channel_id=1, source_target_pairs={{0,192},{64,0},{128,64},{192,128},{1,193},{65,1},{129,65},{193,129... | collective-permute-start | bytes 786440 | tf_op jit(solution)/shard_map/ppermute | solution.py:404
  97.4 2.1 %collective-permute-done.20.refs_11_ = bf16[512,256]{1,0:T(8,128)(2,1)S(1)} collective-permute-done((bf16[512,256]{1,0:T(8,128)(2,1)S(1)}, bf16[512,256]{1,0:T(8,128)(2,1)S(1)}, u32[]{:S(2)}, u32[]{:S(2)}) %collective-permute-start.20) | collective-permute-done | bytes 262176 | tf_op jit(solution)/shard_map/ppermute | solution.py:404
  99.6 3.5 %collective-permute-done.19.refs_8_ = bf16[512,256]{1,0:T(8,128)(2,1)S(1)} collective-permute-done((bf16[512,256]{1,0:T(8,128)(2,1)S(1)}, bf16[512,256]{1,0:T(8,128)(2,1)S(1)}, u32[]{:S(2)}, u32[]{:S(2)}) %collective-permute-start.19) | collective-permute-done | bytes 262176 | tf_op jit(solution)/shard_map/ppermute | solution.py:404
  103.0 2.0 %shard_map.79 = (bf16[4096,256]{1,0:T(8,128)(2,1)S(1)}, bf16[512,256]{1,0:T(8,128)(2,1)S(1)}, bf16[1536,256]{1,0:T(8,128)(2,1)S(1)}) custom-call(bf16[8,512,512]{2,1,0:T(8,128)(2,1)S(1)} %get-tuple-element.25.full_ref, bf16[512,256]{1,0:T(8,128)(2,1)S(1)} %collective-permute-done.14.passed_ref, bf16[256,256]{1,0:T(8,128)(2,1)S(1)} %shard_map.73.refs_0_, ...), custom_call_target="tpu_custom_call" | custom-call | flops 1073741824 | tf_op jit(solution)/shard_map/pallas_call | solution.py:27
  105.0 0.1 collective-permute-start.21
  105.1 2.3 %collective-permute-done.21.come_ref = bf16[1536,256]{1,0:T(8,128)(2,1)S(1)} collective-permute-done((bf16[1536,256]{1,0:T(8,128)(2,1)S(1)}, bf16[1536,256]{1,0:T(8,128)(2,1)S(1)}, u32[]{:S(2)}, u32[]{:S(2)}) %collective-permute-start.21) | collective-permute-done | bytes 786464 | tf_op jit(solution)/shard_map/ppermute | solution.py:414
  107.5 16.7 %all_to_all.22.parts_ref = bf16[32,16,256]{2,1,0:T(8,128)(2,1)S(1)} all-to-all(bf16[32,16,256]{2,1,0:T(8,128)(2,1)S(1)} %shard_map.80), channel_id=1, replica_groups={{0,2,4,6,8,10,12,14,16,18,20,22,24,26,28,30,32,34,36,38,40,42,44,46,48,..., dimensions={0} | all-to-all | bytes 524288 | tf_op jit(solution)/shard_map/all_to_all | solution.py:419
  124.2 16.2 %all_to_all.23.mine_ref = bf16[32,16,256]{2,1,0:T(8,128)(2,1)S(1)} all-to-all(bf16[32,16,256]{2,1,0:T(8,128)(2,1)S(1)} %shard_map.81), channel_id=1, replica_groups={{0,2,4,6,8,10,12,14,16,18,20,22,24,26,28,30,32,34,36,38,40,42,44,46,48,..., dimensions={0} | all-to-all | bytes 524288 | tf_op jit(solution)/shard_map/all_to_all | solution.py:419
  140.4 3.4 %collective-permute-start.23 = (bf16[512,256]{1,0:T(8,128)(2,1)S(1)}, bf16[512,256]{1,0:T(8,128)(2,1)S(1)}, u32[]{:S(2)}, u32[]{:S(2)}) collective-permute-start(bf16[512,256]{1,0:T(8,128)(2,1)S(1)} %shard_map.76), channel_id=1, source_target_pairs={{2,1},{4,3},{6,5},{8,7},{10,9},{12,11},{14,13},{16,15},{18,17},{20... | collective-permute-start | bytes 786440 | tf_op jit(solution)/shard_map/ppermute | solution.py:524
  143.8 0.4 shard_map.82
  144.3 2.6 %collective-permute-start.26 = (bf16[320,128]{1,0:T(8,128)(2,1)S(1)}, bf16[320,128]{1,0:T(8,128)(2,1)S(1)}, u32[]{:S(2)}, u32[]{:S(2)}) collective-permute-start(bf16[320,128]{1,0:T(8,128)(2,1)S(1)} %get-tuple-element.42.refs_0_), channel_id=1, source_target_pairs={{0,128},{64,192},{128,0},{192,64},{1,129},{65,193},{129,1},{193,65... | collective-permute-start | bytes 245768 | tf_op jit(solution)/shard_map/ppermute | solution.py:404
  146.9 1.1 collective-permute-start.25
  147.9 1.0 collective-permute-start.24
  148.9 9.6 %shard_map.83 = (bf16[256,256]{1,0:T(8,128)(2,1)S(1)}, bf16[4096,256]{1,0:T(8,128)(2,1)S(1)}) custom-call(f32[256,256]{1,0:T(8,128)S(1)} %get-tuple-element.38.gram_ref, s32[2,32]{1,0:T(2,128)S(1)} %bitcast.8, bf16[32,3,128,128]{3,2,1,0:T(8,128)(2,1)S(1)} %copy-done.2, bf16[4096,256]{1,0:T(8,128)(2,1)S(1)} %get-tuple-element.39.sample_ref, ...), custom_call_target="tpu_custom_call" | custom-call | flops 17179869184 | tf_op jit(solution)/shard_map/pallas_call | solution.py:27
  158.5 3.1 %final.1 = (bf16[4096,256]{1,0:T(8,128)(2,1)}, bf16[4096,256]{1,0:T(8,128)(2,1)}, f32[256,256]{1,0:T(8,128)}) custom-call(bf16[256,256]{1,0:T(8,128)(2,1)S(1)} %get-tuple-element.40.inv_ref.rows_ref, bf16[256,256]{1,0:T(8,128)(2,1)S(1)} %get-tuple-element.40.inv_ref.rows_ref, bf16[4096,256]{1,0:T(8,128)(2,1)S(1)} %get-tuple-element.39.sample_ref, ...), custom_call_target="tpu_custom_call" | custom-call | tf_op jit(solution)/shard_map/final/pallas_call | solution.py:563
  (38 shorter events, 0.7 us)
Async XLA Ops:
  0.6 0.7 copy-start.3
  1.3 10.8 %copy-start.1 = (bf16[512,4096]{1,0:T(8,128)(2,1)S(1)}, bf16[512,4096]{1,0:T(8,128)(2,1)}, u32[]{:S(2)}) copy-start(bf16[512,4096]{1,0:T(8,128)(2,1)} %jac_ref.3) | copy-start | bytes 12582916
  1.3 10.8 %copy-start.2 = (bf16[32,3,128,128]{3,2,1,0:T(8,128)(2,1)S(1)}, bf16[32,3,128,128]{3,2,1,0:T(8,128)(2,1)}, u32[]{:S(2)}) copy-start(bf16[32,3,128,128]{3,2,1,0:T(8,128)(2,1)} %coef_ref.5) | copy-start | bytes 9437188
  4.2 15.0 %collective-permute-start = (bf16[512,512]{1,0:T(8,128)(2,1)S(1)}, bf16[512,512]{1,0:T(8,128)(2,1)S(1)}, u32[]{:S(2)}, u32[]{:S(2)}) collective-permute-start(bf16[512,512]{1,0:T(8,128)(2,1)S(1)} %get-tuple-element.23), channel_id=1, source_target_pairs={{0,1},{1,0},{2,3},{3,2},{4,5},{5,4},{6,7},{7,6},{8,9},{9,8},{10,11... | collective-permute-start | bytes 1572872 | tf_op jit(solution)/shard_map/ppermute | solution.py:414
  4.3 13.9 %copy-start = (bf16[4096,256]{1,0:T(8,128)(2,1)S(1)}, bf16[4096,256]{1,0:T(8,128)(2,1)}, u32[]{:S(2)}) copy-start(bf16[4096,256]{1,0:T(8,128)(2,1)} %probe_ref.3) | copy-start | bytes 6291460
  4.3 14.9 %collective-permute-start.1 = (bf16[512,512]{1,0:T(8,128)(2,1)S(1)}, bf16[512,512]{1,0:T(8,128)(2,1)S(1)}, u32[]{:S(2)}, u32[]{:S(2)}) collective-permute-start(bf16[512,512]{1,0:T(8,128)(2,1)S(1)} %get-tuple-element.24), channel_id=1, source_target_pairs={{1,2},{2,1},{3,4},{4,3},{5,6},{6,5},{7,8},{8,7},{9,10},{10,9},{11,... | collective-permute-start | bytes 1572872 | tf_op jit(solution)/shard_map/ppermute | solution.py:410
  20.2 1.4 collective-permute-start.2
  53.0 1.3 collective-permute-start.3
  55.7 9.8 %collective-permute-start.16 = (bf16[512,256]{1,0:T(8,128)(2,1)S(1)}, bf16[512,256]{1,0:T(8,128)(2,1)S(1)}, u32[]{:S(2)}, u32[]{:S(2)}) collective-permute-start(bf16[512,256]{1,0:T(8,128)(2,1)S(1)} %get-tuple-element.35), channel_id=1, source_target_pairs={{0,192},{64,0},{128,64},{192,128},{1,193},{65,1},{129,65},{193,129... | collective-permute-start | bytes 786440 | tf_op jit(solution)/shard_map/ppermute | solution.py:404
  58.8 10.5 %collective-permute-start.5 = (bf16[512,256]{1,0:T(8,128)(2,1)S(1)}, bf16[512,256]{1,0:T(8,128)(2,1)S(1)}, u32[]{:S(2)}, u32[]{:S(2)}) collective-permute-start(bf16[512,256]{1,0:T(8,128)(2,1)S(1)} %get-tuple-element.31), channel_id=1, source_target_pairs={{0,64},{64,128},{128,192},{192,0},{1,65},{65,129},{129,193},{193,1... | collective-permute-start | bytes 786440 | tf_op jit(solution)/shard_map/ppermute | solution.py:404
  58.8 12.3 %collective-permute-start.4 = (bf16[512,256]{1,0:T(8,128)(2,1)S(1)}, bf16[512,256]{1,0:T(8,128)(2,1)S(1)}, u32[]{:S(2)}, u32[]{:S(2)}) collective-permute-start(bf16[512,256]{1,0:T(8,128)(2,1)S(1)} %get-tuple-element.29), channel_id=1, source_target_pairs={{0,192},{64,0},{128,64},{192,128},{1,193},{65,1},{129,65},{193,129... | collective-permute-start | bytes 786440 | tf_op jit(solution)/shard_map/ppermute | solution.py:404
  62.0 17.4 %collective-permute-start.15 = (bf16[512,256]{1,0:T(8,128)(2,1)S(1)}, bf16[512,256]{1,0:T(8,128)(2,1)S(1)}, u32[]{:S(2)}, u32[]{:S(2)}) collective-permute-start(bf16[512,256]{1,0:T(8,128)(2,1)S(1)} %get-tuple-element.33), channel_id=1, source_target_pairs={{0,64},{64,128},{128,192},{192,0},{1,65},{65,129},{129,193},{193,1... | collective-permute-start | bytes 786440 | tf_op jit(solution)/shard_map/ppermute | solution.py:404
  65.5 13.9 %collective-permute-start.17 = (bf16[512,256]{1,0:T(8,128)(2,1)S(1)}, bf16[512,256]{1,0:T(8,128)(2,1)S(1)}, u32[]{:S(2)}, u32[]{:S(2)}) collective-permute-start(bf16[512,256]{1,0:T(8,128)(2,1)S(1)} %shard_map.77), channel_id=1, source_target_pairs={{0,192},{64,0},{128,64},{192,128},{1,193},{65,1},{129,65},{193,129... | collective-permute-start | bytes 786440 | tf_op jit(solution)/shard_map/ppermute | solution.py:404
  69.3 8.2 %collective-permute-start.6 = (bf16[256,256]{1,0:T(8,128)(2,1)S(1)}, bf16[256,256]{1,0:T(8,128)(2,1)S(1)}, u32[]{:S(2)}, u32[]{:S(2)}) collective-permute-start(bf16[256,256]{1,0:T(8,128)(2,1)S(1)} %shard_map.72), channel_id=1, source_target_pairs={{0,64},{64,128},{128,192},{192,0},{1,65},{65,129},{129,193},{193,1... | collective-permute-start | bytes 393224 | tf_op jit(solution)/shard_map/ppermute | solution.py:404
  69.6 9.6 %collective-permute-start.7 = (bf16[256,256]{1,0:T(8,128)(2,1)S(1)}, bf16[256,256]{1,0:T(8,128)(2,1)S(1)}, u32[]{:S(2)}, u32[]{:S(2)}) collective-permute-start(bf16[256,256]{1,0:T(8,128)(2,1)S(1)} %shard_map.74), channel_id=1, source_target_pairs={{0,64},{64,128},{128,192},{192,0},{1,65},{65,129},{129,193},{193,1... | collective-permute-start | bytes 393224 | tf_op jit(solution)/shard_map/ppermute | solution.py:404
  77.6 7.4 %collective-permute-start.10 = (bf16[256,256]{1,0:T(8,128)(2,1)S(1)}, bf16[256,256]{1,0:T(8,128)(2,1)S(1)}, u32[]{:S(2)}, u32[]{:S(2)}) collective-permute-start(bf16[256,256]{1,0:T(8,128)(2,1)S(1)} %shard_map.73.refs_0_), channel_id=1, source_target_pairs={{0,64},{64,128},{128,192},{192,0},{1,65},{65,129},{129,193},{193,1... | collective-permute-start | bytes 393224 | tf_op jit(solution)/shard_map/ppermute | solution.py:404
  79.3 8.3 %collective-permute-start.12 = (bf16[256,256]{1,0:T(8,128)(2,1)S(1)}, bf16[256,256]{1,0:T(8,128)(2,1)S(1)}, u32[]{:S(2)}, u32[]{:S(2)}) collective-permute-start(bf16[256,256]{1,0:T(8,128)(2,1)S(1)} %shard_map.75.refs_1_), channel_id=1, source_target_pairs={{0,64},{64,128},{128,192},{192,0},{1,65},{65,129},{129,193},{193,1... | collective-permute-start | bytes 393224 | tf_op jit(solution)/shard_map/ppermute | solution.py:404
  79.6 16.2 %collective-permute-start.18 = (bf16[512,256]{1,0:T(8,128)(2,1)S(1)}, bf16[512,256]{1,0:T(8,128)(2,1)S(1)}, u32[]{:S(2)}, u32[]{:S(2)}) collective-permute-start(bf16[512,256]{1,0:T(8,128)(2,1)S(1)} %shard_map.78.refs_2_), channel_id=1, source_target_pairs={{0,192},{64,0},{128,64},{192,128},{1,193},{65,1},{129,65},{193,129... | collective-permute-start | bytes 786440 | tf_op jit(solution)/shard_map/ppermute | solution.py:404
  82.8 8.7 %collective-permute-start.8 = (bf16[256,256]{1,0:T(8,128)(2,1)S(1)}, bf16[256,256]{1,0:T(8,128)(2,1)S(1)}, u32[]{:S(2)}, u32[]{:S(2)}) collective-permute-start(bf16[256,256]{1,0:T(8,128)(2,1)S(1)} %shard_map.73.refs_0_), channel_id=1, source_target_pairs={{0,192},{64,0},{128,64},{192,128},{1,193},{65,1},{129,65},{193,129... | collective-permute-start | bytes 393224 | tf_op jit(solution)/shard_map/ppermute | solution.py:404
  83.3 9.6 %collective-permute-start.9 = (bf16[256,256]{1,0:T(8,128)(2,1)S(1)}, bf16[256,256]{1,0:T(8,128)(2,1)S(1)}, u32[]{:S(2)}, u32[]{:S(2)}) collective-permute-start(bf16[256,256]{1,0:T(8,128)(2,1)S(1)} %shard_map.75.refs_1_), channel_id=1, source_target_pairs={{0,192},{64,0},{128,64},{192,128},{1,193},{65,1},{129,65},{193,129... | collective-permute-start | bytes 393224 | tf_op jit(solution)/shard_map/ppermute | solution.py:404
  85.0 7.9 %collective-permute-start.11 = (bf16[256,256]{1,0:T(8,128)(2,1)S(1)}, bf16[256,256]{1,0:T(8,128)(2,1)S(1)}, u32[]{:S(2)}, u32[]{:S(2)}) collective-permute-start(bf16[256,256]{1,0:T(8,128)(2,1)S(1)} %collective-permute-done.10.refs_6_.refs_9_), channel_id=1, source_target_pairs={{0,64},{64,128},{128,192},{192,0},{1,65},{65,129},{129,193},{193,1... | collective-permute-start | bytes 393224 | tf_op jit(solution)/shard_map/ppermute | solution.py:404
  87.6 7.4 %collective-permute-start.13 = (bf16[256,256]{1,0:T(8,128)(2,1)S(1)}, bf16[256,256]{1,0:T(8,128)(2,1)S(1)}, u32[]{:S(2)}, u32[]{:S(2)}) collective-permute-start(bf16[256,256]{1,0:T(8,128)(2,1)S(1)} %collective-permute-done.12.refs_7_.refs_10_), channel_id=1, source_target_pairs={{0,64},{64,128},{128,192},{192,0},{1,65},{65,129},{129,193},{193,1... | collective-permute-start | bytes 393224 | tf_op jit(solution)/shard_map/ppermute | solution.py:404
  91.5 8.0 %collective-permute-start.20 = (bf16[512,256]{1,0:T(8,128)(2,1)S(1)}, bf16[512,256]{1,0:T(8,128)(2,1)S(1)}, u32[]{:S(2)}, u32[]{:S(2)}) collective-permute-start(bf16[512,256]{1,0:T(8,128)(2,1)S(1)} %shard_map.78.refs_2_), channel_id=1, source_target_pairs={{0,64},{64,128},{128,192},{192,0},{1,65},{65,129},{129,193},{193,1... | collective-permute-start | bytes 786440 | tf_op jit(solution)/shard_map/ppermute | solution.py:404
  95.1 4.5 %collective-permute-start.14 = (bf16[512,256]{1,0:T(8,128)(2,1)S(1)}, bf16[512,256]{1,0:T(8,128)(2,1)S(1)}, u32[]{:S(2)}, u32[]{:S(2)}) collective-permute-start(bf16[512,256]{1,0:T(8,128)(2,1)S(1)} %shard_map.76), channel_id=1, source_target_pairs={{1,3},{3,5},{5,7},{7,9},{9,11},{11,13},{13,15},{15,17},{17,19},{19... | collective-permute-start | bytes 786440 | tf_op jit(solution)/shard_map/ppermute | solution.py:523
  95.8 7.3 %collective-permute-start.19 = (bf16[512,256]{1,0:T(8,128)(2,1)S(1)}, bf16[512,256]{1,0:T(8,128)(2,1)S(1)}, u32[]{:S(2)}, u32[]{:S(2)}) collective-permute-start(bf16[512,256]{1,0:T(8,128)(2,1)S(1)} %collective-permute-done.18.refs_5_), channel_id=1, source_target_pairs={{0,192},{64,0},{128,64},{192,128},{1,193},{65,1},{129,65},{193,129... | collective-permute-start | bytes 786440 | tf_op jit(solution)/shard_map/ppermute | solution.py:404
  105.0 2.4 %collective-permute-start.21 = (bf16[1536,256]{1,0:T(8,128)(2,1)S(1)}, bf16[1536,256]{1,0:T(8,128)(2,1)S(1)}, u32[]{:S(2)}, u32[]{:S(2)}) collective-permute-start(bf16[1536,256]{1,0:T(8,128)(2,1)S(1)} %get-tuple-element.37), channel_id=1, source_target_pairs={{0,1},{1,0},{2,3},{3,2},{4,5},{5,4},{6,7},{7,6},{8,9},{9,8},{10,11... | collective-permute-start | bytes 2359304 | tf_op jit(solution)/shard_map/ppermute | solution.py:414
  140.4 3.5 %collective-permute-start.22 = (bf16[32,16,256]{2,1,0:T(8,128)(2,1)S(1)}, bf16[32,16,256]{2,1,0:T(8,128)(2,1)S(1)}, u32[]{:S(2)}, u32[]{:S(2)}) collective-permute-start(bf16[32,16,256]{2,1,0:T(8,128)(2,1)S(1)} %all_to_all.23.mine_ref), channel_id=1, source_target_pairs={{0,1},{1,0},{2,3},{3,2},{4,5},{5,4},{6,7},{7,6},{8,9},{9,8},{10,11... | collective-permute-start | bytes 786440 | tf_op jit(solution)/shard_map/ppermute | solution.py:414
  140.4 8.5 %collective-permute-start.23 = (bf16[512,256]{1,0:T(8,128)(2,1)S(1)}, bf16[512,256]{1,0:T(8,128)(2,1)S(1)}, u32[]{:S(2)}, u32[]{:S(2)}) collective-permute-start(bf16[512,256]{1,0:T(8,128)(2,1)S(1)} %shard_map.76), channel_id=1, source_target_pairs={{2,1},{4,3},{6,5},{8,7},{10,9},{12,11},{14,13},{16,15},{18,17},{20... | collective-permute-start | bytes 786440 | tf_op jit(solution)/shard_map/ppermute | solution.py:524
  144.3 14.2 %collective-permute-start.26 = (bf16[320,128]{1,0:T(8,128)(2,1)S(1)}, bf16[320,128]{1,0:T(8,128)(2,1)S(1)}, u32[]{:S(2)}, u32[]{:S(2)}) collective-permute-start(bf16[320,128]{1,0:T(8,128)(2,1)S(1)} %get-tuple-element.42.refs_0_), channel_id=1, source_target_pairs={{0,128},{64,192},{128,0},{192,64},{1,129},{65,193},{129,1},{193,65... | collective-permute-start | bytes 245768 | tf_op jit(solution)/shard_map/ppermute | solution.py:404
  146.9 11.6 %collective-permute-start.25 = (bf16[320,128]{1,0:T(8,128)(2,1)S(1)}, bf16[320,128]{1,0:T(8,128)(2,1)S(1)}, u32[]{:S(2)}, u32[]{:S(2)}) collective-permute-start(bf16[320,128]{1,0:T(8,128)(2,1)S(1)} %get-tuple-element.42.refs_0_), channel_id=1, source_target_pairs={{0,192},{64,0},{128,64},{192,128},{1,193},{65,1},{129,65},{193,129... | collective-permute-start | bytes 245768 | tf_op jit(solution)/shard_map/ppermute | solution.py:404
  147.9 10.6 %collective-permute-start.24 = (bf16[320,128]{1,0:T(8,128)(2,1)S(1)}, bf16[320,128]{1,0:T(8,128)(2,1)S(1)}, u32[]{:S(2)}, u32[]{:S(2)}) collective-permute-start(bf16[320,128]{1,0:T(8,128)(2,1)S(1)} %get-tuple-element.42.refs_0_), channel_id=1, source_target_pairs={{0,64},{64,128},{128,192},{192,0},{1,65},{65,129},{129,193},{193,1... | collective-permute-start | bytes 245768 | tf_op jit(solution)/shard_map/ppermute | solution.py:404

commit v7 on v5

--- a/solution.py
+++ b/solution.py
@@ -245,13 +245,14 @@
     return total.astype(BF16)
 
 
-def fill_ends(sample_ref, come_ref, neighbor_ref, ext):
+def fill_ends(sample_ref, come_ref, passed_ref, neighbor_ref, ext):
     rows = sample_ref.shape[0]
     core = core_index()
     ext[EDGE : 3 * EDGE] = sample_ref[: 2 * EDGE]
     ext[3 * EDGE : 5 * EDGE] = sample_ref[rows - 2 * EDGE :]
     ext[pl.ds(pl.multiple_of((1 - core) * (5 * EDGE), EDGE), EDGE)] = come_ref[come_ref.shape[0] - EDGE :]
-    ext[pl.ds(pl.multiple_of(core * (5 * EDGE), EDGE), EDGE)] = neighbor_ref[...]
+    far = jnp.where(core == 0, passed_ref[...], neighbor_ref[...])
+    ext[pl.ds(pl.multiple_of(core * (5 * EDGE), EDGE), EDGE)] = far
 
 
 def packed(full):
@@ -343,12 +344,13 @@
 
 
 def factor_kernel(
-    scale, gram_ref, off_ref, coef_ref, sample_ref, come_ref, neighbor_ref, out_ref, image_ref, a_ref, m_ref, inv_ref, ext
+    scale, gram_ref, off_ref, coef_ref, sample_ref, come_ref, passed_ref, neighbor_ref, out_ref, image_ref, *scratch
 ):
+    a_ref, m_ref, inv_ref, ext = scratch
     n = out_ref.shape[0]
     count, rows = coef_ref.shape[0], sample_ref.shape[0]
     share = count * NB // n
-    fill_ends(sample_ref, come_ref, neighbor_ref, ext)
+    fill_ends(sample_ref, come_ref, passed_ref, neighbor_ref, ext)
     gram = gram_ref[...] * scale
     index = [lax.broadcasted_iota(jnp.int32, (n, n), d) for d in (0, 1)]
     diagonal = jnp.where(index[0] == index[1], gram, 0.0)
@@ -516,7 +518,9 @@
     neighbor = call(
         functools.partial(pick_kernel, ranks), shape(EDGE, width), [VMEM] * (2 * ranks), [*sums0, *r0, *f0, *l0], mib=4
     )
-    from_neighbor = to_neighbor(neighbor)
+    cores = lax.axis_size("par")
+    passed = lax.ppermute(neighbor, "par", [(i, i + 2) for i in range(1, cores - 2, 2)])
+    from_neighbor = lax.ppermute(neighbor, "par", [(i, i - 1) for i in range(2, cores, 2)])
     sample, keep, give = call(
         functools.partial(project_kernel, ranks),
         [shape(npar, width), shape(nobs, width), shape(nobs + EDGE, width)],
@@ -532,6 +536,7 @@
     total = call(total_gram_kernel, both, [VMEM], [exchanged(part)], mib=4)
     mine = exchanged(total)
     other = swapped(mine)
+    passed = swapped(passed)
     gram, second = call(
         moments_kernel,
         [shape(width, width, dtype=F32), shape(5 * NB, 2 * NB)],
@@ -546,13 +551,13 @@
     inverse, image = call(
         functools.partial(factor_kernel, 1.0 / total_par),
         [shape(width, width), shape(npar, width)],
-        [VMEM, SMEM] + [VMEM] * 4,
-        [gram, offsets, coeffs, sample, come, from_neighbor],
+        [VMEM, SMEM] + [VMEM] * 5,
+        [gram, offsets, coeffs, sample, come, passed, from_neighbor],
         [pltpu.VMEM((width, width), F32)] * 3 + [pltpu.VMEM((6 * EDGE, width), BF16)],
         mib=16,
         flops=16 * flops,
     )
-    steps = 4
+    steps = 2
     by_rows = pl.BlockSpec((npar // steps, width), lambda i: (i, 0))
     few = pl.BlockSpec((width // steps, width), lambda i: (i, 0))
     return pl.pallas_call(
@@ -562,7 +567,7 @@
         out_shape=[shape(npar, width), shape(npar, width), shape(width, width, dtype=F32)],
         in_specs=[whole(width, width), few, by_rows, by_rows] + [whole(*second.shape)] * len(seconds),
         out_specs=[by_rows, by_rows, few],
-        compiler_params=pltpu.CompilerParams(vmem_limit_bytes=12 * 2**20),
+        compiler_params=pltpu.CompilerParams(vmem_limit_bytes=16 * 2**20),
     )(inverse, inverse, sample, image, *seconds)
 
 

time: 165 us -> 170 us (1.030)
  the two profiles are of different devices: /device:TPU:6 before, /device:TPU:1 now
where the time goes in v7:
time: 170 us; the launch traced here: 169 us
  starting transfers between devices  49.9 us (29%)
  blocking collectives  45.9 us (27%)
  waiting for transfers between devices  32.6 us (19%)
  Pallas kernels  29.8 us (18%)
  local copies, waits for them, and re-layouts  9.87 us (6%)
    all_to_all x3, blocking collectives, exchanged(): lax.all_to_all(parts, 'par', 0, 0, axis_index_groups=groups, tiled=True)  45.9 us
    ppermute x19, waiting for transfers between devices, shifted(): lax.ppermute(value, axis, [(i, (i + by) % count) for i in range(count)])  23 us
    pallas_call x17, Pallas kernels, call(): pl.pallas_call(kernel, out_shape=outs, in_specs=specs, out_specs=jax.tree...  22.6 us
    ppermute x19, starting transfers between devices, shifted(): lax.ppermute(value, axis, [(i, (i + by) % count) for i in range(count)])  21.5 us
    ppermute x6, starting transfers between devices, swapped(): lax.ppermute(value, 'par', [(i, i ^ 1) for i in range(lax.axis_size('par'...  14.5 us
    unnamed x42, local copies, waits for them, and re-layouts  9.87 us
    all_to_all x1, starting transfers between devices, exchanged(): lax.all_to_all(parts, 'par', 0, 0, axis_index_groups=groups, tiled=True)  6.84 us
    ppermute x6, waiting for transfers between devices, swapped(): lax.ppermute(value, 'par', [(i, i ^ 1) for i in range(lax.axis_size('par'...  3.87 us
  transfers between devices with their start and end apart: 29, of which 15 were waited for; matrix products, arithmetic and copies ran while one was open for 0% of the time, Pallas kernels for 11%

profile of v7, /device:TPU:1, one launch (start us, length us, event | category | flops | bytes accessed | tf_op | source)
XLA Modules:
  0.0 169.1 jit_solution(2082700517105796380)
XLA Ops:
  1.3 3.2 %edges.1 = (bf16[512,512]{1,0:T(8,128)(2,1)S(1)}, bf16[512,512]{1,0:T(8,128)(2,1)S(1)}) custom-call(s32[2,32]{1,0:T(2,128)S(1)} %bitcast.6, bf16[512,4096]{1,0:T(8,128)(2,1)} %jac_ref.3, bf16[32,3,128,128]{3,2,1,0:T(8,128)(2,1)} %coef_ref.5), custom_call_target="tpu_custom_call" | custom-call | flops 268435456 | tf_op jit(solution)/shard_map/edges/pallas_call | solution.py:433
  4.5 2.8 %collective-permute-start = (bf16[512,512]{1,0:T(8,128)(2,1)S(1)}, bf16[512,512]{1,0:T(8,128)(2,1)S(1)}, u32[]{:S(2)}, u32[]{:S(2)}) collective-permute-start(bf16[512,512]{1,0:T(8,128)(2,1)S(1)} %get-tuple-element.23), channel_id=1, source_target_pairs={{0,1},{1,0},{2,3},{3,2},{4,5},{5,4},{6,7},{7,6},{8,9},{9,8},{10,11... | collective-permute-start | bytes 1572872 | tf_op jit(solution)/shard_map/ppermute | solution.py:413
  7.3 2.0 %collective-permute-start.1 = (bf16[512,512]{1,0:T(8,128)(2,1)S(1)}, bf16[512,512]{1,0:T(8,128)(2,1)S(1)}, u32[]{:S(2)}, u32[]{:S(2)}) collective-permute-start(bf16[512,512]{1,0:T(8,128)(2,1)S(1)} %get-tuple-element.24), channel_id=1, source_target_pairs={{1,2},{2,1},{3,4},{4,3},{5,6},{6,5},{7,8},{8,7},{9,10},{10,9},{11,... | collective-permute-start | bytes 1572872 | tf_op jit(solution)/shard_map/ppermute | solution.py:409
  9.4 6.2 %shard_map.67.own_ref = bf16[8,512,512]{2,1,0:T(8,128)(2,1)S(1)} custom-call(s32[2,32]{1,0:T(2,128)S(1)} %bitcast.7, bf16[512,4096]{1,0:T(8,128)(2,1)S(1)} %copy-done.1, bf16[32,3,128,128]{3,2,1,0:T(8,128)(2,1)S(1)} %copy-done.2), custom_call_target="tpu_custom_call" | custom-call | flops 4294967296 | tf_op jit(solution)/shard_map/pallas_call | solution.py:27
  15.6 1.0 shard_map.68.inner_ref
  16.6 1.4 collective-permute-done.1.neighbor_ref
  19.0 1.3 collective-permute-done.2.come_ref
  20.3 19.7 %all_to_all.20.parts_ref = bf16[32,8,256]{2,1,0:T(8,128)(2,1)S(1)} all-to-all(bf16[32,8,256]{2,1,0:T(8,128)(2,1)S(1)} %bitcast.5), channel_id=1, replica_groups={{0,2,4,6,8,10,12,14,16,18,20,22,24,26,28,30,32,34,36,38,40,42,44,46,48,..., dimensions={0} | all-to-all | bytes 262144 | tf_op jit(solution)/shard_map/all_to_all | solution.py:418
  40.1 13.3 %all_to_all.21 = bf16[32,8,256]{2,1,0:T(8,128)(2,1)S(1)} all-to-all(bf16[32,8,256]{2,1,0:T(8,128)(2,1)S(1)} %shard_map.70), channel_id=1, replica_groups={{0,2,4,6,8,10,12,14,16,18,20,22,24,26,28,30,32,34,36,38,40,42,44,46,48,..., dimensions={0} | all-to-all | bytes 262144 | tf_op jit(solution)/shard_map/all_to_all | solution.py:418
  53.4 2.7 %collective-permute-start.3 = (bf16[256,256]{1,0:T(8,128)(2,1)S(1)}, bf16[256,256]{1,0:T(8,128)(2,1)S(1)}, u32[]{:S(2)}, u32[]{:S(2)}) collective-permute-start(bf16[256,256]{1,0:T(8,128)(2,1)S(1)} %bitcast.3), channel_id=1, source_target_pairs={{0,1},{1,0},{2,3},{3,2},{4,5},{5,4},{6,7},{7,6},{8,9},{9,8},{10,11... | collective-permute-start | bytes 393224 | tf_op jit(solution)/shard_map/ppermute | solution.py:413
  56.1 1.0 collective-permute-done.3.other_ref
  57.1 1.3 shard_map.71
  58.4 2.8 %collective-permute-start.9 = (bf16[512,256]{1,0:T(8,128)(2,1)S(1)}, bf16[512,256]{1,0:T(8,128)(2,1)S(1)}, u32[]{:S(2)}, u32[]{:S(2)}) collective-permute-start(bf16[512,256]{1,0:T(8,128)(2,1)S(1)} %get-tuple-element.35), channel_id=1, source_target_pairs={{0,192},{64,0},{128,64},{192,128},{1,193},{65,1},{129,65},{193,129... | collective-permute-start | bytes 786440 | tf_op jit(solution)/shard_map/ppermute | solution.py:403
  61.2 5.3 %collective-permute-done.9.refs_1_ = bf16[512,256]{1,0:T(8,128)(2,1)S(1)} collective-permute-done((bf16[512,256]{1,0:T(8,128)(2,1)S(1)}, bf16[512,256]{1,0:T(8,128)(2,1)S(1)}, u32[]{:S(2)}, u32[]{:S(2)}) %collective-permute-start.9) | collective-permute-done | bytes 262176 | tf_op jit(solution)/shard_map/ppermute | solution.py:403
  66.6 3.5 %collective-permute-start.10 = (bf16[512,256]{1,0:T(8,128)(2,1)S(1)}, bf16[512,256]{1,0:T(8,128)(2,1)S(1)}, u32[]{:S(2)}, u32[]{:S(2)}) collective-permute-start(bf16[512,256]{1,0:T(8,128)(2,1)S(1)} %shard_map.76), channel_id=1, source_target_pairs={{0,192},{64,0},{128,64},{192,128},{1,193},{65,1},{129,65},{193,129... | collective-permute-start | bytes 786440 | tf_op jit(solution)/shard_map/ppermute | solution.py:403
  70.1 2.7 %collective-permute-start.4 = (bf16[512,256]{1,0:T(8,128)(2,1)S(1)}, bf16[512,256]{1,0:T(8,128)(2,1)S(1)}, u32[]{:S(2)}, u32[]{:S(2)}) collective-permute-start(bf16[512,256]{1,0:T(8,128)(2,1)S(1)} %get-tuple-element.29), channel_id=1, source_target_pairs={{0,192},{64,0},{128,64},{192,128},{1,193},{65,1},{129,65},{193,129... | collective-permute-start | bytes 786440 | tf_op jit(solution)/shard_map/ppermute | solution.py:403
  72.7 1.8 %collective-permute-done.10.refs_2_ = bf16[512,256]{1,0:T(8,128)(2,1)S(1)} collective-permute-done((bf16[512,256]{1,0:T(8,128)(2,1)S(1)}, bf16[512,256]{1,0:T(8,128)(2,1)S(1)}, u32[]{:S(2)}, u32[]{:S(2)}) %collective-permute-start.10) | collective-permute-done | bytes 262176 | tf_op jit(solution)/shard_map/ppermute | solution.py:403
  74.6 3.7 %collective-permute-start.13 = (bf16[512,256]{1,0:T(8,128)(2,1)S(1)}, bf16[512,256]{1,0:T(8,128)(2,1)S(1)}, u32[]{:S(2)}, u32[]{:S(2)}) collective-permute-start(bf16[512,256]{1,0:T(8,128)(2,1)S(1)} %shard_map.77.refs_2_), channel_id=1, source_target_pairs={{0,192},{64,0},{128,64},{192,128},{1,193},{65,1},{129,65},{193,129... | collective-permute-start | bytes 786440 | tf_op jit(solution)/shard_map/ppermute | solution.py:403
  78.5 1.6 collective-permute-done.4.refs_1_
  80.1 3.3 %collective-permute-done.6.refs_2_ = bf16[256,256]{1,0:T(8,128)(2,1)S(1)} collective-permute-done((bf16[256,256]{1,0:T(8,128)(2,1)S(1)}, bf16[256,256]{1,0:T(8,128)(2,1)S(1)}, u32[]{:S(2)}, u32[]{:S(2)}) %collective-permute-start.6) | collective-permute-done | bytes 131104 | tf_op jit(solution)/shard_map/ppermute | solution.py:403
  83.6 2.7 %collective-permute-start.11 = (bf16[256,256]{1,0:T(8,128)(2,1)S(1)}, bf16[256,256]{1,0:T(8,128)(2,1)S(1)}, u32[]{:S(2)}, u32[]{:S(2)}) collective-permute-start(bf16[256,256]{1,0:T(8,128)(2,1)S(1)} %shard_map.73.refs_0_), channel_id=1, source_target_pairs={{0,192},{64,0},{128,64},{192,128},{1,193},{65,1},{129,65},{193,129... | collective-permute-start | bytes 393224 | tf_op jit(solution)/shard_map/ppermute | solution.py:403
  86.5 2.7 %collective-permute-start.18 = (bf16[512,256]{1,0:T(8,128)(2,1)S(1)}, bf16[512,256]{1,0:T(8,128)(2,1)S(1)}, u32[]{:S(2)}, u32[]{:S(2)}) collective-permute-start(bf16[512,256]{1,0:T(8,128)(2,1)S(1)} %collective-permute-done.13.refs_5_), channel_id=1, source_target_pairs={{0,192},{64,0},{128,64},{192,128},{1,193},{65,1},{129,65},{193,129... | collective-permute-start | bytes 786440 | tf_op jit(solution)/shard_map/ppermute | solution.py:403
  89.2 1.1 collective-permute-done.14.refs_9_.refs_6_
  90.5 1.2 collective-permute-start.15
  92.1 3.4 %collective-permute-done.12.refs_4_.refs_3_ = bf16[256,256]{1,0:T(8,128)(2,1)S(1)} collective-permute-done((bf16[256,256]{1,0:T(8,128)(2,1)S(1)}, bf16[256,256]{1,0:T(8,128)(2,1)S(1)}, u32[]{:S(2)}, u32[]{:S(2)}) %collective-permute-start.12) | collective-permute-done | bytes 131104 | tf_op jit(solution)/shard_map/ppermute | solution.py:403
  95.5 3.3 %collective-permute-done.15.refs_6_.refs_4_ = bf16[256,256]{1,0:T(8,128)(2,1)S(1)} collective-permute-done((bf16[256,256]{1,0:T(8,128)(2,1)S(1)}, bf16[256,256]{1,0:T(8,128)(2,1)S(1)}, u32[]{:S(2)}, u32[]{:S(2)}) %collective-permute-start.15) | collective-permute-done | bytes 131104 | tf_op jit(solution)/shard_map/ppermute | solution.py:403
  98.9 2.8 %collective-permute-done.17.refs_7_.refs_5_ = bf16[256,256]{1,0:T(8,128)(2,1)S(1)} collective-permute-done((bf16[256,256]{1,0:T(8,128)(2,1)S(1)}, bf16[256,256]{1,0:T(8,128)(2,1)S(1)}, u32[]{:S(2)}, u32[]{:S(2)}) %collective-permute-start.17) | collective-permute-done | bytes 131104 | tf_op jit(solution)/shard_map/ppermute | solution.py:403
  101.7 2.0 %shard_map.78 = (bf16[4096,256]{1,0:T(8,128)(2,1)S(1)}, bf16[512,256]{1,0:T(8,128)(2,1)S(1)}, bf16[1024,256]{1,0:T(8,128)(2,1)S(1)}) custom-call(bf16[8,512,512]{2,1,0:T(8,128)(2,1)S(1)} %get-tuple-element.25.full_ref, bf16[256,256]{1,0:T(8,128)(2,1)S(1)} %shard_map.73.refs_0_, bf16[256,256]{1,0:T(8,128)(2,1)S(1)} %shard_map.75.refs_1_, ...), custom_call_target="tpu_custom_call" | custom-call | flops 1073741824 | tf_op jit(solution)/shard_map/pallas_call | solution.py:27
  103.7 1.3 copy-done.3
  105.1 5.2 %collective-permute-start.20 = (bf16[1024,256]{1,0:T(8,128)(2,1)S(1)}, bf16[1024,256]{1,0:T(8,128)(2,1)S(1)}, u32[]{:S(2)}, u32[]{:S(2)}) collective-permute-start(bf16[1024,256]{1,0:T(8,128)(2,1)S(1)} %get-tuple-element.37), channel_id=1, source_target_pairs={{0,1},{1,0},{2,3},{3,2},{4,5},{5,4},{6,7},{7,6},{8,9},{9,8},{10,11... | collective-permute-start | bytes 1572872 | tf_op jit(solution)/shard_map/ppermute | solution.py:413
  110.2 1.5 collective-permute-done.20.come_ref
  111.9 12.8 %all_to_all.22.parts_ref = bf16[32,16,256]{2,1,0:T(8,128)(2,1)S(1)} all-to-all(bf16[32,16,256]{2,1,0:T(8,128)(2,1)S(1)} %shard_map.79), channel_id=1, replica_groups={{0,2,4,6,8,10,12,14,16,18,20,22,24,26,28,30,32,34,36,38,40,42,44,46,48,..., dimensions={0} | all-to-all | bytes 524288 | tf_op jit(solution)/shard_map/all_to_all | solution.py:418
  125.5 6.8 %all-to-all-start.3 = ((bf16[32,16,256]{2,1,0:T(8,128)(2,1)}), bf16[32,16,256]{2,1,0:T(8,128)(2,1)}, u32[]{:S(2)}, u32[]{:S(2)}) async-start(bf16[32,16,256]{2,1,0:T(8,128)(2,1)} %copy-done.6), calls=%async_computation.3 | async-start | bytes 524288 | tf_op jit(solution)/shard_map/all_to_all | solution.py:418
  132.3 0.9 copy-done.8
  133.2 0.9 copy-done.10
  134.1 0.9 copy-done.12
  135.0 0.9 copy-done.14
  135.9 0.9 copy-done.16
  137.6 3.8 %collective-permute-start.22 = (bf16[512,256]{1,0:T(8,128)(2,1)}, bf16[512,256]{1,0:T(8,128)(2,1)}, u32[]{:S(2)}, u32[]{:S(2)}) collective-permute-start(bf16[512,256]{1,0:T(8,128)(2,1)} %shard_map.82), channel_id=1, source_target_pairs={{1,3},{3,5},{5,7},{7,9},{9,11},{11,13},{13,15},{15,17},{17,19},{19... | collective-permute-start | bytes 786440 | tf_op jit(solution)/shard_map/ppermute | solution.py:522
  141.9 3.6 %collective-permute-start.21 = (bf16[32,16,256]{2,1,0:T(8,128)(2,1)}, bf16[32,16,256]{2,1,0:T(8,128)(2,1)S(1)}, u32[]{:S(2)}, u32[]{:S(2)}) collective-permute-start(bf16[32,16,256]{2,1,0:T(8,128)(2,1)} %all-to-all-done.3.mine_ref), channel_id=1, source_target_pairs={{0,1},{1,0},{2,3},{3,2},{4,5},{5,4},{6,7},{7,6},{8,9},{9,8},{10,11... | collective-permute-start | bytes 786440 | tf_op jit(solution)/shard_map/ppermute | solution.py:413
  145.6 1.3 collective-permute-start.24
  147.0 1.4 shard_map.81
  148.5 0.9 collective-permute-start.26
  150.0 3.8 %collective-permute-done.24.neighbor_ref = bf16[512,256]{1,0:T(8,128)(2,1)S(1)} collective-permute-done((bf16[512,256]{1,0:T(8,128)(2,1)}, bf16[512,256]{1,0:T(8,128)(2,1)S(1)}, u32[]{:S(2)}, u32[]{:S(2)}) %collective-permute-start.24) | collective-permute-done | bytes 262176 | tf_op jit(solution)/shard_map/ppermute | solution.py:523
  153.8 1.6 copy-done.4
  155.4 1.0 copy-done.18
  156.4 9.6 %shard_map.83 = (bf16[256,256]{1,0:T(8,128)(2,1)S(1)}, bf16[4096,256]{1,0:T(8,128)(2,1)S(1)}) custom-call(f32[256,256]{1,0:T(8,128)S(1)} %get-tuple-element.38.gram_ref, s32[2,32]{1,0:T(2,128)S(1)} %bitcast.8, bf16[32,3,128,128]{3,2,1,0:T(8,128)(2,1)S(1)} %copy-done.2, bf16[4096,256]{1,0:T(8,128)(2,1)S(1)} %copy-done.4, bf16[1024,256]{1,0:T(8,128)(2,1)S(1)} %copy-done.18, ...), custom_call_target="tpu_custom_call" | custom-call | flops 17179869184 | tf_op jit(solution)/shard_map/pallas_call | solution.py:27
  166.0 3.1 %final.1 = (bf16[4096,256]{1,0:T(8,128)(2,1)}, bf16[4096,256]{1,0:T(8,128)(2,1)}, f32[256,256]{1,0:T(8,128)}) custom-call(bf16[256,256]{1,0:T(8,128)(2,1)S(1)} %get-tuple-element.40.inv_ref.rows_ref, bf16[256,256]{1,0:T(8,128)(2,1)S(1)} %get-tuple-element.40.inv_ref.rows_ref, bf16[4096,256]{1,0:T(8,128)(2,1)S(1)} %copy-done.5, ...), custom_call_target="tpu_custom_call" | custom-call | tf_op jit(solution)/shard_map/final/pallas_call | solution.py:563
  (75 shorter events, 6.2 us)
Async XLA Ops:
  1.3 8.1 %copy-start.1 = (bf16[512,4096]{1,0:T(8,128)(2,1)S(1)}, bf16[512,4096]{1,0:T(8,128)(2,1)}, u32[]{:S(2)}) copy-start(bf16[512,4096]{1,0:T(8,128)(2,1)} %jac_ref.3) | copy-start | bytes 12582916
  1.3 8.1 %copy-start.2 = (bf16[32,3,128,128]{3,2,1,0:T(8,128)(2,1)S(1)}, bf16[32,3,128,128]{3,2,1,0:T(8,128)(2,1)}, u32[]{:S(2)}) copy-start(bf16[32,3,128,128]{3,2,1,0:T(8,128)(2,1)} %coef_ref.5) | copy-start | bytes 9437188
  4.5 12.0 %collective-permute-start = (bf16[512,512]{1,0:T(8,128)(2,1)S(1)}, bf16[512,512]{1,0:T(8,128)(2,1)S(1)}, u32[]{:S(2)}, u32[]{:S(2)}) collective-permute-start(bf16[512,512]{1,0:T(8,128)(2,1)S(1)} %get-tuple-element.23), channel_id=1, source_target_pairs={{0,1},{1,0},{2,3},{3,2},{4,5},{5,4},{6,7},{7,6},{8,9},{9,8},{10,11... | collective-permute-start | bytes 1572872 | tf_op jit(solution)/shard_map/ppermute | solution.py:413
  7.3 8.2 %copy-start = (bf16[4096,256]{1,0:T(8,128)(2,1)S(1)}, bf16[4096,256]{1,0:T(8,128)(2,1)}, u32[]{:S(2)}) copy-start(bf16[4096,256]{1,0:T(8,128)(2,1)} %probe_ref.3) | copy-start | bytes 6291460
  7.3 10.6 %collective-permute-start.1 = (bf16[512,512]{1,0:T(8,128)(2,1)S(1)}, bf16[512,512]{1,0:T(8,128)(2,1)S(1)}, u32[]{:S(2)}, u32[]{:S(2)}) collective-permute-start(bf16[512,512]{1,0:T(8,128)(2,1)S(1)} %get-tuple-element.24), channel_id=1, source_target_pairs={{1,2},{2,1},{3,4},{4,3},{5,6},{6,5},{7,8},{8,7},{9,10},{10,9},{11,... | collective-permute-start | bytes 1572872 | tf_op jit(solution)/shard_map/ppermute | solution.py:409
  18.9 1.4 collective-permute-start.2
  53.4 3.7 %collective-permute-start.3 = (bf16[256,256]{1,0:T(8,128)(2,1)S(1)}, bf16[256,256]{1,0:T(8,128)(2,1)S(1)}, u32[]{:S(2)}, u32[]{:S(2)}) collective-permute-start(bf16[256,256]{1,0:T(8,128)(2,1)S(1)} %bitcast.3), channel_id=1, source_target_pairs={{0,1},{1,0},{2,3},{3,2},{4,5},{5,4},{6,7},{7,6},{8,9},{9,8},{10,11... | collective-permute-start | bytes 393224 | tf_op jit(solution)/shard_map/ppermute | solution.py:413
  58.4 8.1 %collective-permute-start.9 = (bf16[512,256]{1,0:T(8,128)(2,1)S(1)}, bf16[512,256]{1,0:T(8,128)(2,1)S(1)}, u32[]{:S(2)}, u32[]{:S(2)}) collective-permute-start(bf16[512,256]{1,0:T(8,128)(2,1)S(1)} %get-tuple-element.35), channel_id=1, source_target_pairs={{0,192},{64,0},{128,64},{192,128},{1,193},{65,1},{129,65},{193,129... | collective-permute-start | bytes 786440 | tf_op jit(solution)/shard_map/ppermute | solution.py:403
  61.2 11.5 %collective-permute-start.8 = (bf16[512,256]{1,0:T(8,128)(2,1)S(1)}, bf16[512,256]{1,0:T(8,128)(2,1)S(1)}, u32[]{:S(2)}, u32[]{:S(2)}) collective-permute-start(bf16[512,256]{1,0:T(8,128)(2,1)S(1)} %get-tuple-element.33), channel_id=1, source_target_pairs={{0,64},{64,128},{128,192},{192,0},{1,65},{65,129},{129,193},{193,1... | collective-permute-start | bytes 786440 | tf_op jit(solution)/shard_map/ppermute | solution.py:403
  66.6 7.9 %collective-permute-start.10 = (bf16[512,256]{1,0:T(8,128)(2,1)S(1)}, bf16[512,256]{1,0:T(8,128)(2,1)S(1)}, u32[]{:S(2)}, u32[]{:S(2)}) collective-permute-start(bf16[512,256]{1,0:T(8,128)(2,1)S(1)} %shard_map.76), channel_id=1, source_target_pairs={{0,192},{64,0},{128,64},{192,128},{1,193},{65,1},{129,65},{193,129... | collective-permute-start | bytes 786440 | tf_op jit(solution)/shard_map/ppermute | solution.py:403
  70.1 8.2 %collective-permute-start.5 = (bf16[512,256]{1,0:T(8,128)(2,1)S(1)}, bf16[512,256]{1,0:T(8,128)(2,1)S(1)}, u32[]{:S(2)}, u32[]{:S(2)}) collective-permute-start(bf16[512,256]{1,0:T(8,128)(2,1)S(1)} %get-tuple-element.31), channel_id=1, source_target_pairs={{0,64},{64,128},{128,192},{192,0},{1,65},{65,129},{129,193},{193,1... | collective-permute-start | bytes 786440 | tf_op jit(solution)/shard_map/ppermute | solution.py:403
  70.1 10.1 %collective-permute-start.4 = (bf16[512,256]{1,0:T(8,128)(2,1)S(1)}, bf16[512,256]{1,0:T(8,128)(2,1)S(1)}, u32[]{:S(2)}, u32[]{:S(2)}) collective-permute-start(bf16[512,256]{1,0:T(8,128)(2,1)S(1)} %get-tuple-element.29), channel_id=1, source_target_pairs={{0,192},{64,0},{128,64},{192,128},{1,193},{65,1},{129,65},{193,129... | collective-permute-start | bytes 786440 | tf_op jit(solution)/shard_map/ppermute | solution.py:403
  74.6 11.9 %collective-permute-start.13 = (bf16[512,256]{1,0:T(8,128)(2,1)S(1)}, bf16[512,256]{1,0:T(8,128)(2,1)S(1)}, u32[]{:S(2)}, u32[]{:S(2)}) collective-permute-start(bf16[512,256]{1,0:T(8,128)(2,1)S(1)} %shard_map.77.refs_2_), channel_id=1, source_target_pairs={{0,192},{64,0},{128,64},{192,128},{1,193},{65,1},{129,65},{193,129... | collective-permute-start | bytes 786440 | tf_op jit(solution)/shard_map/ppermute | solution.py:403
  78.3 5.1 %collective-permute-start.6 = (bf16[256,256]{1,0:T(8,128)(2,1)S(1)}, bf16[256,256]{1,0:T(8,128)(2,1)S(1)}, u32[]{:S(2)}, u32[]{:S(2)}) collective-permute-start(bf16[256,256]{1,0:T(8,128)(2,1)S(1)} %shard_map.72), channel_id=1, source_target_pairs={{0,64},{64,128},{128,192},{192,0},{1,65},{65,129},{129,193},{193,1... | collective-permute-start | bytes 393224 | tf_op jit(solution)/shard_map/ppermute | solution.py:403
  78.5 7.8 %collective-permute-start.7 = (bf16[256,256]{1,0:T(8,128)(2,1)S(1)}, bf16[256,256]{1,0:T(8,128)(2,1)S(1)}, u32[]{:S(2)}, u32[]{:S(2)}) collective-permute-start(bf16[256,256]{1,0:T(8,128)(2,1)S(1)} %shard_map.74), channel_id=1, source_target_pairs={{0,64},{64,128},{128,192},{192,0},{1,65},{65,129},{129,193},{193,1... | collective-permute-start | bytes 393224 | tf_op jit(solution)/shard_map/ppermute | solution.py:403
  83.5 6.8 %collective-permute-start.14 = (bf16[256,256]{1,0:T(8,128)(2,1)S(1)}, bf16[256,256]{1,0:T(8,128)(2,1)S(1)}, u32[]{:S(2)}, u32[]{:S(2)}) collective-permute-start(bf16[256,256]{1,0:T(8,128)(2,1)S(1)} %shard_map.73.refs_0_), channel_id=1, source_target_pairs={{0,64},{64,128},{128,192},{192,0},{1,65},{65,129},{129,193},{193,1... | collective-permute-start | bytes 393224 | tf_op jit(solution)/shard_map/ppermute | solution.py:403
  83.6 7.0 %collective-permute-start.11 = (bf16[256,256]{1,0:T(8,128)(2,1)S(1)}, bf16[256,256]{1,0:T(8,128)(2,1)S(1)}, u32[]{:S(2)}, u32[]{:S(2)}) collective-permute-start(bf16[256,256]{1,0:T(8,128)(2,1)S(1)} %shard_map.73.refs_0_), channel_id=1, source_target_pairs={{0,192},{64,0},{128,64},{192,128},{1,193},{65,1},{129,65},{193,129... | collective-permute-start | bytes 393224 | tf_op jit(solution)/shard_map/ppermute | solution.py:403
  86.3 5.8 %collective-permute-start.16 = (bf16[256,256]{1,0:T(8,128)(2,1)S(1)}, bf16[256,256]{1,0:T(8,128)(2,1)S(1)}, u32[]{:S(2)}, u32[]{:S(2)}) collective-permute-start(bf16[256,256]{1,0:T(8,128)(2,1)S(1)} %shard_map.75.refs_1_), channel_id=1, source_target_pairs={{0,64},{64,128},{128,192},{192,0},{1,65},{65,129},{129,193},{193,1... | collective-permute-start | bytes 393224 | tf_op jit(solution)/shard_map/ppermute | solution.py:403
  86.4 15.3 %collective-permute-start.19 = (bf16[512,256]{1,0:T(8,128)(2,1)S(1)}, bf16[512,256]{1,0:T(8,128)(2,1)S(1)}, u32[]{:S(2)}, u32[]{:S(2)}) collective-permute-start(bf16[512,256]{1,0:T(8,128)(2,1)S(1)} %shard_map.77.refs_2_), channel_id=1, source_target_pairs={{0,64},{64,128},{128,192},{192,0},{1,65},{65,129},{129,193},{193,1... | collective-permute-start | bytes 786440 | tf_op jit(solution)/shard_map/ppermute | solution.py:403
  86.5 15.2 %collective-permute-start.18 = (bf16[512,256]{1,0:T(8,128)(2,1)S(1)}, bf16[512,256]{1,0:T(8,128)(2,1)S(1)}, u32[]{:S(2)}, u32[]{:S(2)}) collective-permute-start(bf16[512,256]{1,0:T(8,128)(2,1)S(1)} %collective-permute-done.13.refs_5_), channel_id=1, source_target_pairs={{0,192},{64,0},{128,64},{192,128},{1,193},{65,1},{129,65},{193,129... | collective-permute-start | bytes 786440 | tf_op jit(solution)/shard_map/ppermute | solution.py:403
  90.3 5.2 %collective-permute-start.12 = (bf16[256,256]{1,0:T(8,128)(2,1)S(1)}, bf16[256,256]{1,0:T(8,128)(2,1)S(1)}, u32[]{:S(2)}, u32[]{:S(2)}) collective-permute-start(bf16[256,256]{1,0:T(8,128)(2,1)S(1)} %shard_map.75.refs_1_), channel_id=1, source_target_pairs={{0,192},{64,0},{128,64},{192,128},{1,193},{65,1},{129,65},{193,129... | collective-permute-start | bytes 393224 | tf_op jit(solution)/shard_map/ppermute | solution.py:403
  90.5 13.2 %copy-start.7 = (bf16[256,256]{1,0:T(8,128)(2,1)}, bf16[256,256]{1,0:T(8,128)(2,1)S(1)}, u32[]{:S(2)}) copy-start(bf16[256,256]{1,0:T(8,128)(2,1)S(1)} %collective-permute-done.11.refs_3_.refs_2_) | copy-start | bytes 393220
  90.5 8.3 %collective-permute-start.15 = (bf16[256,256]{1,0:T(8,128)(2,1)S(1)}, bf16[256,256]{1,0:T(8,128)(2,1)S(1)}, u32[]{:S(2)}, u32[]{:S(2)}) collective-permute-start(bf16[256,256]{1,0:T(8,128)(2,1)S(1)} %collective-permute-done.14.refs_9_.refs_6_), channel_id=1, source_target_pairs={{0,64},{64,128},{128,192},{192,0},{1,65},{65,129},{129,193},{193,1... | collective-permute-start | bytes 393224 | tf_op jit(solution)/shard_map/ppermute | solution.py:403
  92.1 11.6 %copy-start.9 = (bf16[256,256]{1,0:T(8,128)(2,1)}, bf16[256,256]{1,0:T(8,128)(2,1)S(1)}, u32[]{:S(2)}) copy-start(bf16[256,256]{1,0:T(8,128)(2,1)S(1)} %collective-permute-done.16.refs_10_.refs_7_) | copy-start | bytes 393220
  92.1 9.5 %collective-permute-start.17 = (bf16[256,256]{1,0:T(8,128)(2,1)S(1)}, bf16[256,256]{1,0:T(8,128)(2,1)S(1)}, u32[]{:S(2)}, u32[]{:S(2)}) collective-permute-start(bf16[256,256]{1,0:T(8,128)(2,1)S(1)} %collective-permute-done.16.refs_10_.refs_7_), channel_id=1, source_target_pairs={{0,64},{64,128},{128,192},{192,0},{1,65},{65,129},{129,193},{193,1... | collective-permute-start | bytes 393224 | tf_op jit(solution)/shard_map/ppermute | solution.py:403
  95.5 8.2 %copy-start.11 = (bf16[256,256]{1,0:T(8,128)(2,1)}, bf16[256,256]{1,0:T(8,128)(2,1)S(1)}, u32[]{:S(2)}) copy-start(bf16[256,256]{1,0:T(8,128)(2,1)S(1)} %collective-permute-done.12.refs_4_.refs_3_) | copy-start | bytes 393220
  98.9 4.8 %copy-start.13 = (bf16[256,256]{1,0:T(8,128)(2,1)}, bf16[256,256]{1,0:T(8,128)(2,1)S(1)}, u32[]{:S(2)}) copy-start(bf16[256,256]{1,0:T(8,128)(2,1)S(1)} %collective-permute-done.15.refs_6_.refs_4_) | copy-start | bytes 393220
  101.7 2.0 %copy-start.15 = (bf16[256,256]{1,0:T(8,128)(2,1)}, bf16[256,256]{1,0:T(8,128)(2,1)S(1)}, u32[]{:S(2)}) copy-start(bf16[256,256]{1,0:T(8,128)(2,1)S(1)} %collective-permute-done.17.refs_7_.refs_5_) | copy-start | bytes 393220
  103.7 1.3 copy-start.3
  105.1 6.7 %collective-permute-start.20 = (bf16[1024,256]{1,0:T(8,128)(2,1)S(1)}, bf16[1024,256]{1,0:T(8,128)(2,1)S(1)}, u32[]{:S(2)}, u32[]{:S(2)}) collective-permute-start(bf16[1024,256]{1,0:T(8,128)(2,1)S(1)} %get-tuple-element.37), channel_id=1, source_target_pairs={{0,1},{1,0},{2,3},{3,2},{4,5},{5,4},{6,7},{7,6},{8,9},{9,8},{10,11... | collective-permute-start | bytes 1572872 | tf_op jit(solution)/shard_map/ppermute | solution.py:413
  111.8 12.9 %copy-start.17 = (bf16[1024,256]{1,0:T(8,128)(2,1)}, bf16[1024,256]{1,0:T(8,128)(2,1)S(1)}, u32[]{:S(2)}) copy-start(bf16[1024,256]{1,0:T(8,128)(2,1)S(1)} %collective-permute-done.20.come_ref) | copy-start | bytes 1572868
  111.8 42.0 %copy-start.20 = (s32[32,2]{0,1:T(2,128)S(1)}, s32[32,2]{0,1:T(2,128)}, u32[]{:S(2)}) copy-start(s32[32,2]{0,1:T(2,128)} %param.7) | copy-start | bytes 772
  125.5 16.5 %all-to-all-start.3 = ((bf16[32,16,256]{2,1,0:T(8,128)(2,1)}), bf16[32,16,256]{2,1,0:T(8,128)(2,1)}, u32[]{:S(2)}, u32[]{:S(2)}) async-start(bf16[32,16,256]{2,1,0:T(8,128)(2,1)} %copy-done.6), calls=%async_computation.3 | async-start | bytes 524288 | tf_op jit(solution)/shard_map/all_to_all | solution.py:418
  132.3 0.9 copy-start.8
  133.2 0.9 copy-start.10
  134.1 0.9 copy-start.12
  135.0 0.9 copy-start.14
  135.9 0.9 copy-start.16
  137.6 9.3 %collective-permute-start.22 = (bf16[512,256]{1,0:T(8,128)(2,1)}, bf16[512,256]{1,0:T(8,128)(2,1)}, u32[]{:S(2)}, u32[]{:S(2)}) collective-permute-start(bf16[512,256]{1,0:T(8,128)(2,1)} %shard_map.82), channel_id=1, source_target_pairs={{1,3},{3,5},{5,7},{7,9},{9,11},{11,13},{13,15},{15,17},{17,19},{19... | collective-permute-start | bytes 786440 | tf_op jit(solution)/shard_map/ppermute | solution.py:522
  141.9 5.0 %collective-permute-start.21 = (bf16[32,16,256]{2,1,0:T(8,128)(2,1)}, bf16[32,16,256]{2,1,0:T(8,128)(2,1)S(1)}, u32[]{:S(2)}, u32[]{:S(2)}) collective-permute-start(bf16[32,16,256]{2,1,0:T(8,128)(2,1)} %all-to-all-done.3.mine_ref), channel_id=1, source_target_pairs={{0,1},{1,0},{2,3},{3,2},{4,5},{5,4},{6,7},{7,6},{8,9},{9,8},{10,11... | collective-permute-start | bytes 786440 | tf_op jit(solution)/shard_map/ppermute | solution.py:413
  145.6 8.2 %collective-permute-start.24 = (bf16[512,256]{1,0:T(8,128)(2,1)}, bf16[512,256]{1,0:T(8,128)(2,1)S(1)}, u32[]{:S(2)}, u32[]{:S(2)}) collective-permute-start(bf16[512,256]{1,0:T(8,128)(2,1)} %shard_map.82), channel_id=1, source_target_pairs={{2,1},{4,3},{6,5},{8,7},{10,9},{12,11},{14,13},{16,15},{18,17},{20... | collective-permute-start | bytes 786440 | tf_op jit(solution)/shard_map/ppermute | solution.py:523
  146.9 6.9 %collective-permute-start.23 = (bf16[512,256]{1,0:T(8,128)(2,1)}, bf16[512,256]{1,0:T(8,128)(2,1)S(1)}, u32[]{:S(2)}, u32[]{:S(2)}) collective-permute-start(bf16[512,256]{1,0:T(8,128)(2,1)} %collective-permute-done.22), channel_id=1, source_target_pairs={{0,1},{1,0},{2,3},{3,2},{4,5},{5,4},{6,7},{7,6},{8,9},{9,8},{10,11... | collective-permute-start | bytes 786440 | tf_op jit(solution)/shard_map/ppermute | solution.py:413
  148.4 17.6 %collective-permute-start.27 = (bf16[320,128]{1,0:T(8,128)(2,1)S(1)}, bf16[320,128]{1,0:T(8,128)(2,1)S(1)}, u32[]{:S(2)}, u32[]{:S(2)}) collective-permute-start(bf16[320,128]{1,0:T(8,128)(2,1)S(1)} %get-tuple-element.42.refs_0_), channel_id=1, source_target_pairs={{0,128},{64,192},{128,0},{192,64},{1,129},{65,193},{129,1},{193,65... | collective-permute-start | bytes 245768 | tf_op jit(solution)/shard_map/ppermute | solution.py:403
  148.5 17.5 %collective-permute-start.26 = (bf16[320,128]{1,0:T(8,128)(2,1)S(1)}, bf16[320,128]{1,0:T(8,128)(2,1)S(1)}, u32[]{:S(2)}, u32[]{:S(2)}) collective-permute-start(bf16[320,128]{1,0:T(8,128)(2,1)S(1)} %get-tuple-element.42.refs_0_), channel_id=1, source_target_pairs={{0,192},{64,0},{128,64},{192,128},{1,193},{65,1},{129,65},{193,129... | collective-permute-start | bytes 245768 | tf_op jit(solution)/shard_map/ppermute | solution.py:403
  149.4 16.6 %collective-permute-start.25 = (bf16[320,128]{1,0:T(8,128)(2,1)S(1)}, bf16[320,128]{1,0:T(8,128)(2,1)S(1)}, u32[]{:S(2)}, u32[]{:S(2)}) collective-permute-start(bf16[320,128]{1,0:T(8,128)(2,1)S(1)} %get-tuple-element.42.refs_0_), channel_id=1, source_target_pairs={{0,64},{64,128},{128,192},{192,0},{1,65},{65,129},{129,193},{193,1... | collective-permute-start | bytes 245768 | tf_op jit(solution)/shard_map/ppermute | solution.py:403
  153.8 1.6 copy-start.4
  155.4 1.0 copy-start.18
  156.4 9.6 %copy-start.5 = (bf16[4096,256]{1,0:T(8,128)(2,1)S(1)}, bf16[4096,256]{1,0:T(8,128)(2,1)}, u32[]{:S(2)}) copy-start(bf16[4096,256]{1,0:T(8,128)(2,1)} %copy-done.3) | copy-start | bytes 6291460
  (2 other events, 1.4 us)
